TPU v7x, 256 devices: a whole 4x4x8 slice. The times are simulated.
256 devices in a mesh: mem: 32 (over z_hi, y, core), lat: 8 (over z_lo, x).
Axes of the slice: x: 4, y: 4, z: 8 (z_hi: 4, z_lo: 2; z = z_hi * 2 + z_lo), core: 2. Of those that a mesh axis runs over, the one named last changes fastest.
Arguments:
- controls: bfloat16 [128, 64, 256, 256], P('mem', None, 'lat'), may hold values from -6 to 6
- spread: bfloat16 [128, 64, 256, 256], P('mem', None, 'lat'), may hold values from -1.5 to 1.5
- classes: int32 [256, 256], P('lat'), may hold values from 0 to 7
- prec_table: float32 [8, 64], replicated, may hold values from 0.25 to 4
- vert_loc: bfloat16 [64, 64], replicated, may hold values from 0 to 1
- lon_loc: bfloat16 [256, 256], replicated, may hold values from 0 to 1
- lat_loc: bfloat16 [256, 256], replicated, may hold values from 0 to 1
Outputs:
- localized: bfloat16 [128, 64, 256, 256], P('mem', None, 'lat')
All inputs are finite; a program needn't handle non-finite values.
Results may differ from a plain program's by a relative error of at most 0.0064.
Values may be sent and summed in bfloat16 or wider, within the bound.
No kernel may reach another device: no remote copies, remote signals or barrier semaphores. Data moves between devices by JAX's collectives and lax.ppermute only.
A program may use at most 128 MiB of HBM per device.

v0:
```python
import jax
import jax.numpy as jnp
from jax import lax
from jax.experimental import pallas as pl
from jax.experimental.pallas import tpu as pltpu
from jax.sharding import Mesh
from jax.sharding import PartitionSpec as P


F32 = jnp.float32
BF16 = jnp.bfloat16
ZH, Y, CORE = 4, 4, 2
LATS = 8
LAT = "lat"
EACH = 4
GROUPS = ((0, 2), (2, 2))
ORDER = (6, 2, 4, 5, 7, 1, 3)


def nt_dot(a, b):
    return lax.dot_general(a, b, (((1,), (1,)), ((), ())), preferred_element_type=F32)


def compiler_params(mib):
    return pltpu.CompilerParams(
        dimension_semantics=("arbitrary",), vmem_limit_bytes=mib * 1024 * 1024
    )


def own_sum_kernel(start_ref, spread_ref, controls_ref, send_ref, keep_ref):
    at = pl.program_id(0)
    for l in range(spread_ref.shape[1]):
        total = spread_ref[0, l].astype(F32) * controls_ref[0, l].astype(F32)
        for k in range(1, spread_ref.shape[0]):
            total += spread_ref[k, l].astype(F32) * controls_ref[k, l].astype(F32)

        @pl.when(at < Y)
        def _(total=total, l=l):
            send_ref[0, l] = total.astype(BF16)

        @pl.when(at >= Y)
        def _(total=total, l=l):
            keep_ref[0, l] = total


def own_sum(spread, controls, start):
    members, levels, rows, cols = spread.shape
    step = levels // (CORE * Y)

    def source(i, s):
        half = s[0] ^ jnp.where(i < Y, 1, 0)
        return (0, half * Y + ((s[1] + i) & (Y - 1)), 0, 0)

    field = pl.BlockSpec((members, step, rows, cols), source)
    block = (1, step, rows, cols)
    return pl.pallas_call(
        own_sum_kernel,
        grid_spec=pltpu.PrefetchScalarGridSpec(
            num_scalar_prefetch=1,
            grid=(CORE * Y,),
            in_specs=[field, field],
            out_specs=[
                pl.BlockSpec(block, lambda i, s: (jnp.minimum(i, Y - 1), 0, 0, 0)),
                pl.BlockSpec(block, lambda i, s: (jnp.maximum(i - Y, 0), 0, 0, 0)),
            ],
        ),
        out_shape=[
            jax.ShapeDtypeStruct((Y, step, rows, cols), BF16),
            jax.ShapeDtypeStruct((Y, step, rows, cols), F32),
        ],
        compiler_params=compiler_params(12),
        name="own_sum",
    )(start, spread, controls)


def chip_sum_kernel(keep_ref, arrived_ref, *outs):
    for d, out in enumerate(outs):
        for l in range(out.shape[0]):
            out[l] = (keep_ref[d, l] + arrived_ref[d, l].astype(F32)).astype(out.dtype)


def chip_sum(keep, arrived):
    vmem = pl.BlockSpec(memory_space=pltpu.VMEM)
    return pl.pallas_call(
        chip_sum_kernel,
        in_specs=[vmem] * 2,
        out_specs=[vmem] * Y,
        out_shape=[
            jax.ShapeDtypeStruct(keep.shape[1:], BF16 if d else F32) for d in range(Y)
        ],
        compiler_params=pltpu.CompilerParams(vmem_limit_bytes=8 * 1024 * 1024),
        name="chip_sum",
    )(keep, arrived)


def tables_kernel(me_ref, vert_ref, lon_ref, lat_ref, big_ref, lon_out_ref, turned_ref):
    me = me_ref[0]
    levels = vert_ref.shape[0]
    size = levels * 8
    row = lax.broadcasted_iota(jnp.int32, (size, levels), 0) >> 3
    col = lax.broadcasted_iota(jnp.int32, (size, levels), 1)
    source = (row & ~3) | ((row + 8 - me) & 3)
    pick_out = jnp.where(source == col, 1.0, 0.0).astype(BF16)
    pick_in = jnp.where(row == col, 1.0, 0.0).astype(BF16)
    tall = jnp.dot(pick_out, vert_ref[...], preferred_element_type=F32).astype(BF16)
    wide = nt_dot(tall, pick_in)
    r = lax.broadcasted_iota(jnp.int32, (size, size), 0) & 7
    c = lax.broadcasted_iota(jnp.int32, (size, size), 1) & 7
    big_ref[...] = jnp.where(r == c, wide, 0.0).astype(BF16)
    share = lon_ref.shape[0] // LATS
    for d in range(LATS):
        at = pl.multiple_of(((me + d) & (LATS - 1)) * share, share)
        lon_out_ref[share * d : share * d + share, :] = lon_ref[pl.ds(at, share), :]
    rows = lat_ref.shape[0]
    from_col = lax.broadcasted_iota(jnp.int32, (rows, rows), 0)
    to_col = lax.broadcasted_iota(jnp.int32, (rows, rows), 1)
    for turn in range(EACH):
        back = EACH * (to_col >> 7) + ((turn - (to_col >> 5)) & 3)
        want = (((me + 16 - back) & (LATS - 1)) << 5) | (to_col & 31)
        move = jnp.where(from_col == want, 1.0, 0.0).astype(BF16)
        turned_ref[turn] = jnp.dot(
            lat_ref[...], move, preferred_element_type=F32
        ).astype(BF16)


def tables(me, vert_loc, lon_loc, lat_loc):
    levels = vert_loc.shape[0]
    size = lat_loc.shape[0]
    return pl.pallas_call(
        tables_kernel,
        in_specs=[pl.BlockSpec(memory_space=pltpu.SMEM)]
        + [pl.BlockSpec(memory_space=pltpu.VMEM)] * 3,
        out_specs=[pl.BlockSpec(memory_space=pltpu.VMEM)] * 3,
        out_shape=[
            jax.ShapeDtypeStruct((levels * 8, levels * 8), BF16),
            jax.ShapeDtypeStruct(lon_loc.shape, BF16),
            jax.ShapeDtypeStruct((EACH, size, size), BF16),
        ],
        compiler_params=pltpu.CompilerParams(vmem_limit_bytes=16 * 1024 * 1024),
        cost_estimate=pl.CostEstimate(
            flops=600_000_000, bytes_accessed=2_000_000, transcendentals=0
        ),
        name="tables",
    )(me, vert_loc, lon_loc, lat_loc)


def join_kernel(*refs):
    *pieces, out_ref = refs
    for l in range(out_ref.shape[0]):
        total = pieces[0][l].astype(F32)
        for piece in pieces[1:]:
            total += piece[l].astype(F32)
        out_ref[l] = total.astype(BF16)


def join(pieces):
    vmem = pl.BlockSpec(memory_space=pltpu.VMEM)
    return pl.pallas_call(
        join_kernel,
        in_specs=[vmem] * len(pieces),
        out_specs=vmem,
        out_shape=jax.ShapeDtypeStruct(pieces[0].shape, BF16),
        compiler_params=pltpu.CompilerParams(vmem_limit_bytes=8 * 1024 * 1024),
        name="join",
    )(*pieces)


def weigh_kernel(first_ref, classes_ref, table_ref, *refs):
    *pieces, out_ref = refs
    classes = classes_ref[...]
    numbers = range(1, table_ref.shape[0])
    at = [classes == n for n in numbers]
    for l in range(out_ref.shape[0]):
        total = pieces[0][l].astype(F32)
        for piece in pieces[1:]:
            total += piece[l].astype(F32)
        precision = jnp.full(classes.shape, table_ref[0, first_ref[0] + l], F32)
        for n in numbers:
            precision = jnp.where(at[n - 1], table_ref[n, first_ref[0] + l], precision)
        out_ref[l] = (total * precision).astype(BF16)


def weigh(first, classes, prec_table, pieces):
    vmem = pl.BlockSpec(memory_space=pltpu.VMEM)
    smem = pl.BlockSpec(memory_space=pltpu.SMEM)
    return pl.pallas_call(
        weigh_kernel,
        in_specs=[smem, vmem, smem] + [vmem] * len(pieces),
        out_specs=vmem,
        out_shape=jax.ShapeDtypeStruct(pieces[0].shape, BF16),
        compiler_params=pltpu.CompilerParams(vmem_limit_bytes=8 * 1024 * 1024),
        name="weigh",
    )(first, classes, prec_table, *pieces)


def spread_out_kernel(start_ref, spread_ref, *refs):
    weights = refs[: CORE * Y]
    big_ref, lon_ref = refs[CORE * Y : CORE * Y + 2]
    outs = refs[CORE * Y + 2 : CORE * Y + 2 + LATS]
    adj, mixed = refs[CORE * Y + 2 + LATS :]
    levels, rows, cols = adj.shape
    step = levels // (CORE * Y)
    for n, piece in enumerate(weights):
        core = start_ref[0] ^ (n // Y)
        base = (core * Y + ((start_ref[1] - n % Y) & (Y - 1))) * step
        for i in range(step):
            adj[base + i] = spread_ref[0, base + i].astype(F32) * piece[i].astype(F32)
    for g in range(rows // 8):
        x = adj[:, 8 * g : 8 * g + 8, :].reshape(levels * 8, cols).astype(BF16)
        y = jnp.dot(big_ref[...], x, preferred_element_type=F32)
        mixed[:, 8 * g : 8 * g + 8, :] = y.reshape(levels, 8, cols)
    share = cols // LATS
    for n in range(levels * rows // 256):
        at = 256 // rows
        x = mixed[at * n : at * n + at].reshape(256, cols).astype(BF16)
        y = nt_dot(lon_ref[...], x).astype(BF16)
        for d, out in enumerate(outs):
            out[0, :, 256 * n : 256 * n + 256] = y[share * d : share * d + share]


def spread_out(start, spread, weights, big, lon, first, count):
    _, levels, rows, cols = spread.shape
    share = cols // LATS

    def whole(x):
        return pl.BlockSpec(x.shape, lambda k, s: (0,) * x.ndim)

    return pl.pallas_call(
        spread_out_kernel,
        grid_spec=pltpu.PrefetchScalarGridSpec(
            num_scalar_prefetch=1,
            grid=(count,),
            in_specs=[pl.BlockSpec((1, levels, rows, cols), lambda k, s: (first + k, 0, 0, 0))]
            + [whole(x) for x in (*weights, big, lon)],
            out_specs=[pl.BlockSpec((1, share, levels * rows), lambda k, s: (k, 0, 0))] * LATS,
            scratch_shapes=[pltpu.VMEM((levels, rows, cols), F32)] * 2,
        ),
        out_shape=[jax.ShapeDtypeStruct((count, share, levels * rows), BF16)] * LATS,
        compiler_params=compiler_params(24),
        cost_estimate=pl.CostEstimate(
            flops=count * 1_500_000_000, bytes_accessed=count * 2_500_000, transcendentals=0
        ),
        name="spread_out",
    )(start, spread, *weights, big, lon)


def finish_kernel(me_ref, *refs):
    parts = refs[:LATS]
    turned_ref, out_ref = refs[LATS], refs[-1]
    share = parts[0].shape[1]
    groups = parts[0].shape[2] // 128
    lane = lax.broadcasted_iota(jnp.int32, (share, 128), 1) >> 5
    at = [lane == q for q in range(3)]
    for turn in range(EACH):
        lines = []
        for g in range(groups):
            sides = []
            for part in range(2):
                tiles = [
                    parts[EACH * part + (turn - q) % EACH][0, :, 128 * g : 128 * g + 128]
                    for q in range(EACH)
                ]
                side = tiles[3]
                for q in range(3):
                    side = jnp.where(at[q], tiles[q], side)
                sides.append(side)
            lines.append(jnp.concatenate(sides, axis=1))
        x = jnp.concatenate(lines, axis=0)
        y = nt_dot(x, turned_ref[turn]).astype(BF16)
        level = (turn + 8 - me_ref[0]) & 3
        for g in range(groups):
            out_ref[0, EACH * g + level] = y[share * g : share * g + share]


def finish(me, parts, turned, first, members, so_far=None):
    count, share, wide = parts[0].shape
    size = turned.shape[1]
    levels = wide // 32
    args = (*parts, turned) if so_far is None else (*parts, turned, so_far)
    extra = [] if so_far is None else [pl.BlockSpec(memory_space=pl.ANY)]
    return pl.pallas_call(
        finish_kernel,
        grid_spec=pltpu.PrefetchScalarGridSpec(
            num_scalar_prefetch=1,
            grid=(count,),
            in_specs=[pl.BlockSpec((1, share, wide), lambda k, s: (k, 0, 0))] * LATS
            + [pl.BlockSpec(turned.shape, lambda k, s: (0, 0, 0))]
            + extra,
            out_specs=pl.BlockSpec((1, levels, share, size), lambda k, s: (first + k, 0, 0, 0)),
        ),
        out_shape=jax.ShapeDtypeStruct((members, levels, share, size), BF16),
        input_output_aliases={} if so_far is None else {len(args): 0},
        compiler_params=compiler_params(16),
        cost_estimate=pl.CostEstimate(
            flops=count * 700_000_000, bytes_accessed=count * 2_500_000, transcendentals=0
        ),
        name="finish",
    )(me, *args)


def passed_on(axis, pieces, order):
    count = len(pieces)
    parts = [pieces[0]] + [None] * (count - 1)
    for d in order:
        parts[d] = lax.ppermute(pieces[d], axis, [(i, (i + d) % count) for i in range(count)])
    return parts


def local(controls, spread, classes, prec_table, vert_loc, lon_loc, lat_loc):
    controls = pltpu.with_memory_space_constraint(controls, pltpu.HBM)
    spread = pltpu.with_memory_space_constraint(spread, pltpu.HBM)
    members, levels = spread.shape[:2]
    core, y = lax.axis_index("core"), lax.axis_index("y")
    here = jnp.stack([core, y])
    me = lax.axis_index(LAT).reshape(1)
    first = ((core * Y + y) * (levels // (CORE * Y))).reshape(1)
    swap = [(0, 1), (1, 0)]

    big, lon, turned = tables(me, vert_loc, lon_loc, lat_loc)
    send, keep = own_sum(spread, controls, here)
    pieces = chip_sum(keep, lax.ppermute(send, "core", swap))
    along_y = join(passed_on("y", pieces, range(1, Y)))
    along_z = passed_on("zh", [along_y] * ZH, range(1, ZH))
    weighted = weigh(first, classes, prec_table, along_z)
    own = passed_on("y", [weighted] * Y, range(1, Y))
    weights = own + [lax.ppermute(x, "core", swap) for x in own]

    result = None
    for start, count in GROUPS:
        sending = spread_out(here, spread, weights, big, lon, start, count)
        parts = passed_on(LAT, sending, ORDER)
        result = finish(me, parts, turned, start, members, result)
    return result


def solution(mesh):
    finer = Mesh(
        mesh.devices.reshape(ZH, Y, CORE, mesh.shape["lat"]), ("zh", "y", "core", LAT)
    )
    members = P(("zh", "y", "core"), None, LAT, None)
    return jax.shard_map(
        local,
        mesh=finer,
        in_specs=(members, members, P(LAT, None), P(), P(), P(), P()),
        out_specs=members,
        check_vma=False,
    )
```

profile of v0, /device:TPU:1, one launch (start us, length us, event | category | flops | bytes accessed | tf_op | source)
XLA Modules:
  0.0 128.0 jit_solution(6528586499985809891)
XLA Ops:
  0.0 0.1 pad_add_fusion.start_ref
  0.1 0.0 copy-start.4
  0.1 6.5 %own_sum.1 = (bf16[4,8,32,256]{3,2,1,0:T(8,128)(2,1)S(1)}, f32[4,8,32,256]{3,2,1,0:T(8,128)S(1)}) custom-call(s32[2]{0:T(128)S(1)} %pad_add_fusion.start_ref, bf16[4,64,32,256]{3,2,1,0:T(8,128)(2,1)} %spread_ref.5, bf16[4,64,32,256]{3,2,1,0:T(8,128)(2,1)} %controls_ref.1), custom_call_target="tpu_custom_call" | custom-call | tf_op jit(solution)/shard_map/own_sum/pallas_call | solution.py:56
  6.6 3.3 %collective-permute-start = (bf16[4,8,32,256]{3,2,1,0:T(8,128)(2,1)S(1)}, bf16[4,8,32,256]{3,2,1,0:T(8,128)(2,1)S(1)}, u32[]{:S(2)}, u32[]{:S(2)}) collective-permute-start(bf16[4,8,32,256]{3,2,1,0:T(8,128)(2,1)S(1)} %get-tuple-element.31), channel_id=1, source_target_pairs={{0,8},{8,0},{1,9},{9,1},{2,10},{10,2},{3,11},{11,3},{4,12},{12,4},... | collective-permute-start | bytes 1572872 | tf_op jit(solution)/shard_map/ppermute | solution.py:321
  9.9 1.5 %collective-permute-done.arrived_ref = bf16[4,8,32,256]{3,2,1,0:T(8,128)(2,1)S(1)} collective-permute-done((bf16[4,8,32,256]{3,2,1,0:T(8,128)(2,1)S(1)}, bf16[4,8,32,256]{3,2,1,0:T(8,128)(2,1)S(1)}, u32[]{:S(2)}, u32[]{:S(2)}) %collective-permute-start) | collective-permute-done | bytes 524320 | tf_op jit(solution)/shard_map/ppermute | solution.py:321
  11.4 0.1 chip_sum.1
  11.5 0.1 collective-permute-start.1
  11.6 2.2 %collective-permute-start.2 = (bf16[8,32,256]{2,1,0:T(8,128)(2,1)S(1)}, bf16[8,32,256]{2,1,0:T(8,128)(2,1)S(1)}, u32[]{:S(2)}, u32[]{:S(2)}) collective-permute-start(bf16[8,32,256]{2,1,0:T(8,128)(2,1)S(1)} %get-tuple-element.34), channel_id=1, source_target_pairs={{0,32},{16,48},{32,0},{48,16},{1,33},{17,49},{33,1},{49,17},{2,34}... | collective-permute-start | bytes 393224 | tf_op jit(solution)/shard_map/ppermute | solution.py:305
  13.8 1.1 collective-permute-start.3
  14.9 3.1 %collective-permute-done.1.refs_1_ = bf16[8,32,256]{2,1,0:T(8,128)(2,1)S(1)} collective-permute-done((bf16[8,32,256]{2,1,0:T(8,128)(2,1)S(1)}, bf16[8,32,256]{2,1,0:T(8,128)(2,1)S(1)}, u32[]{:S(2)}, u32[]{:S(2)}) %collective-permute-start.1) | collective-permute-done | bytes 131104 | tf_op jit(solution)/shard_map/ppermute | solution.py:305
  18.0 1.9 %collective-permute-done.2.refs_2_ = bf16[8,32,256]{2,1,0:T(8,128)(2,1)S(1)} collective-permute-done((bf16[8,32,256]{2,1,0:T(8,128)(2,1)S(1)}, bf16[8,32,256]{2,1,0:T(8,128)(2,1)S(1)}, u32[]{:S(2)}, u32[]{:S(2)}) %collective-permute-start.2) | collective-permute-done | bytes 131104 | tf_op jit(solution)/shard_map/ppermute | solution.py:305
  19.9 0.7 collective-permute-done.3.refs_3_
  20.6 0.1 join.1.refs_0_
  20.7 5.3 %collective-permute-start.6 = (bf16[8,32,256]{2,1,0:T(8,128)(2,1)S(1)}, bf16[8,32,256]{2,1,0:T(8,128)(2,1)S(1)}, u32[]{:S(2)}, u32[]{:S(2)}) collective-permute-start(bf16[8,32,256]{2,1,0:T(8,128)(2,1)S(1)} %join.1.refs_0_), channel_id=1, source_target_pairs={{0,192},{64,0},{128,64},{192,128},{1,193},{65,1},{129,65},{193,129... | collective-permute-start | bytes 393224 | tf_op jit(solution)/shard_map/ppermute | solution.py:305
  26.0 1.0 collective-permute-start.5
  27.0 2.3 %collective-permute-start.4 = (bf16[8,32,256]{2,1,0:T(8,128)(2,1)S(1)}, bf16[8,32,256]{2,1,0:T(8,128)(2,1)S(1)}, u32[]{:S(2)}, u32[]{:S(2)}) collective-permute-start(bf16[8,32,256]{2,1,0:T(8,128)(2,1)S(1)} %join.1.refs_0_), channel_id=1, source_target_pairs={{0,64},{64,128},{128,192},{192,0},{1,65},{65,129},{129,193},{193,1... | collective-permute-start | bytes 393224 | tf_op jit(solution)/shard_map/ppermute | solution.py:305
  29.3 0.0 collective-permute-done.6.refs_3_
  29.3 7.6 %collective-permute-done.5.refs_2_ = bf16[8,32,256]{2,1,0:T(8,128)(2,1)S(1)} collective-permute-done((bf16[8,32,256]{2,1,0:T(8,128)(2,1)S(1)}, bf16[8,32,256]{2,1,0:T(8,128)(2,1)S(1)}, u32[]{:S(2)}, u32[]{:S(2)}) %collective-permute-start.5) | collective-permute-done | bytes 131104 | tf_op jit(solution)/shard_map/ppermute | solution.py:305
  36.8 0.8 weigh.1.refs_0_
  37.6 1.9 %collective-permute-start.9 = (bf16[8,32,256]{2,1,0:T(8,128)(2,1)S(1)}, bf16[8,32,256]{2,1,0:T(8,128)(2,1)S(1)}, u32[]{:S(2)}, u32[]{:S(2)}) collective-permute-start(bf16[8,32,256]{2,1,0:T(8,128)(2,1)S(1)} %weigh.1.refs_0_), channel_id=1, source_target_pairs={{0,48},{16,0},{32,16},{48,32},{1,49},{17,1},{33,17},{49,33},{2,50}... | collective-permute-start | bytes 393224 | tf_op jit(solution)/shard_map/ppermute | solution.py:305
  39.6 0.9 collective-permute-start.8
  40.5 3.9 %collective-permute-start.10 = (bf16[8,32,256]{2,1,0:T(8,128)(2,1)S(1)}, bf16[8,32,256]{2,1,0:T(8,128)(2,1)S(1)}, u32[]{:S(2)}, u32[]{:S(2)}) collective-permute-start(bf16[8,32,256]{2,1,0:T(8,128)(2,1)S(1)} %weigh.1.refs_0_), channel_id=1, source_target_pairs={{0,8},{8,0},{1,9},{9,1},{2,10},{10,2},{3,11},{11,3},{4,12},{12,4},... | collective-permute-start | bytes 393224 | tf_op jit(solution)/shard_map/ppermute | solution.py:326
  44.4 3.0 %collective-permute-start.13 = (bf16[8,32,256]{2,1,0:T(8,128)(2,1)S(1)}, bf16[8,32,256]{2,1,0:T(8,128)(2,1)S(1)}, u32[]{:S(2)}, u32[]{:S(2)}) collective-permute-start(bf16[8,32,256]{2,1,0:T(8,128)(2,1)S(1)} %collective-permute-done.9.refs_3_), channel_id=1, source_target_pairs={{0,8},{8,0},{1,9},{9,1},{2,10},{10,2},{3,11},{11,3},{4,12},{12,4},... | collective-permute-start | bytes 393224 | tf_op jit(solution)/shard_map/ppermute | solution.py:326
  47.4 2.6 %collective-permute-start.12 = (bf16[8,32,256]{2,1,0:T(8,128)(2,1)S(1)}, bf16[8,32,256]{2,1,0:T(8,128)(2,1)S(1)}, u32[]{:S(2)}, u32[]{:S(2)}) collective-permute-start(bf16[8,32,256]{2,1,0:T(8,128)(2,1)S(1)} %collective-permute-done.8.refs_2_), channel_id=1, source_target_pairs={{0,8},{8,0},{1,9},{9,1},{2,10},{10,2},{3,11},{11,3},{4,12},{12,4},... | collective-permute-start | bytes 393224 | tf_op jit(solution)/shard_map/ppermute | solution.py:326
  50.0 1.3 %collective-permute-start.11 = (bf16[8,32,256]{2,1,0:T(8,128)(2,1)S(1)}, bf16[8,32,256]{2,1,0:T(8,128)(2,1)S(1)}, u32[]{:S(2)}, u32[]{:S(2)}) collective-permute-start(bf16[8,32,256]{2,1,0:T(8,128)(2,1)S(1)} %collective-permute-done.7.refs_1_), channel_id=1, source_target_pairs={{0,8},{8,0},{1,9},{9,1},{2,10},{10,2},{3,11},{11,3},{4,12},{12,4},... | collective-permute-start | bytes 393224 | tf_op jit(solution)/shard_map/ppermute | solution.py:326
  51.3 0.6 tables.1
  52.0 0.4 collective-permute-done.11.refs_5_
  52.3 4.4 %spread_out.3 = (bf16[2,32,2048]{2,1,0:T(8,128)(2,1)S(1)}, bf16[2,32,2048]{2,1,0:T(8,128)(2,1)S(1)}, bf16[2,32,2048]{2,1,0:T(8,128)(2,1)S(1)}, bf16[2,32,2048]{2...) custom-call(s32[2]{0:T(128)S(1)} %pad_add_fusion.start_ref, ...), custom_call_target="tpu_custom_call" | custom-call | flops 3000000000 | bytes 5000000 | tf_op jit(solution)/shard_map/spread_out/pallas_call | solution.py:228
  56.7 0.8 collective-permute-start.21
  57.6 2.5 %collective-permute-start.22 = (bf16[2,32,2048]{2,1,0:T(8,128)(2,1)S(1)}, bf16[2,32,2048]{2,1,0:T(8,128)(2,1)S(1)}, u32[]{:S(2)}, u32[]{:S(2)}) collective-permute-start(bf16[2,32,2048]{2,1,0:T(8,128)(2,1)S(1)} %get-tuple-element.49), channel_id=1, source_target_pairs={{0,2},{1,3},{2,4},{3,5},{4,6},{5,7},{6,0},{7,1},{8,10},{9,11},{10,... | collective-permute-start | bytes 786440 | tf_op jit(solution)/shard_map/ppermute | solution.py:305
  60.0 3.4 %collective-permute-start.23 = (bf16[2,32,2048]{2,1,0:T(8,128)(2,1)S(1)}, bf16[2,32,2048]{2,1,0:T(8,128)(2,1)S(1)}, u32[]{:S(2)}, u32[]{:S(2)}) collective-permute-start(bf16[2,32,2048]{2,1,0:T(8,128)(2,1)S(1)} %get-tuple-element.50), channel_id=1, source_target_pairs={{0,3},{1,4},{2,5},{3,6},{4,7},{5,0},{6,1},{7,2},{8,11},{9,12},{10,... | collective-permute-start | bytes 786440 | tf_op jit(solution)/shard_map/ppermute | solution.py:305
  63.4 1.5 %collective-permute-start.25 = (bf16[2,32,2048]{2,1,0:T(8,128)(2,1)S(1)}, bf16[2,32,2048]{2,1,0:T(8,128)(2,1)S(1)}, u32[]{:S(2)}, u32[]{:S(2)}) collective-permute-start(bf16[2,32,2048]{2,1,0:T(8,128)(2,1)S(1)} %get-tuple-element.52), channel_id=1, source_target_pairs={{0,5},{1,6},{2,7},{3,0},{4,1},{5,2},{6,3},{7,4},{8,13},{9,14},{10,... | collective-permute-start | bytes 786440 | tf_op jit(solution)/shard_map/ppermute | solution.py:305
  64.9 4.4 %spread_out.2 = (bf16[2,32,2048]{2,1,0:T(8,128)(2,1)S(1)}, bf16[2,32,2048]{2,1,0:T(8,128)(2,1)S(1)}, bf16[2,32,2048]{2,1,0:T(8,128)(2,1)S(1)}, bf16[2,32,2048]{2...) custom-call(s32[2]{0:T(128)S(1)} %pad_add_fusion.start_ref, ...), custom_call_target="tpu_custom_call" | custom-call | flops 3000000000 | bytes 5000000 | tf_op jit(solution)/shard_map/spread_out/pallas_call | solution.py:228
  69.3 2.4 %collective-permute-done.21.refs_1_ = bf16[2,32,2048]{2,1,0:T(8,128)(2,1)S(1)} collective-permute-done((bf16[2,32,2048]{2,1,0:T(8,128)(2,1)S(1)}, bf16[2,32,2048]{2,1,0:T(8,128)(2,1)S(1)}, u32[]{:S(2)}, u32[]{:S(2)}) %collective-permute-start.21) | collective-permute-done | bytes 262176 | tf_op jit(solution)/shard_map/ppermute | solution.py:305
  71.7 0.0 collective-permute-start.26
  71.8 0.4 collective-permute-done.22.refs_2_
  72.1 6.3 %collective-permute-start.27 = (bf16[2,32,2048]{2,1,0:T(8,128)(2,1)S(1)}, bf16[2,32,2048]{2,1,0:T(8,128)(2,1)S(1)}, u32[]{:S(2)}, u32[]{:S(2)}) collective-permute-start(bf16[2,32,2048]{2,1,0:T(8,128)(2,1)S(1)} %get-tuple-element.54), channel_id=1, source_target_pairs={{0,7},{1,0},{2,1},{3,2},{4,3},{5,4},{6,5},{7,6},{8,15},{9,8},{10,9... | collective-permute-start | bytes 786440 | tf_op jit(solution)/shard_map/ppermute | solution.py:305
  78.4 2.6 %collective-permute-start.14 = (bf16[2,32,2048]{2,1,0:T(8,128)(2,1)S(1)}, bf16[2,32,2048]{2,1,0:T(8,128)(2,1)S(1)}, u32[]{:S(2)}, u32[]{:S(2)}) collective-permute-start(bf16[2,32,2048]{2,1,0:T(8,128)(2,1)S(1)} %get-tuple-element.39), channel_id=1, source_target_pairs={{0,1},{1,2},{2,3},{3,4},{4,5},{5,6},{6,7},{7,0},{8,9},{9,10},{10,1... | collective-permute-start | bytes 786440 | tf_op jit(solution)/shard_map/ppermute | solution.py:305
  81.1 5.7 %collective-permute-start.15 = (bf16[2,32,2048]{2,1,0:T(8,128)(2,1)S(1)}, bf16[2,32,2048]{2,1,0:T(8,128)(2,1)S(1)}, u32[]{:S(2)}, u32[]{:S(2)}) collective-permute-start(bf16[2,32,2048]{2,1,0:T(8,128)(2,1)S(1)} %get-tuple-element.40), channel_id=1, source_target_pairs={{0,2},{1,3},{2,4},{3,5},{4,6},{5,7},{6,0},{7,1},{8,10},{9,11},{10,... | collective-permute-start | bytes 786440 | tf_op jit(solution)/shard_map/ppermute | solution.py:305
  86.8 4.7 %collective-permute-start.16 = (bf16[2,32,2048]{2,1,0:T(8,128)(2,1)S(1)}, bf16[2,32,2048]{2,1,0:T(8,128)(2,1)S(1)}, u32[]{:S(2)}, u32[]{:S(2)}) collective-permute-start(bf16[2,32,2048]{2,1,0:T(8,128)(2,1)S(1)} %get-tuple-element.41), channel_id=1, source_target_pairs={{0,3},{1,4},{2,5},{3,6},{4,7},{5,0},{6,1},{7,2},{8,11},{9,12},{10,... | collective-permute-start | bytes 786440 | tf_op jit(solution)/shard_map/ppermute | solution.py:305
  91.5 1.1 collective-permute-start.17
  92.5 17.2 %collective-permute-start.18 = (bf16[2,32,2048]{2,1,0:T(8,128)(2,1)S(1)}, bf16[2,32,2048]{2,1,0:T(8,128)(2,1)S(1)}, u32[]{:S(2)}, u32[]{:S(2)}) collective-permute-start(bf16[2,32,2048]{2,1,0:T(8,128)(2,1)S(1)} %get-tuple-element.43), channel_id=1, source_target_pairs={{0,5},{1,6},{2,7},{3,0},{4,1},{5,2},{6,3},{7,4},{8,13},{9,14},{10,... | collective-permute-start | bytes 786440 | tf_op jit(solution)/shard_map/ppermute | solution.py:305
  109.8 2.4 %collective-permute-start.20 = (bf16[2,32,2048]{2,1,0:T(8,128)(2,1)S(1)}, bf16[2,32,2048]{2,1,0:T(8,128)(2,1)S(1)}, u32[]{:S(2)}, u32[]{:S(2)}) collective-permute-start(bf16[2,32,2048]{2,1,0:T(8,128)(2,1)S(1)} %get-tuple-element.45), channel_id=1, source_target_pairs={{0,7},{1,0},{2,1},{3,2},{4,3},{5,4},{6,5},{7,6},{8,15},{9,8},{10,9... | collective-permute-start | bytes 786440 | tf_op jit(solution)/shard_map/ppermute | solution.py:305
  112.1 2.0 %finish.2.refs_9_ = bf16[4,64,32,256]{3,2,1,0:T(8,128)(2,1)} custom-call(s32[1]{0:T(128)} %bitcast.me_ref, bf16[2,32,2048]{2,1,0:T(8,128)(2,1)S(1)} %get-tuple-element.47.refs_0_, bf16[2,32,2048]{2,1,0:T(8,128)(2,1)S(1)} %collective-permute-done.21.refs_1_, bf16[2,32,2048]{2,1,0:T(8,128)(2,1)S(1)} %collective-permute-done.22.refs_2_, ...), custom_call_target="tpu_custom_call" | custom-call | flops 1400000000 | bytes 5000000 | tf_op jit(solution)/shard_map/finish/pallas_call | solution.py:281
  114.1 0.7 collective-permute-done.18.refs_5_
  114.8 6.4 %collective-permute-done.19.refs_6_ = bf16[2,32,2048]{2,1,0:T(8,128)(2,1)S(1)} collective-permute-done((bf16[2,32,2048]{2,1,0:T(8,128)(2,1)S(1)}, bf16[2,32,2048]{2,1,0:T(8,128)(2,1)S(1)}, u32[]{:S(2)}, u32[]{:S(2)}) %collective-permute-start.19) | collective-permute-done | bytes 262176 | tf_op jit(solution)/shard_map/ppermute | solution.py:305
  121.2 4.8 %collective-permute-done.20.refs_7_ = bf16[2,32,2048]{2,1,0:T(8,128)(2,1)S(1)} collective-permute-done((bf16[2,32,2048]{2,1,0:T(8,128)(2,1)S(1)}, bf16[2,32,2048]{2,1,0:T(8,128)(2,1)S(1)}, u32[]{:S(2)}, u32[]{:S(2)}) %collective-permute-start.20) | collective-permute-done | bytes 262176 | tf_op jit(solution)/shard_map/ppermute | solution.py:305
  126.0 2.0 %finish.3 = bf16[4,64,32,256]{3,2,1,0:T(8,128)(2,1)} custom-call(s32[1]{0:T(128)} %bitcast.me_ref, bf16[2,32,2048]{2,1,0:T(8,128)(2,1)S(1)} %get-tuple-element.38.refs_0_, bf16[2,32,2048]{2,1,0:T(8,128)(2,1)S(1)} %collective-permute-done.14.refs_1_, bf16[2,32,2048]{2,1,0:T(8,128)(2,1)S(1)} %collective-permute-done.15.refs_2_, ...), custom_call_target="tpu_custom_call", output_to_operand_aliasing={{}: (10, {})} | custom-call | flops 1400000000 | bytes 5000000 | tf_op jit(solution)/shard_map/finish/pallas_call | solution.py:281
  (28 shorter events, 0.1 us)
Async XLA Ops:
  0.1 36.8 %copy-start = (s32[32,256]{1,0:T(8,128)S(1)}, s32[32,256]{1,0:T(8,128)}, u32[]{:S(2)}) copy-start(s32[32,256]{1,0:T(8,128)} %classes_ref.1) | copy-start | bytes 98308
  0.1 36.8 %copy-start.1 = (f32[8,64]{1,0:T(8,128)S(1)}, f32[8,64]{1,0:T(8,128)}, u32[]{:S(2)}) copy-start(f32[8,64]{1,0:T(8,128)} %table_ref.1) | copy-start | bytes 6148
  0.1 51.3 %copy-start.2 = (bf16[256,256]{1,0:T(8,128)(2,1)S(1)}, bf16[256,256]{1,0:T(8,128)(2,1)}, u32[]{:S(2)}) copy-start(bf16[256,256]{1,0:T(8,128)(2,1)} %lon_ref.1) | copy-start | bytes 393220
  0.1 51.3 %copy-start.3 = (bf16[256,256]{1,0:T(8,128)(2,1)S(1)}, bf16[256,256]{1,0:T(8,128)(2,1)}, u32[]{:S(2)}) copy-start(bf16[256,256]{1,0:T(8,128)(2,1)} %lat_ref.1) | copy-start | bytes 393220
  0.1 51.3 %copy-start.4 = (bf16[64,64]{1,0:T(8,128)(2,1)S(1)}, bf16[64,64]{1,0:T(8,128)(2,1)}, u32[]{:S(2)}) copy-start(bf16[64,64]{1,0:T(8,128)(2,1)} %vert_ref.1) | copy-start | bytes 24580
  6.6 4.8 %collective-permute-start = (bf16[4,8,32,256]{3,2,1,0:T(8,128)(2,1)S(1)}, bf16[4,8,32,256]{3,2,1,0:T(8,128)(2,1)S(1)}, u32[]{:S(2)}, u32[]{:S(2)}) collective-permute-start(bf16[4,8,32,256]{3,2,1,0:T(8,128)(2,1)S(1)} %get-tuple-element.31), channel_id=1, source_target_pairs={{0,8},{8,0},{1,9},{9,1},{2,10},{10,2},{3,11},{11,3},{4,12},{12,4},... | collective-permute-start | bytes 1572872 | tf_op jit(solution)/shard_map/ppermute | solution.py:321
  11.5 6.4 %collective-permute-start.1 = (bf16[8,32,256]{2,1,0:T(8,128)(2,1)S(1)}, bf16[8,32,256]{2,1,0:T(8,128)(2,1)S(1)}, u32[]{:S(2)}, u32[]{:S(2)}) collective-permute-start(bf16[8,32,256]{2,1,0:T(8,128)(2,1)S(1)} %get-tuple-element.33), channel_id=1, source_target_pairs={{0,16},{16,32},{32,48},{48,0},{1,17},{17,33},{33,49},{49,1},{2,18}... | collective-permute-start | bytes 393224 | tf_op jit(solution)/shard_map/ppermute | solution.py:305
  11.6 8.3 %collective-permute-start.2 = (bf16[8,32,256]{2,1,0:T(8,128)(2,1)S(1)}, bf16[8,32,256]{2,1,0:T(8,128)(2,1)S(1)}, u32[]{:S(2)}, u32[]{:S(2)}) collective-permute-start(bf16[8,32,256]{2,1,0:T(8,128)(2,1)S(1)} %get-tuple-element.34), channel_id=1, source_target_pairs={{0,32},{16,48},{32,0},{48,16},{1,33},{17,49},{33,1},{49,17},{2,34}... | collective-permute-start | bytes 393224 | tf_op jit(solution)/shard_map/ppermute | solution.py:305
  13.8 6.8 %collective-permute-start.3 = (bf16[8,32,256]{2,1,0:T(8,128)(2,1)S(1)}, bf16[8,32,256]{2,1,0:T(8,128)(2,1)S(1)}, u32[]{:S(2)}, u32[]{:S(2)}) collective-permute-start(bf16[8,32,256]{2,1,0:T(8,128)(2,1)S(1)} %get-tuple-element.35), channel_id=1, source_target_pairs={{0,48},{16,0},{32,16},{48,32},{1,49},{17,1},{33,17},{49,33},{2,50}... | collective-permute-start | bytes 393224 | tf_op jit(solution)/shard_map/ppermute | solution.py:305
  20.7 8.6 %collective-permute-start.6 = (bf16[8,32,256]{2,1,0:T(8,128)(2,1)S(1)}, bf16[8,32,256]{2,1,0:T(8,128)(2,1)S(1)}, u32[]{:S(2)}, u32[]{:S(2)}) collective-permute-start(bf16[8,32,256]{2,1,0:T(8,128)(2,1)S(1)} %join.1.refs_0_), channel_id=1, source_target_pairs={{0,192},{64,0},{128,64},{192,128},{1,193},{65,1},{129,65},{193,129... | collective-permute-start | bytes 393224 | tf_op jit(solution)/shard_map/ppermute | solution.py:305
  26.0 10.8 %collective-permute-start.5 = (bf16[8,32,256]{2,1,0:T(8,128)(2,1)S(1)}, bf16[8,32,256]{2,1,0:T(8,128)(2,1)S(1)}, u32[]{:S(2)}, u32[]{:S(2)}) collective-permute-start(bf16[8,32,256]{2,1,0:T(8,128)(2,1)S(1)} %join.1.refs_0_), channel_id=1, source_target_pairs={{0,128},{64,192},{128,0},{192,64},{1,129},{65,193},{129,1},{193,65... | collective-permute-start | bytes 393224 | tf_op jit(solution)/shard_map/ppermute | solution.py:305
  27.0 9.8 %collective-permute-start.4 = (bf16[8,32,256]{2,1,0:T(8,128)(2,1)S(1)}, bf16[8,32,256]{2,1,0:T(8,128)(2,1)S(1)}, u32[]{:S(2)}, u32[]{:S(2)}) collective-permute-start(bf16[8,32,256]{2,1,0:T(8,128)(2,1)S(1)} %join.1.refs_0_), channel_id=1, source_target_pairs={{0,64},{64,128},{128,192},{192,0},{1,65},{65,129},{129,193},{193,1... | collective-permute-start | bytes 393224 | tf_op jit(solution)/shard_map/ppermute | solution.py:305
  37.6 6.8 %collective-permute-start.9 = (bf16[8,32,256]{2,1,0:T(8,128)(2,1)S(1)}, bf16[8,32,256]{2,1,0:T(8,128)(2,1)S(1)}, u32[]{:S(2)}, u32[]{:S(2)}) collective-permute-start(bf16[8,32,256]{2,1,0:T(8,128)(2,1)S(1)} %weigh.1.refs_0_), channel_id=1, source_target_pairs={{0,48},{16,0},{32,16},{48,32},{1,49},{17,1},{33,17},{49,33},{2,50}... | collective-permute-start | bytes 393224 | tf_op jit(solution)/shard_map/ppermute | solution.py:305
  39.6 7.8 %collective-permute-start.8 = (bf16[8,32,256]{2,1,0:T(8,128)(2,1)S(1)}, bf16[8,32,256]{2,1,0:T(8,128)(2,1)S(1)}, u32[]{:S(2)}, u32[]{:S(2)}) collective-permute-start(bf16[8,32,256]{2,1,0:T(8,128)(2,1)S(1)} %weigh.1.refs_0_), channel_id=1, source_target_pairs={{0,32},{16,48},{32,0},{48,16},{1,33},{17,49},{33,1},{49,17},{2,34}... | collective-permute-start | bytes 393224 | tf_op jit(solution)/shard_map/ppermute | solution.py:305
  40.5 9.5 %collective-permute-start.7 = (bf16[8,32,256]{2,1,0:T(8,128)(2,1)S(1)}, bf16[8,32,256]{2,1,0:T(8,128)(2,1)S(1)}, u32[]{:S(2)}, u32[]{:S(2)}) collective-permute-start(bf16[8,32,256]{2,1,0:T(8,128)(2,1)S(1)} %weigh.1.refs_0_), channel_id=1, source_target_pairs={{0,16},{16,32},{32,48},{48,0},{1,17},{17,33},{33,49},{49,1},{2,18}... | collective-permute-start | bytes 393224 | tf_op jit(solution)/shard_map/ppermute | solution.py:305
  40.5 11.4 %collective-permute-start.10 = (bf16[8,32,256]{2,1,0:T(8,128)(2,1)S(1)}, bf16[8,32,256]{2,1,0:T(8,128)(2,1)S(1)}, u32[]{:S(2)}, u32[]{:S(2)}) collective-permute-start(bf16[8,32,256]{2,1,0:T(8,128)(2,1)S(1)} %weigh.1.refs_0_), channel_id=1, source_target_pairs={{0,8},{8,0},{1,9},{9,1},{2,10},{10,2},{3,11},{11,3},{4,12},{12,4},... | collective-permute-start | bytes 393224 | tf_op jit(solution)/shard_map/ppermute | solution.py:326
  44.4 7.5 %collective-permute-start.13 = (bf16[8,32,256]{2,1,0:T(8,128)(2,1)S(1)}, bf16[8,32,256]{2,1,0:T(8,128)(2,1)S(1)}, u32[]{:S(2)}, u32[]{:S(2)}) collective-permute-start(bf16[8,32,256]{2,1,0:T(8,128)(2,1)S(1)} %collective-permute-done.9.refs_3_), channel_id=1, source_target_pairs={{0,8},{8,0},{1,9},{9,1},{2,10},{10,2},{3,11},{11,3},{4,12},{12,4},... | collective-permute-start | bytes 393224 | tf_op jit(solution)/shard_map/ppermute | solution.py:326
  47.4 4.6 %collective-permute-start.12 = (bf16[8,32,256]{2,1,0:T(8,128)(2,1)S(1)}, bf16[8,32,256]{2,1,0:T(8,128)(2,1)S(1)}, u32[]{:S(2)}, u32[]{:S(2)}) collective-permute-start(bf16[8,32,256]{2,1,0:T(8,128)(2,1)S(1)} %collective-permute-done.8.refs_2_), channel_id=1, source_target_pairs={{0,8},{8,0},{1,9},{9,1},{2,10},{10,2},{3,11},{11,3},{4,12},{12,4},... | collective-permute-start | bytes 393224 | tf_op jit(solution)/shard_map/ppermute | solution.py:326
  50.0 2.3 %collective-permute-start.11 = (bf16[8,32,256]{2,1,0:T(8,128)(2,1)S(1)}, bf16[8,32,256]{2,1,0:T(8,128)(2,1)S(1)}, u32[]{:S(2)}, u32[]{:S(2)}) collective-permute-start(bf16[8,32,256]{2,1,0:T(8,128)(2,1)S(1)} %collective-permute-done.7.refs_1_), channel_id=1, source_target_pairs={{0,8},{8,0},{1,9},{9,1},{2,10},{10,2},{3,11},{11,3},{4,12},{12,4},... | collective-permute-start | bytes 393224 | tf_op jit(solution)/shard_map/ppermute | solution.py:326
  56.7 15.0 %collective-permute-start.21 = (bf16[2,32,2048]{2,1,0:T(8,128)(2,1)S(1)}, bf16[2,32,2048]{2,1,0:T(8,128)(2,1)S(1)}, u32[]{:S(2)}, u32[]{:S(2)}) collective-permute-start(bf16[2,32,2048]{2,1,0:T(8,128)(2,1)S(1)} %get-tuple-element.48), channel_id=1, source_target_pairs={{0,1},{1,2},{2,3},{3,4},{4,5},{5,6},{6,7},{7,0},{8,9},{9,10},{10,1... | collective-permute-start | bytes 786440 | tf_op jit(solution)/shard_map/ppermute | solution.py:305
  57.6 14.6 %collective-permute-start.22 = (bf16[2,32,2048]{2,1,0:T(8,128)(2,1)S(1)}, bf16[2,32,2048]{2,1,0:T(8,128)(2,1)S(1)}, u32[]{:S(2)}, u32[]{:S(2)}) collective-permute-start(bf16[2,32,2048]{2,1,0:T(8,128)(2,1)S(1)} %get-tuple-element.49), channel_id=1, source_target_pairs={{0,2},{1,3},{2,4},{3,5},{4,6},{5,7},{6,0},{7,1},{8,10},{9,11},{10,... | collective-permute-start | bytes 786440 | tf_op jit(solution)/shard_map/ppermute | solution.py:305
  60.0 18.4 %collective-permute-start.23 = (bf16[2,32,2048]{2,1,0:T(8,128)(2,1)S(1)}, bf16[2,32,2048]{2,1,0:T(8,128)(2,1)S(1)}, u32[]{:S(2)}, u32[]{:S(2)}) collective-permute-start(bf16[2,32,2048]{2,1,0:T(8,128)(2,1)S(1)} %get-tuple-element.50), channel_id=1, source_target_pairs={{0,3},{1,4},{2,5},{3,6},{4,7},{5,0},{6,1},{7,2},{8,11},{9,12},{10,... | collective-permute-start | bytes 786440 | tf_op jit(solution)/shard_map/ppermute | solution.py:305
  63.4 17.7 %collective-permute-start.24 = (bf16[2,32,2048]{2,1,0:T(8,128)(2,1)S(1)}, bf16[2,32,2048]{2,1,0:T(8,128)(2,1)S(1)}, u32[]{:S(2)}, u32[]{:S(2)}) collective-permute-start(bf16[2,32,2048]{2,1,0:T(8,128)(2,1)S(1)} %get-tuple-element.51), channel_id=1, source_target_pairs={{0,4},{1,5},{2,6},{3,7},{4,0},{5,1},{6,2},{7,3},{8,12},{9,13},{10,... | collective-permute-start | bytes 786440 | tf_op jit(solution)/shard_map/ppermute | solution.py:305
  63.4 23.4 %collective-permute-start.25 = (bf16[2,32,2048]{2,1,0:T(8,128)(2,1)S(1)}, bf16[2,32,2048]{2,1,0:T(8,128)(2,1)S(1)}, u32[]{:S(2)}, u32[]{:S(2)}) collective-permute-start(bf16[2,32,2048]{2,1,0:T(8,128)(2,1)S(1)} %get-tuple-element.52), channel_id=1, source_target_pairs={{0,5},{1,6},{2,7},{3,0},{4,1},{5,2},{6,3},{7,4},{8,13},{9,14},{10,... | collective-permute-start | bytes 786440 | tf_op jit(solution)/shard_map/ppermute | solution.py:305
  71.7 19.8 %collective-permute-start.26 = (bf16[2,32,2048]{2,1,0:T(8,128)(2,1)S(1)}, bf16[2,32,2048]{2,1,0:T(8,128)(2,1)S(1)}, u32[]{:S(2)}, u32[]{:S(2)}) collective-permute-start(bf16[2,32,2048]{2,1,0:T(8,128)(2,1)S(1)} %get-tuple-element.53), channel_id=1, source_target_pairs={{0,6},{1,7},{2,0},{3,1},{4,2},{5,3},{6,4},{7,5},{8,14},{9,15},{10,... | collective-permute-start | bytes 786440 | tf_op jit(solution)/shard_map/ppermute | solution.py:305
  72.1 20.4 %collective-permute-start.27 = (bf16[2,32,2048]{2,1,0:T(8,128)(2,1)S(1)}, bf16[2,32,2048]{2,1,0:T(8,128)(2,1)S(1)}, u32[]{:S(2)}, u32[]{:S(2)}) collective-permute-start(bf16[2,32,2048]{2,1,0:T(8,128)(2,1)S(1)} %get-tuple-element.54), channel_id=1, source_target_pairs={{0,7},{1,0},{2,1},{3,2},{4,3},{5,4},{6,5},{7,6},{8,15},{9,8},{10,9... | collective-permute-start | bytes 786440 | tf_op jit(solution)/shard_map/ppermute | solution.py:305
  78.4 31.3 %collective-permute-start.14 = (bf16[2,32,2048]{2,1,0:T(8,128)(2,1)S(1)}, bf16[2,32,2048]{2,1,0:T(8,128)(2,1)S(1)}, u32[]{:S(2)}, u32[]{:S(2)}) collective-permute-start(bf16[2,32,2048]{2,1,0:T(8,128)(2,1)S(1)} %get-tuple-element.39), channel_id=1, source_target_pairs={{0,1},{1,2},{2,3},{3,4},{4,5},{5,6},{6,7},{7,0},{8,9},{9,10},{10,1... | collective-permute-start | bytes 786440 | tf_op jit(solution)/shard_map/ppermute | solution.py:305
  81.1 28.7 %collective-permute-start.15 = (bf16[2,32,2048]{2,1,0:T(8,128)(2,1)S(1)}, bf16[2,32,2048]{2,1,0:T(8,128)(2,1)S(1)}, u32[]{:S(2)}, u32[]{:S(2)}) collective-permute-start(bf16[2,32,2048]{2,1,0:T(8,128)(2,1)S(1)} %get-tuple-element.40), channel_id=1, source_target_pairs={{0,2},{1,3},{2,4},{3,5},{4,6},{5,7},{6,0},{7,1},{8,10},{9,11},{10,... | collective-permute-start | bytes 786440 | tf_op jit(solution)/shard_map/ppermute | solution.py:305
  86.8 27.3 %collective-permute-start.16 = (bf16[2,32,2048]{2,1,0:T(8,128)(2,1)S(1)}, bf16[2,32,2048]{2,1,0:T(8,128)(2,1)S(1)}, u32[]{:S(2)}, u32[]{:S(2)}) collective-permute-start(bf16[2,32,2048]{2,1,0:T(8,128)(2,1)S(1)} %get-tuple-element.41), channel_id=1, source_target_pairs={{0,3},{1,4},{2,5},{3,6},{4,7},{5,0},{6,1},{7,2},{8,11},{9,12},{10,... | collective-permute-start | bytes 786440 | tf_op jit(solution)/shard_map/ppermute | solution.py:305
  91.5 22.6 %collective-permute-start.17 = (bf16[2,32,2048]{2,1,0:T(8,128)(2,1)S(1)}, bf16[2,32,2048]{2,1,0:T(8,128)(2,1)S(1)}, u32[]{:S(2)}, u32[]{:S(2)}) collective-permute-start(bf16[2,32,2048]{2,1,0:T(8,128)(2,1)S(1)} %get-tuple-element.42), channel_id=1, source_target_pairs={{0,4},{1,5},{2,6},{3,7},{4,0},{5,1},{6,2},{7,3},{8,12},{9,13},{10,... | collective-permute-start | bytes 786440 | tf_op jit(solution)/shard_map/ppermute | solution.py:305
  92.5 22.3 %collective-permute-start.18 = (bf16[2,32,2048]{2,1,0:T(8,128)(2,1)S(1)}, bf16[2,32,2048]{2,1,0:T(8,128)(2,1)S(1)}, u32[]{:S(2)}, u32[]{:S(2)}) collective-permute-start(bf16[2,32,2048]{2,1,0:T(8,128)(2,1)S(1)} %get-tuple-element.43), channel_id=1, source_target_pairs={{0,5},{1,6},{2,7},{3,0},{4,1},{5,2},{6,3},{7,4},{8,13},{9,14},{10,... | collective-permute-start | bytes 786440 | tf_op jit(solution)/shard_map/ppermute | solution.py:305
  109.7 11.5 %collective-permute-start.19 = (bf16[2,32,2048]{2,1,0:T(8,128)(2,1)S(1)}, bf16[2,32,2048]{2,1,0:T(8,128)(2,1)S(1)}, u32[]{:S(2)}, u32[]{:S(2)}) collective-permute-start(bf16[2,32,2048]{2,1,0:T(8,128)(2,1)S(1)} %get-tuple-element.44), channel_id=1, source_target_pairs={{0,6},{1,7},{2,0},{3,1},{4,2},{5,3},{6,4},{7,5},{8,14},{9,15},{10,... | collective-permute-start | bytes 786440 | tf_op jit(solution)/shard_map/ppermute | solution.py:305
  109.8 16.3 %collective-permute-start.20 = (bf16[2,32,2048]{2,1,0:T(8,128)(2,1)S(1)}, bf16[2,32,2048]{2,1,0:T(8,128)(2,1)S(1)}, u32[]{:S(2)}, u32[]{:S(2)}) collective-permute-start(bf16[2,32,2048]{2,1,0:T(8,128)(2,1)S(1)} %get-tuple-element.45), channel_id=1, source_target_pairs={{0,7},{1,0},{2,1},{3,2},{4,3},{5,4},{6,5},{7,6},{8,15},{9,8},{10,9... | collective-permute-start | bytes 786440 | tf_op jit(solution)/shard_map/ppermute | solution.py:305
where the time goes:
time: 129 us; the launch traced here: 128 us
  starting transfers between devices  77.1 us (60%)
  waiting for transfers between devices  30 us (23%)
  Pallas kernels  20.8 us (16%)
    ppermute x23, starting transfers between devices, passed_on(): lax.ppermute(pieces[d], axis, [(i, (i + d) % count) for i in range(count)])  63 us
    ppermute x23, waiting for transfers between devices, passed_on(): lax.ppermute(pieces[d], axis, [(i, (i + d) % count) for i in range(count)])  28.1 us
    ppermute x4, starting transfers between devices, local(): weights = own + [lax.ppermute(x, 'core', swap) for x in own]  10.8 us
    pallas_call x2, Pallas kernels, spread_out(): pl.pallas_call(spread_out_kernel, grid_spec=pltpu.PrefetchScalarGridSpec(...  8.82 us
    pallas_call x1, Pallas kernels, own_sum(): pl.pallas_call(own_sum_kernel, grid_spec=pltpu.PrefetchScalarGridSpec(num...  6.48 us
    pallas_call x2, Pallas kernels, finish(): pl.pallas_call(finish_kernel, grid_spec=pltpu.PrefetchScalarGridSpec(num_...  3.91 us
    ppermute x1, starting transfers between devices, local(): pieces = chip_sum(keep, lax.ppermute(send, 'core', swap))  3.29 us
  transfers between devices with their start and end apart: 28, of which 11 were waited for; matrix products, arithmetic and copies ran while one was open for 0% of the time, Pallas kernels for 5%

commit v1 on v0

v1 whole, which is shorter than its diff:
```python
import functools

import jax
import jax.numpy as jnp
from jax import lax
from jax.experimental import pallas as pl
from jax.experimental.pallas import tpu as pltpu
from jax.sharding import Mesh
from jax.sharding import PartitionSpec as P


F32 = jnp.float32
BF16 = jnp.bfloat16
ZH, Y, CORE = 4, 4, 2
LATS = 8
LAT = "lat"
EACH = 4
GROUPS = ((0, 1), (1, 2), (3, 1))
ORDER = (6, 4, 2, 5, 7, 1, 3)


def nt_dot(a, b):
    return lax.dot_general(a, b, (((1,), (1,)), ((), ())), preferred_element_type=F32)


def half_sum_kernel(other, here_ref, spread_ref, controls_ref, out_ref, kept_ref, controls_buf, sems):
    step = out_ref.shape[1]
    copies = []
    for d in range(Y):
        at = ((here_ref[0] ^ other) * Y + ((here_ref[1] + d) & (Y - 1))) * step
        pair = (
            pltpu.make_async_copy(
                spread_ref.at[:, pl.ds(at, step)], kept_ref.at[d], sems.at[0, d]
            ),
            pltpu.make_async_copy(
                controls_ref.at[:, pl.ds(at, step)], controls_buf.at[d], sems.at[1, d]
            ),
        )
        for copy in pair:
            copy.start()
        copies.append(pair)
    for d, pair in enumerate(copies):
        for copy in pair:
            copy.wait()
        for l in range(step):
            total = kept_ref[d, 0, l].astype(F32) * controls_buf[d, 0, l].astype(F32)
            for k in range(1, kept_ref.shape[1]):
                total += kept_ref[d, k, l].astype(F32) * controls_buf[d, k, l].astype(F32)
            out_ref[d, l] = total.astype(out_ref.dtype)


def half_sum(other, here, spread, controls, dtype):
    members, levels, rows, cols = spread.shape
    step = levels // (CORE * Y)
    smem, vmem = (pl.BlockSpec(memory_space=space) for space in (pltpu.SMEM, pltpu.VMEM))
    hbm = pl.BlockSpec(memory_space=pltpu.HBM)
    field = (Y, members, step, rows, cols)
    return pl.pallas_call(
        functools.partial(half_sum_kernel, other),
        in_specs=[smem, hbm, hbm],
        out_specs=[vmem, vmem],
        out_shape=[
            jax.ShapeDtypeStruct((Y, step, rows, cols), dtype),
            jax.ShapeDtypeStruct(field, BF16),
        ],
        scratch_shapes=[pltpu.VMEM(field, BF16), pltpu.SemaphoreType.DMA((2, Y))],
        compiler_params=pltpu.CompilerParams(vmem_limit_bytes=12 * 1024 * 1024),
        cost_estimate=pl.CostEstimate(
            flops=300_000_000, bytes_accessed=4_200_000, transcendentals=0
        ),
    )(here, spread, controls)


def chip_sum_kernel(keep_ref, arrived_ref, *outs):
    for d, out in enumerate(outs):
        for l in range(out.shape[0]):
            out[l] = (keep_ref[d, l] + arrived_ref[d, l].astype(F32)).astype(out.dtype)


def chip_sum(keep, arrived):
    vmem = pl.BlockSpec(memory_space=pltpu.VMEM)
    return pl.pallas_call(
        chip_sum_kernel,
        in_specs=[vmem] * 2,
        out_specs=[vmem] * Y,
        out_shape=[
            jax.ShapeDtypeStruct(keep.shape[1:], BF16 if d else F32) for d in range(Y)
        ],
        compiler_params=pltpu.CompilerParams(vmem_limit_bytes=8 * 1024 * 1024),
        name="chip_sum",
    )(keep, arrived)


def tables_kernel(here_ref, vert_ref, lon_ref, lat_ref, big_ref, lon_out_ref, turned_ref):
    me = here_ref[2]
    levels = vert_ref.shape[0]
    size = levels * 8
    row = lax.broadcasted_iota(jnp.int32, (size, levels), 0) >> 3
    col = lax.broadcasted_iota(jnp.int32, (size, levels), 1)
    source = (row & ~3) | ((row + 8 - me) & 3)
    pick_out = jnp.where(source == col, 1.0, 0.0).astype(BF16)
    piece, step = row >> 3, levels // (CORE * Y)
    core = here_ref[0] ^ (piece >> 2)
    held = (core * Y + ((here_ref[1] + 8 - piece) & (Y - 1))) * step + (row & 7)
    pick_in = jnp.where(held == col, 1.0, 0.0).astype(BF16)
    tall = jnp.dot(pick_out, vert_ref[...], preferred_element_type=F32).astype(BF16)
    wide = nt_dot(tall, pick_in)
    r = lax.broadcasted_iota(jnp.int32, (size, size), 0) & 7
    c = lax.broadcasted_iota(jnp.int32, (size, size), 1) & 7
    big_ref[...] = jnp.where(r == c, wide, 0.0).astype(BF16)
    share = lon_ref.shape[0] // LATS
    for d in range(LATS):
        at = pl.multiple_of(((me + d) & (LATS - 1)) * share, share)
        lon_out_ref[share * d : share * d + share, :] = lon_ref[pl.ds(at, share), :]
    rows = lat_ref.shape[0]
    from_col = lax.broadcasted_iota(jnp.int32, (rows, rows), 0)
    to_col = lax.broadcasted_iota(jnp.int32, (rows, rows), 1)
    for turn in range(EACH):
        back = EACH * (to_col >> 7) + ((turn - (to_col >> 5)) & 3)
        want = (((me + 16 - back) & (LATS - 1)) << 5) | (to_col & 31)
        move = jnp.where(from_col == want, 1.0, 0.0).astype(BF16)
        turned_ref[turn] = jnp.dot(
            lat_ref[...], move, preferred_element_type=F32
        ).astype(BF16)


def tables(here, vert_loc, lon_loc, lat_loc):
    levels = vert_loc.shape[0]
    size = lat_loc.shape[0]
    return pl.pallas_call(
        tables_kernel,
        in_specs=[pl.BlockSpec(memory_space=pltpu.SMEM)]
        + [pl.BlockSpec(memory_space=pltpu.VMEM)] * 3,
        out_specs=[pl.BlockSpec(memory_space=pltpu.VMEM)] * 3,
        out_shape=[
            jax.ShapeDtypeStruct((levels * 8, levels * 8), BF16),
            jax.ShapeDtypeStruct(lon_loc.shape, BF16),
            jax.ShapeDtypeStruct((EACH, size, size), BF16),
        ],
        compiler_params=pltpu.CompilerParams(vmem_limit_bytes=16 * 1024 * 1024),
        cost_estimate=pl.CostEstimate(
            flops=600_000_000, bytes_accessed=2_000_000, transcendentals=0
        ),
        name="tables",
    )(here, vert_loc, lon_loc, lat_loc)


def join_kernel(*refs):
    *pieces, out_ref = refs
    for l in range(out_ref.shape[0]):
        total = pieces[0][l].astype(F32)
        for piece in pieces[1:]:
            total += piece[l].astype(F32)
        out_ref[l] = total.astype(BF16)


def join(pieces):
    vmem = pl.BlockSpec(memory_space=pltpu.VMEM)
    return pl.pallas_call(
        join_kernel,
        in_specs=[vmem] * len(pieces),
        out_specs=vmem,
        out_shape=jax.ShapeDtypeStruct(pieces[0].shape, BF16),
        compiler_params=pltpu.CompilerParams(vmem_limit_bytes=8 * 1024 * 1024),
        name="join",
    )(*pieces)


def weigh_kernel(here_ref, classes_ref, table_ref, *refs):
    *pieces, out_ref = refs
    classes = classes_ref[...]
    first = (here_ref[0] * Y + here_ref[1]) * out_ref.shape[0]
    numbers = range(1, table_ref.shape[0])
    at = [classes == n for n in numbers]
    for l in range(out_ref.shape[0]):
        total = pieces[0][l].astype(F32)
        for piece in pieces[1:]:
            total += piece[l].astype(F32)
        precision = jnp.full(classes.shape, table_ref[0, first + l], F32)
        for n in numbers:
            precision = jnp.where(at[n - 1], table_ref[n, first + l], precision)
        out_ref[l] = (total * precision).astype(BF16)


def weigh(here, classes, prec_table, pieces):
    vmem = pl.BlockSpec(memory_space=pltpu.VMEM)
    smem = pl.BlockSpec(memory_space=pltpu.SMEM)
    return pl.pallas_call(
        weigh_kernel,
        in_specs=[smem, vmem, smem] + [vmem] * len(pieces),
        out_specs=vmem,
        out_shape=jax.ShapeDtypeStruct(pieces[0].shape, BF16),
        compiler_params=pltpu.CompilerParams(vmem_limit_bytes=8 * 1024 * 1024),
        name="weigh",
    )(here, classes, prec_table, *pieces)


def spread_out_kernel(first, *refs):
    pieces = CORE * Y
    weights, kept, refs = refs[:pieces], refs[pieces : pieces + CORE], refs[pieces + CORE :]
    big_ref, lon_ref, outs = refs[0], refs[1], refs[2 : 2 + LATS]
    adj, mixed = refs[2 + LATS :]
    levels, rows, cols = adj.shape
    step = levels // pieces
    share = cols // LATS

    def member(k):
        for low in range(0, rows, 16):
            for n, piece in enumerate(weights):
                for i in range(step):
                    own = kept[n // Y][-n % Y, first + k, i, low : low + 16, :]
                    weight = piece[i, low : low + 16, :]
                    adj[n * step + i, low : low + 16, :] = own.astype(F32) * weight.astype(F32)
            for at in range(low, low + 16, 8):
                x = adj[:, at : at + 8, :].reshape(levels * 8, cols).astype(BF16)
                y = jnp.dot(big_ref[...], x, preferred_element_type=F32)
                mixed[:, at : at + 8, :] = y.reshape(levels, 8, cols)
        block = 256 // rows
        for n in range(levels // block):
            x = mixed[block * n : block * n + block].reshape(256, cols).astype(BF16)
            y = nt_dot(lon_ref[...], x).astype(BF16)
            for d, out in enumerate(outs):
                out[k, :, 256 * n : 256 * n + 256] = y[share * d : share * d + share]

    count = outs[0].shape[0]
    if count == 1:
        member(0)
    else:
        pl.loop(0, count)(member)


def spread_out(weights, kept, big, lon, first, count):
    levels = len(weights) * weights[0].shape[0]
    _, rows, cols = weights[0].shape
    share = cols // LATS
    vmem = pl.BlockSpec(memory_space=pltpu.VMEM)
    args = (*weights, *kept, big, lon)
    return pl.pallas_call(
        functools.partial(spread_out_kernel, first),
        in_specs=[vmem] * len(args),
        out_specs=[vmem] * LATS,
        out_shape=[jax.ShapeDtypeStruct((count, share, levels * rows), BF16)] * LATS,
        scratch_shapes=[pltpu.VMEM((levels, rows, cols), F32)] * 2,
        compiler_params=pltpu.CompilerParams(vmem_limit_bytes=24 * 1024 * 1024),
        cost_estimate=pl.CostEstimate(
            flops=count * 1_500_000_000, bytes_accessed=count * 2_500_000, transcendentals=0
        ),
        name="spread_out",
    )(*args)


def finish_kernel(here_ref, *refs):
    parts = refs[:LATS]
    turned_ref, out_ref = refs[LATS], refs[-1]
    k, h = pl.program_id(0), pl.program_id(1)
    share = parts[0].shape[1]
    groups = out_ref.shape[1] // EACH
    lane = lax.broadcasted_iota(jnp.int32, (share, 128), 1) >> 5
    at = [lane == q for q in range(3)]
    for turn in range(EACH):
        lines = []
        for g in range(groups):
            lanes = pl.ds(pl.multiple_of((h * groups + g) * 128, 128), 128)
            sides = []
            for part in range(2):
                tiles = [parts[EACH * part + (turn - q) % EACH][k, :, lanes] for q in range(EACH)]
                side = tiles[3]
                for q in range(3):
                    side = jnp.where(at[q], tiles[q], side)
                sides.append(side)
            lines.append(jnp.concatenate(sides, axis=1))
        x = jnp.concatenate(lines, axis=0)
        y = nt_dot(x, turned_ref[turn]).astype(BF16)
        level = (turn + 8 - here_ref[2]) & 3
        for g in range(groups):
            out_ref[0, EACH * g + level] = y[share * g : share * g + share]


def finish(here, parts, turned, first, members, so_far=None):
    count, share, wide = parts[0].shape
    size = turned.shape[1]
    levels = wide // 32
    args = (*parts, turned) if so_far is None else (*parts, turned, so_far)
    extra = [] if so_far is None else [pl.BlockSpec(memory_space=pl.ANY)]
    vmem = pl.BlockSpec(memory_space=pltpu.VMEM)
    return pl.pallas_call(
        finish_kernel,
        grid_spec=pltpu.PrefetchScalarGridSpec(
            num_scalar_prefetch=1,
            grid=(count, 2),
            in_specs=[vmem] * (LATS + 1) + extra,
            out_specs=pl.BlockSpec(
                (1, levels // 2, share, size), lambda k, h, s: (first + k, h, 0, 0)
            ),
        ),
        out_shape=jax.ShapeDtypeStruct((members, levels, share, size), BF16),
        input_output_aliases={} if so_far is None else {len(args): 0},
        compiler_params=pltpu.CompilerParams(
            dimension_semantics=("arbitrary", "arbitrary"), vmem_limit_bytes=16 * 1024 * 1024
        ),
        cost_estimate=pl.CostEstimate(
            flops=count * 700_000_000, bytes_accessed=count * 2_500_000, transcendentals=0
        ),
        name="finish",
    )(here, *args)


def passed_on(axis, pieces, order):
    count = len(pieces)
    parts = [pieces[0]] + [None] * (count - 1)
    for d in order:
        parts[d] = lax.ppermute(pieces[d], axis, [(i, (i + d) % count) for i in range(count)])
    return parts


def local(controls, spread, classes, prec_table, vert_loc, lon_loc, lat_loc):
    controls = pltpu.with_memory_space_constraint(controls, pltpu.HBM)
    spread = pltpu.with_memory_space_constraint(spread, pltpu.HBM)
    members = spread.shape[0]
    here = jnp.stack([lax.axis_index(name) for name in ("core", "y", LAT)])
    swap = [(0, 1), (1, 0)]

    big, lon, turned = tables(here, vert_loc, lon_loc, lat_loc)
    send, kept_other = half_sum(1, here, spread, controls, BF16)
    keep, kept_own = half_sum(0, here, spread, controls, F32)
    arrived = lax.ppermute(send, "core", swap)
    pieces = chip_sum(keep, arrived)
    along_y = join(passed_on("y", pieces, range(1, Y)))
    along_z = passed_on("zh", [along_y] * ZH, range(1, ZH))
    weighted = weigh(here, classes, prec_table, along_z)
    own = passed_on("y", [weighted] * Y, range(1, Y))
    weights = own + [lax.ppermute(x, "core", swap) for x in own]

    result = None
    for start, count in GROUPS:
        sending = spread_out(weights, (kept_own, kept_other), big, lon, start, count)
        parts = passed_on(LAT, sending, ORDER)
        result = finish(here, parts, turned, start, members, result)
    return result


def solution(mesh):
    finer = Mesh(
        mesh.devices.reshape(ZH, Y, CORE, mesh.shape["lat"]), ("zh", "y", "core", LAT)
    )
    members = P(("zh", "y", "core"), None, LAT, None)
    return jax.shard_map(
        local,
        mesh=finer,
        in_specs=(members, members, P(LAT, None), P(), P(), P(), P()),
        out_specs=members,
        check_vma=False,
    )
```

time: 129 us -> 124 us (0.961)
  the two profiles are of different devices: /device:TPU:1 before, /device:TPU:6 now
where the time goes in v1:
time: 124 us
  starting transfers between devices  54.9 us (44%)
  waiting for transfers between devices  48.4 us (39%)
  Pallas kernels  20.3 us (16%)
    ppermute x30, starting transfers between devices, passed_on(): lax.ppermute(pieces[d], axis, [(i, (i + d) % count) for i in range(count)])  54.8 us
    ppermute x30, waiting for transfers between devices, passed_on(): lax.ppermute(pieces[d], axis, [(i, (i + d) % count) for i in range(count)])  48.3 us
    pallas_call x3, Pallas kernels, finish(): pl.pallas_call(finish_kernel, grid_spec=pltpu.PrefetchScalarGridSpec(num_...  8.12 us
    pallas_call x2, Pallas kernels, half_sum(): pl.pallas_call(functools.partial(half_sum_kernel, other), in_specs=[smem,...  5.69 us
    pallas_call x3, Pallas kernels, spread_out(): pl.pallas_call(functools.partial(spread_out_kernel, first), in_specs=[vme...  4.38 us
  transfers between devices with their start and end apart: 35, of which 17 were waited for; matrix products, arithmetic and copies ran while one was open for 0% of the time, Pallas kernels for 11%

profile of v1, /device:TPU:6, one launch (start us, length us, event | category | flops | bytes accessed | tf_op | source)
XLA Modules:
  0.0 123.9 jit_solution(15017965333306119262)
XLA Ops:
  0.1 2.9 %shard_map.74 = (bf16[4,8,32,256]{3,2,1,0:T(8,128)(2,1)S(1)}, bf16[4,4,8,32,256]{4,3,2,1,0:T(8,128)(2,1)S(1)}) custom-call(s32[3]{0:T(128)S(1)} %pad_add_fusion.here_ref, bf16[4,64,32,256]{3,2,1,0:T(8,128)(2,1)} %spread_ref.3, bf16[4,64,32,256]{3,2,1,0:T(8,128)(2,1)} %controls_ref.3), custom_call_target="tpu_custom_call" | custom-call | flops 300000000 | bytes 4200000 | tf_op jit(solution)/shard_map/pallas_call | solution.py:58
  3.1 2.8 %shard_map.73 = (f32[4,8,32,256]{3,2,1,0:T(8,128)S(1)}, bf16[4,4,8,32,256]{4,3,2,1,0:T(8,128)(2,1)S(1)}) custom-call(s32[3]{0:T(128)S(1)} %pad_add_fusion.here_ref, bf16[4,64,32,256]{3,2,1,0:T(8,128)(2,1)} %spread_ref.3, bf16[4,64,32,256]{3,2,1,0:T(8,128)(2,1)} %controls_ref.3), custom_call_target="tpu_custom_call" | custom-call | flops 300000000 | bytes 4200000 | tf_op jit(solution)/shard_map/pallas_call | solution.py:58
  6.1 1.7 %collective-permute-start.1 = (bf16[8,32,256]{2,1,0:T(8,128)(2,1)S(1)}, bf16[8,32,256]{2,1,0:T(8,128)(2,1)S(1)}, u32[]{:S(2)}, u32[]{:S(2)}) collective-permute-start(bf16[8,32,256]{2,1,0:T(8,128)(2,1)S(1)} %get-tuple-element.43), channel_id=1, source_target_pairs={{0,16},{16,32},{32,48},{48,0},{1,17},{17,33},{33,49},{49,1},{2,18}... | collective-permute-start | bytes 393224 | tf_op jit(solution)/shard_map/ppermute | solution.py:312
  7.7 2.9 %collective-permute-start.2 = (bf16[8,32,256]{2,1,0:T(8,128)(2,1)S(1)}, bf16[8,32,256]{2,1,0:T(8,128)(2,1)S(1)}, u32[]{:S(2)}, u32[]{:S(2)}) collective-permute-start(bf16[8,32,256]{2,1,0:T(8,128)(2,1)S(1)} %get-tuple-element.44), channel_id=1, source_target_pairs={{0,32},{16,48},{32,0},{48,16},{1,33},{17,49},{33,1},{49,17},{2,34}... | collective-permute-start | bytes 393224 | tf_op jit(solution)/shard_map/ppermute | solution.py:312
  10.6 1.3 %collective-permute-start.3 = (bf16[8,32,256]{2,1,0:T(8,128)(2,1)S(1)}, bf16[8,32,256]{2,1,0:T(8,128)(2,1)S(1)}, u32[]{:S(2)}, u32[]{:S(2)}) collective-permute-start(bf16[8,32,256]{2,1,0:T(8,128)(2,1)S(1)} %get-tuple-element.45), channel_id=1, source_target_pairs={{0,48},{16,0},{32,16},{48,32},{1,49},{17,1},{33,17},{49,33},{2,50}... | collective-permute-start | bytes 393224 | tf_op jit(solution)/shard_map/ppermute | solution.py:312
  12.0 1.4 %collective-permute-done.1.refs_1_ = bf16[8,32,256]{2,1,0:T(8,128)(2,1)S(1)} collective-permute-done((bf16[8,32,256]{2,1,0:T(8,128)(2,1)S(1)}, bf16[8,32,256]{2,1,0:T(8,128)(2,1)S(1)}, u32[]{:S(2)}, u32[]{:S(2)}) %collective-permute-start.1) | collective-permute-done | bytes 131104 | tf_op jit(solution)/shard_map/ppermute | solution.py:312
  13.3 4.0 %collective-permute-done.2.refs_2_ = bf16[8,32,256]{2,1,0:T(8,128)(2,1)S(1)} collective-permute-done((bf16[8,32,256]{2,1,0:T(8,128)(2,1)S(1)}, bf16[8,32,256]{2,1,0:T(8,128)(2,1)S(1)}, u32[]{:S(2)}, u32[]{:S(2)}) %collective-permute-start.2) | collective-permute-done | bytes 131104 | tf_op jit(solution)/shard_map/ppermute | solution.py:312
  17.4 6.4 %collective-permute-start.6 = (bf16[8,32,256]{2,1,0:T(8,128)(2,1)S(1)}, bf16[8,32,256]{2,1,0:T(8,128)(2,1)S(1)}, u32[]{:S(2)}, u32[]{:S(2)}) collective-permute-start(bf16[8,32,256]{2,1,0:T(8,128)(2,1)S(1)} %join.1.refs_0_), channel_id=1, source_target_pairs={{0,192},{64,0},{128,64},{192,128},{1,193},{65,1},{129,65},{193,129... | collective-permute-start | bytes 393224 | tf_op jit(solution)/shard_map/ppermute | solution.py:312
  23.8 1.0 collective-permute-start.5
  24.8 2.8 %collective-permute-start.4 = (bf16[8,32,256]{2,1,0:T(8,128)(2,1)S(1)}, bf16[8,32,256]{2,1,0:T(8,128)(2,1)S(1)}, u32[]{:S(2)}, u32[]{:S(2)}) collective-permute-start(bf16[8,32,256]{2,1,0:T(8,128)(2,1)S(1)} %join.1.refs_0_), channel_id=1, source_target_pairs={{0,64},{64,128},{128,192},{192,0},{1,65},{65,129},{129,193},{193,1... | collective-permute-start | bytes 393224 | tf_op jit(solution)/shard_map/ppermute | solution.py:312
  27.6 7.2 %collective-permute-done.6.refs_3_ = bf16[8,32,256]{2,1,0:T(8,128)(2,1)S(1)} collective-permute-done((bf16[8,32,256]{2,1,0:T(8,128)(2,1)S(1)}, bf16[8,32,256]{2,1,0:T(8,128)(2,1)S(1)}, u32[]{:S(2)}, u32[]{:S(2)}) %collective-permute-start.6) | collective-permute-done | bytes 131104 | tf_op jit(solution)/shard_map/ppermute | solution.py:312
  34.8 1.8 %collective-permute-done.5.refs_2_ = bf16[8,32,256]{2,1,0:T(8,128)(2,1)S(1)} collective-permute-done((bf16[8,32,256]{2,1,0:T(8,128)(2,1)S(1)}, bf16[8,32,256]{2,1,0:T(8,128)(2,1)S(1)}, u32[]{:S(2)}, u32[]{:S(2)}) %collective-permute-start.5) | collective-permute-done | bytes 131104 | tf_op jit(solution)/shard_map/ppermute | solution.py:312
  36.6 0.8 weigh.1.refs_0_
  37.4 2.5 %collective-permute-start.9 = (bf16[8,32,256]{2,1,0:T(8,128)(2,1)S(1)}, bf16[8,32,256]{2,1,0:T(8,128)(2,1)S(1)}, u32[]{:S(2)}, u32[]{:S(2)}) collective-permute-start(bf16[8,32,256]{2,1,0:T(8,128)(2,1)S(1)} %weigh.1.refs_0_), channel_id=1, source_target_pairs={{0,48},{16,0},{32,16},{48,32},{1,49},{17,1},{33,17},{49,33},{2,50}... | collective-permute-start | bytes 393224 | tf_op jit(solution)/shard_map/ppermute | solution.py:312
  40.2 0.8 collective-permute-start.7
  40.9 2.8 %collective-permute-done.9.refs_3_ = bf16[8,32,256]{2,1,0:T(8,128)(2,1)S(1)} collective-permute-done((bf16[8,32,256]{2,1,0:T(8,128)(2,1)S(1)}, bf16[8,32,256]{2,1,0:T(8,128)(2,1)S(1)}, u32[]{:S(2)}, u32[]{:S(2)}) %collective-permute-start.9) | collective-permute-done | bytes 131104 | tf_op jit(solution)/shard_map/ppermute | solution.py:312
  43.8 2.6 %collective-permute-done.8.refs_2_ = bf16[8,32,256]{2,1,0:T(8,128)(2,1)S(1)} collective-permute-done((bf16[8,32,256]{2,1,0:T(8,128)(2,1)S(1)}, bf16[8,32,256]{2,1,0:T(8,128)(2,1)S(1)}, u32[]{:S(2)}, u32[]{:S(2)}) %collective-permute-start.8) | collective-permute-done | bytes 131104 | tf_op jit(solution)/shard_map/ppermute | solution.py:312
  46.4 1.3 %collective-permute-done.7.refs_1_ = bf16[8,32,256]{2,1,0:T(8,128)(2,1)S(1)} collective-permute-done((bf16[8,32,256]{2,1,0:T(8,128)(2,1)S(1)}, bf16[8,32,256]{2,1,0:T(8,128)(2,1)S(1)}, u32[]{:S(2)}, u32[]{:S(2)}) %collective-permute-start.7) | collective-permute-done | bytes 131104 | tf_op jit(solution)/shard_map/ppermute | solution.py:312
  47.7 1.2 tables.1
  49.1 1.1 spread_out.5
  50.2 2.8 %collective-permute-start.28 = (bf16[1,32,2048]{2,1,0:T(8,128)(2,1)S(1)}, bf16[1,32,2048]{2,1,0:T(8,128)(2,1)S(1)}, u32[]{:S(2)}, u32[]{:S(2)}) collective-permute-start(bf16[1,32,2048]{2,1,0:T(8,128)(2,1)S(1)} %get-tuple-element.68), channel_id=1, source_target_pairs={{0,1},{1,2},{2,3},{3,4},{4,5},{5,6},{6,7},{7,0},{8,9},{9,10},{10,1... | collective-permute-start | bytes 393224 | tf_op jit(solution)/shard_map/ppermute | solution.py:312
  53.0 2.4 %collective-permute-start.29 = (bf16[1,32,2048]{2,1,0:T(8,128)(2,1)S(1)}, bf16[1,32,2048]{2,1,0:T(8,128)(2,1)S(1)}, u32[]{:S(2)}, u32[]{:S(2)}) collective-permute-start(bf16[1,32,2048]{2,1,0:T(8,128)(2,1)S(1)} %get-tuple-element.69), channel_id=1, source_target_pairs={{0,2},{1,3},{2,4},{3,5},{4,6},{5,7},{6,0},{7,1},{8,10},{9,11},{10,... | collective-permute-start | bytes 393224 | tf_op jit(solution)/shard_map/ppermute | solution.py:312
  55.4 1.4 %collective-permute-start.31 = (bf16[1,32,2048]{2,1,0:T(8,128)(2,1)S(1)}, bf16[1,32,2048]{2,1,0:T(8,128)(2,1)S(1)}, u32[]{:S(2)}, u32[]{:S(2)}) collective-permute-start(bf16[1,32,2048]{2,1,0:T(8,128)(2,1)S(1)} %get-tuple-element.71), channel_id=1, source_target_pairs={{0,4},{1,5},{2,6},{3,7},{4,0},{5,1},{6,2},{7,3},{8,12},{9,13},{10,... | collective-permute-start | bytes 393224 | tf_op jit(solution)/shard_map/ppermute | solution.py:312
  56.8 1.9 %collective-permute-start.32 = (bf16[1,32,2048]{2,1,0:T(8,128)(2,1)S(1)}, bf16[1,32,2048]{2,1,0:T(8,128)(2,1)S(1)}, u32[]{:S(2)}, u32[]{:S(2)}) collective-permute-start(bf16[1,32,2048]{2,1,0:T(8,128)(2,1)S(1)} %get-tuple-element.72), channel_id=1, source_target_pairs={{0,5},{1,6},{2,7},{3,0},{4,1},{5,2},{6,3},{7,4},{8,13},{9,14},{10,... | collective-permute-start | bytes 393224 | tf_op jit(solution)/shard_map/ppermute | solution.py:312
  58.6 2.2 %spread_out.4 = (bf16[2,32,2048]{2,1,0:T(8,128)(2,1)S(1)}, bf16[2,32,2048]{2,1,0:T(8,128)(2,1)S(1)}, bf16[2,32,2048]{2,1,0:T(8,128)(2,1)S(1)}, bf16[2,32,2048]{2...) custom-call(bf16[8,32,256]{2,1,0:T(8,128)(2,1)S(1)} %weigh.1.refs_0_, ...), custom_call_target="tpu_custom_call" | custom-call | flops 3000000000 | bytes 5000000 | tf_op jit(solution)/shard_map/spread_out/pallas_call | solution.py:238
  60.8 1.0 collective-permute-start.33
  61.9 1.1 collective-permute-done.29.refs_2_
  63.0 1.8 %collective-permute-start.21 = (bf16[2,32,2048]{2,1,0:T(8,128)(2,1)S(1)}, bf16[2,32,2048]{2,1,0:T(8,128)(2,1)S(1)}, u32[]{:S(2)}, u32[]{:S(2)}) collective-permute-start(bf16[2,32,2048]{2,1,0:T(8,128)(2,1)S(1)} %get-tuple-element.60), channel_id=1, source_target_pairs={{0,1},{1,2},{2,3},{3,4},{4,5},{5,6},{6,7},{7,0},{8,9},{9,10},{10,1... | collective-permute-start | bytes 786440 | tf_op jit(solution)/shard_map/ppermute | solution.py:312
  64.7 1.7 %collective-permute-start.22 = (bf16[2,32,2048]{2,1,0:T(8,128)(2,1)S(1)}, bf16[2,32,2048]{2,1,0:T(8,128)(2,1)S(1)}, u32[]{:S(2)}, u32[]{:S(2)}) collective-permute-start(bf16[2,32,2048]{2,1,0:T(8,128)(2,1)S(1)} %get-tuple-element.61), channel_id=1, source_target_pairs={{0,2},{1,3},{2,4},{3,5},{4,6},{5,7},{6,0},{7,1},{8,10},{9,11},{10,... | collective-permute-start | bytes 786440 | tf_op jit(solution)/shard_map/ppermute | solution.py:312
  66.4 1.1 spread_out.3
  67.5 0.9 collective-permute-start.34
  68.7 3.0 %collective-permute-start.14 = (bf16[1,32,2048]{2,1,0:T(8,128)(2,1)S(1)}, bf16[1,32,2048]{2,1,0:T(8,128)(2,1)S(1)}, u32[]{:S(2)}, u32[]{:S(2)}) collective-permute-start(bf16[1,32,2048]{2,1,0:T(8,128)(2,1)S(1)} %get-tuple-element.51), channel_id=1, source_target_pairs={{0,1},{1,2},{2,3},{3,4},{4,5},{5,6},{6,7},{7,0},{8,9},{9,10},{10,1... | collective-permute-start | bytes 393224 | tf_op jit(solution)/shard_map/ppermute | solution.py:312
  71.8 0.9 collective-permute-start.15
  72.6 4.3 %collective-permute-done.34.refs_7_ = bf16[1,32,2048]{2,1,0:T(8,128)(2,1)S(1)} collective-permute-done((bf16[1,32,2048]{2,1,0:T(8,128)(2,1)S(1)}, bf16[1,32,2048]{2,1,0:T(8,128)(2,1)S(1)}, u32[]{:S(2)}, u32[]{:S(2)}) %collective-permute-start.34) | collective-permute-done | bytes 131104 | tf_op jit(solution)/shard_map/ppermute | solution.py:312
  76.9 9.3 %collective-permute-start.23 = (bf16[2,32,2048]{2,1,0:T(8,128)(2,1)S(1)}, bf16[2,32,2048]{2,1,0:T(8,128)(2,1)S(1)}, u32[]{:S(2)}, u32[]{:S(2)}) collective-permute-start(bf16[2,32,2048]{2,1,0:T(8,128)(2,1)S(1)} %get-tuple-element.62), channel_id=1, source_target_pairs={{0,3},{1,4},{2,5},{3,6},{4,7},{5,0},{6,1},{7,2},{8,11},{9,12},{10,... | collective-permute-start | bytes 786440 | tf_op jit(solution)/shard_map/ppermute | solution.py:312
  86.2 3.7 %collective-permute-done.14.refs_1_ = bf16[1,32,2048]{2,1,0:T(8,128)(2,1)S(1)} collective-permute-done((bf16[1,32,2048]{2,1,0:T(8,128)(2,1)S(1)}, bf16[1,32,2048]{2,1,0:T(8,128)(2,1)S(1)}, u32[]{:S(2)}, u32[]{:S(2)}) %collective-permute-start.14) | collective-permute-done | bytes 131104 | tf_op jit(solution)/shard_map/ppermute | solution.py:312
  90.0 2.4 %collective-permute-start.25 = (bf16[2,32,2048]{2,1,0:T(8,128)(2,1)S(1)}, bf16[2,32,2048]{2,1,0:T(8,128)(2,1)S(1)}, u32[]{:S(2)}, u32[]{:S(2)}) collective-permute-start(bf16[2,32,2048]{2,1,0:T(8,128)(2,1)S(1)} %get-tuple-element.64), channel_id=1, source_target_pairs={{0,5},{1,6},{2,7},{3,0},{4,1},{5,2},{6,3},{7,4},{8,13},{9,14},{10,... | collective-permute-start | bytes 786440 | tf_op jit(solution)/shard_map/ppermute | solution.py:312
  93.1 0.7 collective-permute-start.27
  93.8 2.3 %finish.3.refs_9_ = bf16[4,64,32,256]{3,2,1,0:T(8,128)(2,1)} custom-call(s32[3]{0:T(128)S(1)} %pad_add_fusion.here_ref, bf16[1,32,2048]{2,1,0:T(8,128)(2,1)S(1)} %get-tuple-element.67.refs_0_, bf16[1,32,2048]{2,1,0:T(8,128)(2,1)S(1)} %collective-permute-done.28.refs_1_, bf16[1,32,2048]{2,1,0:T(8,128)(2,1)S(1)} %collective-permute-done.29.refs_2_, ...), custom_call_target="tpu_custom_call" | custom-call | flops 700000000 | bytes 2500000 | tf_op jit(solution)/shard_map/finish/pallas_call | solution.py:286
  96.1 3.0 %collective-permute-start.16 = (bf16[1,32,2048]{2,1,0:T(8,128)(2,1)S(1)}, bf16[1,32,2048]{2,1,0:T(8,128)(2,1)S(1)}, u32[]{:S(2)}, u32[]{:S(2)}) collective-permute-start(bf16[1,32,2048]{2,1,0:T(8,128)(2,1)S(1)} %get-tuple-element.53), channel_id=1, source_target_pairs={{0,3},{1,4},{2,5},{3,6},{4,7},{5,0},{6,1},{7,2},{8,11},{9,12},{10,... | collective-permute-start | bytes 393224 | tf_op jit(solution)/shard_map/ppermute | solution.py:312
  99.2 1.2 collective-permute-start.17
  100.4 6.3 %collective-permute-done.25.refs_5_ = bf16[2,32,2048]{2,1,0:T(8,128)(2,1)S(1)} collective-permute-done((bf16[2,32,2048]{2,1,0:T(8,128)(2,1)S(1)}, bf16[2,32,2048]{2,1,0:T(8,128)(2,1)S(1)}, u32[]{:S(2)}, u32[]{:S(2)}) %collective-permute-start.25) | collective-permute-done | bytes 262176 | tf_op jit(solution)/shard_map/ppermute | solution.py:312
  106.7 4.3 %collective-permute-done.26.refs_6_ = bf16[2,32,2048]{2,1,0:T(8,128)(2,1)S(1)} collective-permute-done((bf16[2,32,2048]{2,1,0:T(8,128)(2,1)S(1)}, bf16[2,32,2048]{2,1,0:T(8,128)(2,1)S(1)}, u32[]{:S(2)}, u32[]{:S(2)}) %collective-permute-start.26) | collective-permute-done | bytes 262176 | tf_op jit(solution)/shard_map/ppermute | solution.py:312
  111.0 2.3 %collective-permute-done.27.refs_7_ = bf16[2,32,2048]{2,1,0:T(8,128)(2,1)S(1)} collective-permute-done((bf16[2,32,2048]{2,1,0:T(8,128)(2,1)S(1)}, bf16[2,32,2048]{2,1,0:T(8,128)(2,1)S(1)}, u32[]{:S(2)}, u32[]{:S(2)}) %collective-permute-start.27) | collective-permute-done | bytes 262176 | tf_op jit(solution)/shard_map/ppermute | solution.py:312
  113.3 3.5 %finish.4.refs_9_ = bf16[4,64,32,256]{3,2,1,0:T(8,128)(2,1)} custom-call(s32[3]{0:T(128)S(1)} %pad_add_fusion.here_ref, bf16[2,32,2048]{2,1,0:T(8,128)(2,1)S(1)} %get-tuple-element.59.refs_0_, bf16[2,32,2048]{2,1,0:T(8,128)(2,1)S(1)} %collective-permute-done.21.refs_1_, ...), custom_call_target="tpu_custom_call", output_to_operand_aliasing={{}: (10, {})} | custom-call | flops 1400000000 | bytes 5000000 | tf_op jit(solution)/shard_map/finish/pallas_call | solution.py:286
  116.9 2.3 %collective-permute-done.19.refs_6_ = bf16[1,32,2048]{2,1,0:T(8,128)(2,1)S(1)} collective-permute-done((bf16[1,32,2048]{2,1,0:T(8,128)(2,1)S(1)}, bf16[1,32,2048]{2,1,0:T(8,128)(2,1)S(1)}, u32[]{:S(2)}, u32[]{:S(2)}) %collective-permute-start.19) | collective-permute-done | bytes 131104 | tf_op jit(solution)/shard_map/ppermute | solution.py:312
  119.2 2.4 %collective-permute-done.20.refs_7_ = bf16[1,32,2048]{2,1,0:T(8,128)(2,1)S(1)} collective-permute-done((bf16[1,32,2048]{2,1,0:T(8,128)(2,1)S(1)}, bf16[1,32,2048]{2,1,0:T(8,128)(2,1)S(1)}, u32[]{:S(2)}, u32[]{:S(2)}) %collective-permute-start.20) | collective-permute-done | bytes 131104 | tf_op jit(solution)/shard_map/ppermute | solution.py:312
  121.6 2.3 %finish.5 = bf16[4,64,32,256]{3,2,1,0:T(8,128)(2,1)} custom-call(s32[3]{0:T(128)S(1)} %pad_add_fusion.here_ref, bf16[1,32,2048]{2,1,0:T(8,128)(2,1)S(1)} %get-tuple-element.50.refs_0_, bf16[1,32,2048]{2,1,0:T(8,128)(2,1)S(1)} %collective-permute-done.14.refs_1_, ...), custom_call_target="tpu_custom_call", output_to_operand_aliasing={{}: (10, {})} | custom-call | flops 700000000 | bytes 2500000 | tf_op jit(solution)/shard_map/finish/pallas_call | solution.py:286
  (45 shorter events, 1.9 us)
Async XLA Ops:
  2.9 33.6 %copy-start = (s32[32,256]{1,0:T(8,128)S(1)}, s32[32,256]{1,0:T(8,128)}, u32[]{:S(2)}) copy-start(s32[32,256]{1,0:T(8,128)} %classes_ref.1) | copy-start | bytes 98308
  3.0 33.6 %copy-start.1 = (f32[8,64]{1,0:T(8,128)S(1)}, f32[8,64]{1,0:T(8,128)}, u32[]{:S(2)}) copy-start(f32[8,64]{1,0:T(8,128)} %table_ref.1) | copy-start | bytes 6148
  3.0 44.8 %copy-start.2 = (bf16[256,256]{1,0:T(8,128)(2,1)S(1)}, bf16[256,256]{1,0:T(8,128)(2,1)}, u32[]{:S(2)}) copy-start(bf16[256,256]{1,0:T(8,128)(2,1)} %lon_ref.1) | copy-start | bytes 393220
  3.0 44.8 %copy-start.3 = (bf16[256,256]{1,0:T(8,128)(2,1)S(1)}, bf16[256,256]{1,0:T(8,128)(2,1)}, u32[]{:S(2)}) copy-start(bf16[256,256]{1,0:T(8,128)(2,1)} %lat_ref.1) | copy-start | bytes 393220
  3.0 44.7 %copy-start.4 = (bf16[64,64]{1,0:T(8,128)(2,1)S(1)}, bf16[64,64]{1,0:T(8,128)(2,1)}, u32[]{:S(2)}) copy-start(bf16[64,64]{1,0:T(8,128)(2,1)} %vert_ref.1) | copy-start | bytes 24580
  3.0 2.9 %collective-permute-start = (bf16[4,8,32,256]{3,2,1,0:T(8,128)(2,1)S(1)}, bf16[4,8,32,256]{3,2,1,0:T(8,128)(2,1)S(1)}, u32[]{:S(2)}, u32[]{:S(2)}) collective-permute-start(bf16[4,8,32,256]{3,2,1,0:T(8,128)(2,1)S(1)} %get-tuple-element.41), channel_id=1, source_target_pairs={{0,8},{8,0},{1,9},{9,1},{2,10},{10,2},{3,11},{11,3},{4,12},{12,4},... | collective-permute-start | bytes 1572872 | tf_op jit(solution)/shard_map/ppermute | solution.py:326
  6.1 7.3 %collective-permute-start.1 = (bf16[8,32,256]{2,1,0:T(8,128)(2,1)S(1)}, bf16[8,32,256]{2,1,0:T(8,128)(2,1)S(1)}, u32[]{:S(2)}, u32[]{:S(2)}) collective-permute-start(bf16[8,32,256]{2,1,0:T(8,128)(2,1)S(1)} %get-tuple-element.43), channel_id=1, source_target_pairs={{0,16},{16,32},{32,48},{48,0},{1,17},{17,33},{33,49},{49,1},{2,18}... | collective-permute-start | bytes 393224 | tf_op jit(solution)/shard_map/ppermute | solution.py:312
  7.7 9.6 %collective-permute-start.2 = (bf16[8,32,256]{2,1,0:T(8,128)(2,1)S(1)}, bf16[8,32,256]{2,1,0:T(8,128)(2,1)S(1)}, u32[]{:S(2)}, u32[]{:S(2)}) collective-permute-start(bf16[8,32,256]{2,1,0:T(8,128)(2,1)S(1)} %get-tuple-element.44), channel_id=1, source_target_pairs={{0,32},{16,48},{32,0},{48,16},{1,33},{17,49},{33,1},{49,17},{2,34}... | collective-permute-start | bytes 393224 | tf_op jit(solution)/shard_map/ppermute | solution.py:312
  10.6 6.7 %collective-permute-start.3 = (bf16[8,32,256]{2,1,0:T(8,128)(2,1)S(1)}, bf16[8,32,256]{2,1,0:T(8,128)(2,1)S(1)}, u32[]{:S(2)}, u32[]{:S(2)}) collective-permute-start(bf16[8,32,256]{2,1,0:T(8,128)(2,1)S(1)} %get-tuple-element.45), channel_id=1, source_target_pairs={{0,48},{16,0},{32,16},{48,32},{1,49},{17,1},{33,17},{49,33},{2,50}... | collective-permute-start | bytes 393224 | tf_op jit(solution)/shard_map/ppermute | solution.py:312
  17.4 17.4 %collective-permute-start.6 = (bf16[8,32,256]{2,1,0:T(8,128)(2,1)S(1)}, bf16[8,32,256]{2,1,0:T(8,128)(2,1)S(1)}, u32[]{:S(2)}, u32[]{:S(2)}) collective-permute-start(bf16[8,32,256]{2,1,0:T(8,128)(2,1)S(1)} %join.1.refs_0_), channel_id=1, source_target_pairs={{0,192},{64,0},{128,64},{192,128},{1,193},{65,1},{129,65},{193,129... | collective-permute-start | bytes 393224 | tf_op jit(solution)/shard_map/ppermute | solution.py:312
  23.8 12.8 %collective-permute-start.5 = (bf16[8,32,256]{2,1,0:T(8,128)(2,1)S(1)}, bf16[8,32,256]{2,1,0:T(8,128)(2,1)S(1)}, u32[]{:S(2)}, u32[]{:S(2)}) collective-permute-start(bf16[8,32,256]{2,1,0:T(8,128)(2,1)S(1)} %join.1.refs_0_), channel_id=1, source_target_pairs={{0,128},{64,192},{128,0},{192,64},{1,129},{65,193},{129,1},{193,65... | collective-permute-start | bytes 393224 | tf_op jit(solution)/shard_map/ppermute | solution.py:312
  24.8 11.8 %collective-permute-start.4 = (bf16[8,32,256]{2,1,0:T(8,128)(2,1)S(1)}, bf16[8,32,256]{2,1,0:T(8,128)(2,1)S(1)}, u32[]{:S(2)}, u32[]{:S(2)}) collective-permute-start(bf16[8,32,256]{2,1,0:T(8,128)(2,1)S(1)} %join.1.refs_0_), channel_id=1, source_target_pairs={{0,64},{64,128},{128,192},{192,0},{1,65},{65,129},{129,193},{193,1... | collective-permute-start | bytes 393224 | tf_op jit(solution)/shard_map/ppermute | solution.py:312
  37.4 6.4 %collective-permute-start.9 = (bf16[8,32,256]{2,1,0:T(8,128)(2,1)S(1)}, bf16[8,32,256]{2,1,0:T(8,128)(2,1)S(1)}, u32[]{:S(2)}, u32[]{:S(2)}) collective-permute-start(bf16[8,32,256]{2,1,0:T(8,128)(2,1)S(1)} %weigh.1.refs_0_), channel_id=1, source_target_pairs={{0,48},{16,0},{32,16},{48,32},{1,49},{17,1},{33,17},{49,33},{2,50}... | collective-permute-start | bytes 393224 | tf_op jit(solution)/shard_map/ppermute | solution.py:312
  39.8 6.6 %collective-permute-start.8 = (bf16[8,32,256]{2,1,0:T(8,128)(2,1)S(1)}, bf16[8,32,256]{2,1,0:T(8,128)(2,1)S(1)}, u32[]{:S(2)}, u32[]{:S(2)}) collective-permute-start(bf16[8,32,256]{2,1,0:T(8,128)(2,1)S(1)} %weigh.1.refs_0_), channel_id=1, source_target_pairs={{0,32},{16,48},{32,0},{48,16},{1,33},{17,49},{33,1},{49,17},{2,34}... | collective-permute-start | bytes 393224 | tf_op jit(solution)/shard_map/ppermute | solution.py:312
  40.2 7.6 %collective-permute-start.7 = (bf16[8,32,256]{2,1,0:T(8,128)(2,1)S(1)}, bf16[8,32,256]{2,1,0:T(8,128)(2,1)S(1)}, u32[]{:S(2)}, u32[]{:S(2)}) collective-permute-start(bf16[8,32,256]{2,1,0:T(8,128)(2,1)S(1)} %weigh.1.refs_0_), channel_id=1, source_target_pairs={{0,16},{16,32},{32,48},{48,0},{1,17},{17,33},{33,49},{49,1},{2,18}... | collective-permute-start | bytes 393224 | tf_op jit(solution)/shard_map/ppermute | solution.py:312
  40.9 8.0 %collective-permute-start.10 = (bf16[8,32,256]{2,1,0:T(8,128)(2,1)S(1)}, bf16[8,32,256]{2,1,0:T(8,128)(2,1)S(1)}, u32[]{:S(2)}, u32[]{:S(2)}) collective-permute-start(bf16[8,32,256]{2,1,0:T(8,128)(2,1)S(1)} %weigh.1.refs_0_), channel_id=1, source_target_pairs={{0,8},{8,0},{1,9},{9,1},{2,10},{10,2},{3,11},{11,3},{4,12},{12,4},... | collective-permute-start | bytes 393224 | tf_op jit(solution)/shard_map/ppermute | solution.py:332
  43.8 5.2 %collective-permute-start.13 = (bf16[8,32,256]{2,1,0:T(8,128)(2,1)S(1)}, bf16[8,32,256]{2,1,0:T(8,128)(2,1)S(1)}, u32[]{:S(2)}, u32[]{:S(2)}) collective-permute-start(bf16[8,32,256]{2,1,0:T(8,128)(2,1)S(1)} %collective-permute-done.9.refs_3_), channel_id=1, source_target_pairs={{0,8},{8,0},{1,9},{9,1},{2,10},{10,2},{3,11},{11,3},{4,12},{12,4},... | collective-permute-start | bytes 393224 | tf_op jit(solution)/shard_map/ppermute | solution.py:332
  46.4 2.5 %collective-permute-start.12 = (bf16[8,32,256]{2,1,0:T(8,128)(2,1)S(1)}, bf16[8,32,256]{2,1,0:T(8,128)(2,1)S(1)}, u32[]{:S(2)}, u32[]{:S(2)}) collective-permute-start(bf16[8,32,256]{2,1,0:T(8,128)(2,1)S(1)} %collective-permute-done.8.refs_2_), channel_id=1, source_target_pairs={{0,8},{8,0},{1,9},{9,1},{2,10},{10,2},{3,11},{11,3},{4,12},{12,4},... | collective-permute-start | bytes 393224 | tf_op jit(solution)/shard_map/ppermute | solution.py:332
  47.7 1.3 %collective-permute-start.11 = (bf16[8,32,256]{2,1,0:T(8,128)(2,1)S(1)}, bf16[8,32,256]{2,1,0:T(8,128)(2,1)S(1)}, u32[]{:S(2)}, u32[]{:S(2)}) collective-permute-start(bf16[8,32,256]{2,1,0:T(8,128)(2,1)S(1)} %collective-permute-done.7.refs_1_), channel_id=1, source_target_pairs={{0,8},{8,0},{1,9},{9,1},{2,10},{10,2},{3,11},{11,3},{4,12},{12,4},... | collective-permute-start | bytes 393224 | tf_op jit(solution)/shard_map/ppermute | solution.py:332
  50.2 10.6 %collective-permute-start.28 = (bf16[1,32,2048]{2,1,0:T(8,128)(2,1)S(1)}, bf16[1,32,2048]{2,1,0:T(8,128)(2,1)S(1)}, u32[]{:S(2)}, u32[]{:S(2)}) collective-permute-start(bf16[1,32,2048]{2,1,0:T(8,128)(2,1)S(1)} %get-tuple-element.68), channel_id=1, source_target_pairs={{0,1},{1,2},{2,3},{3,4},{4,5},{5,6},{6,7},{7,0},{8,9},{9,10},{10,1... | collective-permute-start | bytes 393224 | tf_op jit(solution)/shard_map/ppermute | solution.py:312
  53.0 9.9 %collective-permute-start.29 = (bf16[1,32,2048]{2,1,0:T(8,128)(2,1)S(1)}, bf16[1,32,2048]{2,1,0:T(8,128)(2,1)S(1)}, u32[]{:S(2)}, u32[]{:S(2)}) collective-permute-start(bf16[1,32,2048]{2,1,0:T(8,128)(2,1)S(1)} %get-tuple-element.69), channel_id=1, source_target_pairs={{0,2},{1,3},{2,4},{3,5},{4,6},{5,7},{6,0},{7,1},{8,10},{9,11},{10,... | collective-permute-start | bytes 393224 | tf_op jit(solution)/shard_map/ppermute | solution.py:312
  55.4 9.4 %collective-permute-start.30 = (bf16[1,32,2048]{2,1,0:T(8,128)(2,1)S(1)}, bf16[1,32,2048]{2,1,0:T(8,128)(2,1)S(1)}, u32[]{:S(2)}, u32[]{:S(2)}) collective-permute-start(bf16[1,32,2048]{2,1,0:T(8,128)(2,1)S(1)} %get-tuple-element.70), channel_id=1, source_target_pairs={{0,3},{1,4},{2,5},{3,6},{4,7},{5,0},{6,1},{7,2},{8,11},{9,12},{10,... | collective-permute-start | bytes 393224 | tf_op jit(solution)/shard_map/ppermute | solution.py:312
  55.4 12.2 %collective-permute-start.31 = (bf16[1,32,2048]{2,1,0:T(8,128)(2,1)S(1)}, bf16[1,32,2048]{2,1,0:T(8,128)(2,1)S(1)}, u32[]{:S(2)}, u32[]{:S(2)}) collective-permute-start(bf16[1,32,2048]{2,1,0:T(8,128)(2,1)S(1)} %get-tuple-element.71), channel_id=1, source_target_pairs={{0,4},{1,5},{2,6},{3,7},{4,0},{5,1},{6,2},{7,3},{8,12},{9,13},{10,... | collective-permute-start | bytes 393224 | tf_op jit(solution)/shard_map/ppermute | solution.py:312
  56.8 12.0 %collective-permute-start.32 = (bf16[1,32,2048]{2,1,0:T(8,128)(2,1)S(1)}, bf16[1,32,2048]{2,1,0:T(8,128)(2,1)S(1)}, u32[]{:S(2)}, u32[]{:S(2)}) collective-permute-start(bf16[1,32,2048]{2,1,0:T(8,128)(2,1)S(1)} %get-tuple-element.72), channel_id=1, source_target_pairs={{0,5},{1,6},{2,7},{3,0},{4,1},{5,2},{6,3},{7,4},{8,13},{9,14},{10,... | collective-permute-start | bytes 393224 | tf_op jit(solution)/shard_map/ppermute | solution.py:312
  60.8 10.9 %collective-permute-start.33 = (bf16[1,32,2048]{2,1,0:T(8,128)(2,1)S(1)}, bf16[1,32,2048]{2,1,0:T(8,128)(2,1)S(1)}, u32[]{:S(2)}, u32[]{:S(2)}) collective-permute-start(bf16[1,32,2048]{2,1,0:T(8,128)(2,1)S(1)} %get-tuple-element.73), channel_id=1, source_target_pairs={{0,6},{1,7},{2,0},{3,1},{4,2},{5,3},{6,4},{7,5},{8,14},{9,15},{10,... | collective-permute-start | bytes 393224 | tf_op jit(solution)/shard_map/ppermute | solution.py:312
  63.0 29.5 %collective-permute-start.21 = (bf16[2,32,2048]{2,1,0:T(8,128)(2,1)S(1)}, bf16[2,32,2048]{2,1,0:T(8,128)(2,1)S(1)}, u32[]{:S(2)}, u32[]{:S(2)}) collective-permute-start(bf16[2,32,2048]{2,1,0:T(8,128)(2,1)S(1)} %get-tuple-element.60), channel_id=1, source_target_pairs={{0,1},{1,2},{2,3},{3,4},{4,5},{5,6},{6,7},{7,0},{8,9},{9,10},{10,1... | collective-permute-start | bytes 786440 | tf_op jit(solution)/shard_map/ppermute | solution.py:312
  64.7 28.4 %collective-permute-start.22 = (bf16[2,32,2048]{2,1,0:T(8,128)(2,1)S(1)}, bf16[2,32,2048]{2,1,0:T(8,128)(2,1)S(1)}, u32[]{:S(2)}, u32[]{:S(2)}) collective-permute-start(bf16[2,32,2048]{2,1,0:T(8,128)(2,1)S(1)} %get-tuple-element.61), channel_id=1, source_target_pairs={{0,2},{1,3},{2,4},{3,5},{4,6},{5,7},{6,0},{7,1},{8,10},{9,11},{10,... | collective-permute-start | bytes 786440 | tf_op jit(solution)/shard_map/ppermute | solution.py:312
  67.5 9.4 %collective-permute-start.34 = (bf16[1,32,2048]{2,1,0:T(8,128)(2,1)S(1)}, bf16[1,32,2048]{2,1,0:T(8,128)(2,1)S(1)}, u32[]{:S(2)}, u32[]{:S(2)}) collective-permute-start(bf16[1,32,2048]{2,1,0:T(8,128)(2,1)S(1)} %get-tuple-element.74), channel_id=1, source_target_pairs={{0,7},{1,0},{2,1},{3,2},{4,3},{5,4},{6,5},{7,6},{8,15},{9,8},{10,9... | collective-permute-start | bytes 393224 | tf_op jit(solution)/shard_map/ppermute | solution.py:312
  68.7 21.2 %collective-permute-start.14 = (bf16[1,32,2048]{2,1,0:T(8,128)(2,1)S(1)}, bf16[1,32,2048]{2,1,0:T(8,128)(2,1)S(1)}, u32[]{:S(2)}, u32[]{:S(2)}) collective-permute-start(bf16[1,32,2048]{2,1,0:T(8,128)(2,1)S(1)} %get-tuple-element.51), channel_id=1, source_target_pairs={{0,1},{1,2},{2,3},{3,4},{4,5},{5,6},{6,7},{7,0},{8,9},{9,10},{10,1... | collective-permute-start | bytes 393224 | tf_op jit(solution)/shard_map/ppermute | solution.py:312
  71.8 18.2 %collective-permute-start.15 = (bf16[1,32,2048]{2,1,0:T(8,128)(2,1)S(1)}, bf16[1,32,2048]{2,1,0:T(8,128)(2,1)S(1)}, u32[]{:S(2)}, u32[]{:S(2)}) collective-permute-start(bf16[1,32,2048]{2,1,0:T(8,128)(2,1)S(1)} %get-tuple-element.52), channel_id=1, source_target_pairs={{0,2},{1,3},{2,4},{3,5},{4,6},{5,7},{6,0},{7,1},{8,10},{9,11},{10,... | collective-permute-start | bytes 393224 | tf_op jit(solution)/shard_map/ppermute | solution.py:312
  76.9 19.2 %collective-permute-start.23 = (bf16[2,32,2048]{2,1,0:T(8,128)(2,1)S(1)}, bf16[2,32,2048]{2,1,0:T(8,128)(2,1)S(1)}, u32[]{:S(2)}, u32[]{:S(2)}) collective-permute-start(bf16[2,32,2048]{2,1,0:T(8,128)(2,1)S(1)} %get-tuple-element.62), channel_id=1, source_target_pairs={{0,3},{1,4},{2,5},{3,6},{4,7},{5,0},{6,1},{7,2},{8,11},{9,12},{10,... | collective-permute-start | bytes 786440 | tf_op jit(solution)/shard_map/ppermute | solution.py:312
  90.0 9.2 %collective-permute-start.24 = (bf16[2,32,2048]{2,1,0:T(8,128)(2,1)S(1)}, bf16[2,32,2048]{2,1,0:T(8,128)(2,1)S(1)}, u32[]{:S(2)}, u32[]{:S(2)}) collective-permute-start(bf16[2,32,2048]{2,1,0:T(8,128)(2,1)S(1)} %get-tuple-element.63), channel_id=1, source_target_pairs={{0,4},{1,5},{2,6},{3,7},{4,0},{5,1},{6,2},{7,3},{8,12},{9,13},{10,... | collective-permute-start | bytes 786440 | tf_op jit(solution)/shard_map/ppermute | solution.py:312
  90.0 16.7 %collective-permute-start.25 = (bf16[2,32,2048]{2,1,0:T(8,128)(2,1)S(1)}, bf16[2,32,2048]{2,1,0:T(8,128)(2,1)S(1)}, u32[]{:S(2)}, u32[]{:S(2)}) collective-permute-start(bf16[2,32,2048]{2,1,0:T(8,128)(2,1)S(1)} %get-tuple-element.64), channel_id=1, source_target_pairs={{0,5},{1,6},{2,7},{3,0},{4,1},{5,2},{6,3},{7,4},{8,13},{9,14},{10,... | collective-permute-start | bytes 786440 | tf_op jit(solution)/shard_map/ppermute | solution.py:312
  92.4 18.5 %collective-permute-start.26 = (bf16[2,32,2048]{2,1,0:T(8,128)(2,1)S(1)}, bf16[2,32,2048]{2,1,0:T(8,128)(2,1)S(1)}, u32[]{:S(2)}, u32[]{:S(2)}) collective-permute-start(bf16[2,32,2048]{2,1,0:T(8,128)(2,1)S(1)} %get-tuple-element.65), channel_id=1, source_target_pairs={{0,6},{1,7},{2,0},{3,1},{4,2},{5,3},{6,4},{7,5},{8,14},{9,15},{10,... | collective-permute-start | bytes 786440 | tf_op jit(solution)/shard_map/ppermute | solution.py:312
  93.1 20.2 %collective-permute-start.27 = (bf16[2,32,2048]{2,1,0:T(8,128)(2,1)S(1)}, bf16[2,32,2048]{2,1,0:T(8,128)(2,1)S(1)}, u32[]{:S(2)}, u32[]{:S(2)}) collective-permute-start(bf16[2,32,2048]{2,1,0:T(8,128)(2,1)S(1)} %get-tuple-element.66), channel_id=1, source_target_pairs={{0,7},{1,0},{2,1},{3,2},{4,3},{5,4},{6,5},{7,6},{8,15},{9,8},{10,9... | collective-permute-start | bytes 786440 | tf_op jit(solution)/shard_map/ppermute | solution.py:312
  96.1 20.8 %collective-permute-start.16 = (bf16[1,32,2048]{2,1,0:T(8,128)(2,1)S(1)}, bf16[1,32,2048]{2,1,0:T(8,128)(2,1)S(1)}, u32[]{:S(2)}, u32[]{:S(2)}) collective-permute-start(bf16[1,32,2048]{2,1,0:T(8,128)(2,1)S(1)} %get-tuple-element.53), channel_id=1, source_target_pairs={{0,3},{1,4},{2,5},{3,6},{4,7},{5,0},{6,1},{7,2},{8,11},{9,12},{10,... | collective-permute-start | bytes 393224 | tf_op jit(solution)/shard_map/ppermute | solution.py:312
  99.2 17.7 %collective-permute-start.17 = (bf16[1,32,2048]{2,1,0:T(8,128)(2,1)S(1)}, bf16[1,32,2048]{2,1,0:T(8,128)(2,1)S(1)}, u32[]{:S(2)}, u32[]{:S(2)}) collective-permute-start(bf16[1,32,2048]{2,1,0:T(8,128)(2,1)S(1)} %get-tuple-element.54), channel_id=1, source_target_pairs={{0,4},{1,5},{2,6},{3,7},{4,0},{5,1},{6,2},{7,3},{8,12},{9,13},{10,... | collective-permute-start | bytes 393224 | tf_op jit(solution)/shard_map/ppermute | solution.py:312
  106.7 10.2 %collective-permute-start.18 = (bf16[1,32,2048]{2,1,0:T(8,128)(2,1)S(1)}, bf16[1,32,2048]{2,1,0:T(8,128)(2,1)S(1)}, u32[]{:S(2)}, u32[]{:S(2)}) collective-permute-start(bf16[1,32,2048]{2,1,0:T(8,128)(2,1)S(1)} %get-tuple-element.55), channel_id=1, source_target_pairs={{0,5},{1,6},{2,7},{3,0},{4,1},{5,2},{6,3},{7,4},{8,13},{9,14},{10,... | collective-permute-start | bytes 393224 | tf_op jit(solution)/shard_map/ppermute | solution.py:312
  111.0 8.2 %collective-permute-start.19 = (bf16[1,32,2048]{2,1,0:T(8,128)(2,1)S(1)}, bf16[1,32,2048]{2,1,0:T(8,128)(2,1)S(1)}, u32[]{:S(2)}, u32[]{:S(2)}) collective-permute-start(bf16[1,32,2048]{2,1,0:T(8,128)(2,1)S(1)} %get-tuple-element.56), channel_id=1, source_target_pairs={{0,6},{1,7},{2,0},{3,1},{4,2},{5,3},{6,4},{7,5},{8,14},{9,15},{10,... | collective-permute-start | bytes 393224 | tf_op jit(solution)/shard_map/ppermute | solution.py:312
  113.3 8.3 %collective-permute-start.20 = (bf16[1,32,2048]{2,1,0:T(8,128)(2,1)S(1)}, bf16[1,32,2048]{2,1,0:T(8,128)(2,1)S(1)}, u32[]{:S(2)}, u32[]{:S(2)}) collective-permute-start(bf16[1,32,2048]{2,1,0:T(8,128)(2,1)S(1)} %get-tuple-element.57), channel_id=1, source_target_pairs={{0,7},{1,0},{2,1},{3,2},{4,3},{5,4},{6,5},{7,6},{8,15},{9,8},{10,9... | collective-permute-start | bytes 393224 | tf_op jit(solution)/shard_map/ppermute | solution.py:312

commit v2 on v1

--- a/solution.py
+++ b/solution.py
@@ -15,6 +15,7 @@
 LATS = 8
 LAT = "lat"
 EACH = 4
+Z_ORDER = (2, 1, 3)
 GROUPS = ((0, 1), (1, 2), (3, 1))
 ORDER = (6, 4, 2, 5, 7, 1, 3)
 
@@ -249,60 +250,74 @@
     )(*args)
 
 
-def finish_kernel(here_ref, *refs):
-    parts = refs[:LATS]
-    turned_ref, out_ref = refs[LATS], refs[-1]
-    k, h = pl.program_id(0), pl.program_id(1)
-    share = parts[0].shape[1]
-    groups = out_ref.shape[1] // EACH
+def finish_kernel(first, here_ref, *refs):
+    parts, turned_ref = refs[:LATS], refs[LATS]
+    out_ref, done, sems = refs[-3:]
+    count, share, _ = parts[0].shape
+    levels = done.shape[1]
+    groups = levels // EACH // 2
     lane = lax.broadcasted_iota(jnp.int32, (share, 128), 1) >> 5
     at = [lane == q for q in range(3)]
-    for turn in range(EACH):
-        lines = []
-        for g in range(groups):
-            lanes = pl.ds(pl.multiple_of((h * groups + g) * 128, 128), 128)
-            sides = []
-            for part in range(2):
-                tiles = [parts[EACH * part + (turn - q) % EACH][k, :, lanes] for q in range(EACH)]
-                side = tiles[3]
-                for q in range(3):
-                    side = jnp.where(at[q], tiles[q], side)
-                sides.append(side)
-            lines.append(jnp.concatenate(sides, axis=1))
-        x = jnp.concatenate(lines, axis=0)
-        y = nt_dot(x, turned_ref[turn]).astype(BF16)
-        level = (turn + 8 - here_ref[2]) & 3
-        for g in range(groups):
-            out_ref[0, EACH * g + level] = y[share * g : share * g + share]
+    copies = []
+    for k in range(count):
+        for h in range(2):
+            for turn in range(EACH):
+                lines = []
+                for g in range(h * groups, h * groups + groups):
+                    sides = []
+                    for part in range(2):
+                        tiles = [
+                            parts[EACH * part + (turn - q) % EACH][k, :, 128 * g : 128 * g + 128]
+                            for q in range(EACH)
+                        ]
+                        side = tiles[3]
+                        for q in range(3):
+                            side = jnp.where(at[q], tiles[q], side)
+                        sides.append(side)
+                    lines.append(jnp.concatenate(sides, axis=1))
+                x = jnp.concatenate(lines, axis=0)
+                y = nt_dot(x, turned_ref[turn]).astype(BF16)
+                level = (turn + 8 - here_ref[2]) & 3
+                for g in range(groups):
+                    done[k, EACH * (h * groups + g) + level] = y[share * g : share * g + share]
+            half = pl.ds(h * (levels // 2), levels // 2)
+            copy = pltpu.make_async_copy(
+                done.at[k, half], out_ref.at[first + k, half], sems.at[k, h]
+            )
+            copy.start()
+            copies.append(copy)
+    for copy in copies:
+        copy.wait()
 
 
 def finish(here, parts, turned, first, members, so_far=None):
     count, share, wide = parts[0].shape
     size = turned.shape[1]
     levels = wide // 32
-    args = (*parts, turned) if so_far is None else (*parts, turned, so_far)
-    extra = [] if so_far is None else [pl.BlockSpec(memory_space=pl.ANY)]
-    vmem = pl.BlockSpec(memory_space=pltpu.VMEM)
-    return pl.pallas_call(
-        finish_kernel,
-        grid_spec=pltpu.PrefetchScalarGridSpec(
-            num_scalar_prefetch=1,
-            grid=(count, 2),
-            in_specs=[vmem] * (LATS + 1) + extra,
-            out_specs=pl.BlockSpec(
-                (1, levels // 2, share, size), lambda k, h, s: (first + k, h, 0, 0)
-            ),
-        ),
+    args = (here, *parts, turned)
+    smem, vmem = (pl.BlockSpec(memory_space=space) for space in (pltpu.SMEM, pltpu.VMEM))
+    hbm = pl.BlockSpec(memory_space=pltpu.HBM)
+    in_specs = [smem] + [vmem] * (LATS + 1)
+    aliases = {}
+    if so_far is not None:
+        aliases = {len(args): 0}
+        args, in_specs = (*args, so_far), in_specs + [hbm]
+    return pl.pallas_call(
+        functools.partial(finish_kernel, first),
+        in_specs=in_specs,
+        out_specs=hbm,
         out_shape=jax.ShapeDtypeStruct((members, levels, share, size), BF16),
-        input_output_aliases={} if so_far is None else {len(args): 0},
-        compiler_params=pltpu.CompilerParams(
-            dimension_semantics=("arbitrary", "arbitrary"), vmem_limit_bytes=16 * 1024 * 1024
-        ),
+        input_output_aliases=aliases,
+        scratch_shapes=[
+            pltpu.VMEM((count, levels, share, size), BF16),
+            pltpu.SemaphoreType.DMA((count, 2)),
+        ],
+        compiler_params=pltpu.CompilerParams(vmem_limit_bytes=16 * 1024 * 1024),
         cost_estimate=pl.CostEstimate(
             flops=count * 700_000_000, bytes_accessed=count * 2_500_000, transcendentals=0
         ),
         name="finish",
-    )(here, *args)
+    )(*args)
 
 
 def passed_on(axis, pieces, order):
@@ -326,7 +341,7 @@
     arrived = lax.ppermute(send, "core", swap)
     pieces = chip_sum(keep, arrived)
     along_y = join(passed_on("y", pieces, range(1, Y)))
-    along_z = passed_on("zh", [along_y] * ZH, range(1, ZH))
+    along_z = passed_on("zh", [along_y] * ZH, Z_ORDER)
     weighted = weigh(here, classes, prec_table, along_z)
     own = passed_on("y", [weighted] * Y, range(1, Y))
     weights = own + [lax.ppermute(x, "core", swap) for x in own]

time: 124 us -> 124 us (level)
  Pallas kernels: 20.3 us -> 18.4 us
  waiting for transfers between devices: 48.4 us -> 49.8 us
    pallas_call x3, Pallas kernels: 8.12 us -> 6.18 us  [finish(): pl.pallas_call(functools.partial(finish_kernel, first), in_specs=in_specs...]
    ppermute x30, waiting for transfers between devices: 48.3 us -> 49.7 us  [passed_on(): lax.ppermute(pieces[d], axis, [(i, (i + d) % count) for i in range(count)])]
  transfers between devices with their start and end apart: 35 -> 35, of which waited for: 17 -> 18; matrix products, arithmetic and copies ran while one was open for 0% -> 0% of each run, Pallas kernels for 11% -> 9%
where the time goes in v2:
time: 124 us
  starting transfers between devices  54.9 us (44%)
  waiting for transfers between devices  49.8 us (40%)
  Pallas kernels  18.4 us (15%)
    ppermute x30, starting transfers between devices, passed_on(): lax.ppermute(pieces[d], axis, [(i, (i + d) % count) for i in range(count)])  54.8 us
    ppermute x30, waiting for transfers between devices, passed_on(): lax.ppermute(pieces[d], axis, [(i, (i + d) % count) for i in range(count)])  49.7 us
    pallas_call x3, Pallas kernels, finish(): pl.pallas_call(functools.partial(finish_kernel, first), in_specs=in_specs...  6.18 us
    pallas_call x2, Pallas kernels, half_sum(): pl.pallas_call(functools.partial(half_sum_kernel, other), in_specs=[smem,...  5.69 us
    pallas_call x3, Pallas kernels, spread_out(): pl.pallas_call(functools.partial(spread_out_kernel, first), in_specs=[vme...  4.38 us
  transfers between devices with their start and end apart: 35, of which 18 were waited for; matrix products, arithmetic and copies ran while one was open for 0% of the time, Pallas kernels for 9%

profile of v2, /device:TPU:6, one launch (start us, length us, event | category | flops | bytes accessed | tf_op | source)
XLA Modules:
  0.0 123.7 jit_solution(13250745185792896105)
XLA Ops:
  0.1 2.9 %shard_map.74 = (bf16[4,8,32,256]{3,2,1,0:T(8,128)(2,1)S(1)}, bf16[4,4,8,32,256]{4,3,2,1,0:T(8,128)(2,1)S(1)}) custom-call(s32[3]{0:T(128)S(1)} %pad_add_fusion.here_ref, bf16[4,64,32,256]{3,2,1,0:T(8,128)(2,1)} %spread_ref.3, bf16[4,64,32,256]{3,2,1,0:T(8,128)(2,1)} %controls_ref.3), custom_call_target="tpu_custom_call" | custom-call | flops 300000000 | bytes 4200000 | tf_op jit(solution)/shard_map/pallas_call | solution.py:59
  3.1 2.8 %shard_map.73 = (f32[4,8,32,256]{3,2,1,0:T(8,128)S(1)}, bf16[4,4,8,32,256]{4,3,2,1,0:T(8,128)(2,1)S(1)}) custom-call(s32[3]{0:T(128)S(1)} %pad_add_fusion.here_ref, bf16[4,64,32,256]{3,2,1,0:T(8,128)(2,1)} %spread_ref.3, bf16[4,64,32,256]{3,2,1,0:T(8,128)(2,1)} %controls_ref.3), custom_call_target="tpu_custom_call" | custom-call | flops 300000000 | bytes 4200000 | tf_op jit(solution)/shard_map/pallas_call | solution.py:59
  6.1 1.7 %collective-permute-start.1 = (bf16[8,32,256]{2,1,0:T(8,128)(2,1)S(1)}, bf16[8,32,256]{2,1,0:T(8,128)(2,1)S(1)}, u32[]{:S(2)}, u32[]{:S(2)}) collective-permute-start(bf16[8,32,256]{2,1,0:T(8,128)(2,1)S(1)} %get-tuple-element.43), channel_id=1, source_target_pairs={{0,16},{16,32},{32,48},{48,0},{1,17},{17,33},{33,49},{49,1},{2,18}... | collective-permute-start | bytes 393224 | tf_op jit(solution)/shard_map/ppermute | solution.py:327
  7.7 2.9 %collective-permute-start.2 = (bf16[8,32,256]{2,1,0:T(8,128)(2,1)S(1)}, bf16[8,32,256]{2,1,0:T(8,128)(2,1)S(1)}, u32[]{:S(2)}, u32[]{:S(2)}) collective-permute-start(bf16[8,32,256]{2,1,0:T(8,128)(2,1)S(1)} %get-tuple-element.44), channel_id=1, source_target_pairs={{0,32},{16,48},{32,0},{48,16},{1,33},{17,49},{33,1},{49,17},{2,34}... | collective-permute-start | bytes 393224 | tf_op jit(solution)/shard_map/ppermute | solution.py:327
  10.6 1.3 %collective-permute-start.3 = (bf16[8,32,256]{2,1,0:T(8,128)(2,1)S(1)}, bf16[8,32,256]{2,1,0:T(8,128)(2,1)S(1)}, u32[]{:S(2)}, u32[]{:S(2)}) collective-permute-start(bf16[8,32,256]{2,1,0:T(8,128)(2,1)S(1)} %get-tuple-element.45), channel_id=1, source_target_pairs={{0,48},{16,0},{32,16},{48,32},{1,49},{17,1},{33,17},{49,33},{2,50}... | collective-permute-start | bytes 393224 | tf_op jit(solution)/shard_map/ppermute | solution.py:327
  12.0 1.4 %collective-permute-done.1.refs_1_ = bf16[8,32,256]{2,1,0:T(8,128)(2,1)S(1)} collective-permute-done((bf16[8,32,256]{2,1,0:T(8,128)(2,1)S(1)}, bf16[8,32,256]{2,1,0:T(8,128)(2,1)S(1)}, u32[]{:S(2)}, u32[]{:S(2)}) %collective-permute-start.1) | collective-permute-done | bytes 131104 | tf_op jit(solution)/shard_map/ppermute | solution.py:327
  13.3 4.0 %collective-permute-done.2.refs_2_ = bf16[8,32,256]{2,1,0:T(8,128)(2,1)S(1)} collective-permute-done((bf16[8,32,256]{2,1,0:T(8,128)(2,1)S(1)}, bf16[8,32,256]{2,1,0:T(8,128)(2,1)S(1)}, u32[]{:S(2)}, u32[]{:S(2)}) %collective-permute-start.2) | collective-permute-done | bytes 131104 | tf_op jit(solution)/shard_map/ppermute | solution.py:327
  17.4 6.4 %collective-permute-start.6 = (bf16[8,32,256]{2,1,0:T(8,128)(2,1)S(1)}, bf16[8,32,256]{2,1,0:T(8,128)(2,1)S(1)}, u32[]{:S(2)}, u32[]{:S(2)}) collective-permute-start(bf16[8,32,256]{2,1,0:T(8,128)(2,1)S(1)} %join.1.refs_0_), channel_id=1, source_target_pairs={{0,192},{64,0},{128,64},{192,128},{1,193},{65,1},{129,65},{193,129... | collective-permute-start | bytes 393224 | tf_op jit(solution)/shard_map/ppermute | solution.py:327
  23.8 1.0 collective-permute-start.5
  24.8 2.8 %collective-permute-start.4 = (bf16[8,32,256]{2,1,0:T(8,128)(2,1)S(1)}, bf16[8,32,256]{2,1,0:T(8,128)(2,1)S(1)}, u32[]{:S(2)}, u32[]{:S(2)}) collective-permute-start(bf16[8,32,256]{2,1,0:T(8,128)(2,1)S(1)} %join.1.refs_0_), channel_id=1, source_target_pairs={{0,64},{64,128},{128,192},{192,0},{1,65},{65,129},{129,193},{193,1... | collective-permute-start | bytes 393224 | tf_op jit(solution)/shard_map/ppermute | solution.py:327
  27.6 7.2 %collective-permute-done.6.refs_3_ = bf16[8,32,256]{2,1,0:T(8,128)(2,1)S(1)} collective-permute-done((bf16[8,32,256]{2,1,0:T(8,128)(2,1)S(1)}, bf16[8,32,256]{2,1,0:T(8,128)(2,1)S(1)}, u32[]{:S(2)}, u32[]{:S(2)}) %collective-permute-start.6) | collective-permute-done | bytes 131104 | tf_op jit(solution)/shard_map/ppermute | solution.py:327
  34.8 1.8 %collective-permute-done.5.refs_2_ = bf16[8,32,256]{2,1,0:T(8,128)(2,1)S(1)} collective-permute-done((bf16[8,32,256]{2,1,0:T(8,128)(2,1)S(1)}, bf16[8,32,256]{2,1,0:T(8,128)(2,1)S(1)}, u32[]{:S(2)}, u32[]{:S(2)}) %collective-permute-start.5) | collective-permute-done | bytes 131104 | tf_op jit(solution)/shard_map/ppermute | solution.py:327
  36.6 0.8 weigh.1.refs_0_
  37.4 2.5 %collective-permute-start.9 = (bf16[8,32,256]{2,1,0:T(8,128)(2,1)S(1)}, bf16[8,32,256]{2,1,0:T(8,128)(2,1)S(1)}, u32[]{:S(2)}, u32[]{:S(2)}) collective-permute-start(bf16[8,32,256]{2,1,0:T(8,128)(2,1)S(1)} %weigh.1.refs_0_), channel_id=1, source_target_pairs={{0,48},{16,0},{32,16},{48,32},{1,49},{17,1},{33,17},{49,33},{2,50}... | collective-permute-start | bytes 393224 | tf_op jit(solution)/shard_map/ppermute | solution.py:327
  40.2 0.8 collective-permute-start.7
  40.9 2.8 %collective-permute-done.9.refs_3_ = bf16[8,32,256]{2,1,0:T(8,128)(2,1)S(1)} collective-permute-done((bf16[8,32,256]{2,1,0:T(8,128)(2,1)S(1)}, bf16[8,32,256]{2,1,0:T(8,128)(2,1)S(1)}, u32[]{:S(2)}, u32[]{:S(2)}) %collective-permute-start.9) | collective-permute-done | bytes 131104 | tf_op jit(solution)/shard_map/ppermute | solution.py:327
  43.8 2.6 %collective-permute-done.8.refs_2_ = bf16[8,32,256]{2,1,0:T(8,128)(2,1)S(1)} collective-permute-done((bf16[8,32,256]{2,1,0:T(8,128)(2,1)S(1)}, bf16[8,32,256]{2,1,0:T(8,128)(2,1)S(1)}, u32[]{:S(2)}, u32[]{:S(2)}) %collective-permute-start.8) | collective-permute-done | bytes 131104 | tf_op jit(solution)/shard_map/ppermute | solution.py:327
  46.4 1.3 %collective-permute-done.7.refs_1_ = bf16[8,32,256]{2,1,0:T(8,128)(2,1)S(1)} collective-permute-done((bf16[8,32,256]{2,1,0:T(8,128)(2,1)S(1)}, bf16[8,32,256]{2,1,0:T(8,128)(2,1)S(1)}, u32[]{:S(2)}, u32[]{:S(2)}) %collective-permute-start.7) | collective-permute-done | bytes 131104 | tf_op jit(solution)/shard_map/ppermute | solution.py:327
  47.7 1.2 tables.1
  49.1 1.1 spread_out.5
  50.2 2.8 %collective-permute-start.28 = (bf16[1,32,2048]{2,1,0:T(8,128)(2,1)S(1)}, bf16[1,32,2048]{2,1,0:T(8,128)(2,1)S(1)}, u32[]{:S(2)}, u32[]{:S(2)}) collective-permute-start(bf16[1,32,2048]{2,1,0:T(8,128)(2,1)S(1)} %get-tuple-element.68), channel_id=1, source_target_pairs={{0,1},{1,2},{2,3},{3,4},{4,5},{5,6},{6,7},{7,0},{8,9},{9,10},{10,1... | collective-permute-start | bytes 393224 | tf_op jit(solution)/shard_map/ppermute | solution.py:327
  53.0 2.4 %collective-permute-start.29 = (bf16[1,32,2048]{2,1,0:T(8,128)(2,1)S(1)}, bf16[1,32,2048]{2,1,0:T(8,128)(2,1)S(1)}, u32[]{:S(2)}, u32[]{:S(2)}) collective-permute-start(bf16[1,32,2048]{2,1,0:T(8,128)(2,1)S(1)} %get-tuple-element.69), channel_id=1, source_target_pairs={{0,2},{1,3},{2,4},{3,5},{4,6},{5,7},{6,0},{7,1},{8,10},{9,11},{10,... | collective-permute-start | bytes 393224 | tf_op jit(solution)/shard_map/ppermute | solution.py:327
  55.4 1.4 %collective-permute-start.31 = (bf16[1,32,2048]{2,1,0:T(8,128)(2,1)S(1)}, bf16[1,32,2048]{2,1,0:T(8,128)(2,1)S(1)}, u32[]{:S(2)}, u32[]{:S(2)}) collective-permute-start(bf16[1,32,2048]{2,1,0:T(8,128)(2,1)S(1)} %get-tuple-element.71), channel_id=1, source_target_pairs={{0,4},{1,5},{2,6},{3,7},{4,0},{5,1},{6,2},{7,3},{8,12},{9,13},{10,... | collective-permute-start | bytes 393224 | tf_op jit(solution)/shard_map/ppermute | solution.py:327
  56.8 1.9 %collective-permute-start.32 = (bf16[1,32,2048]{2,1,0:T(8,128)(2,1)S(1)}, bf16[1,32,2048]{2,1,0:T(8,128)(2,1)S(1)}, u32[]{:S(2)}, u32[]{:S(2)}) collective-permute-start(bf16[1,32,2048]{2,1,0:T(8,128)(2,1)S(1)} %get-tuple-element.72), channel_id=1, source_target_pairs={{0,5},{1,6},{2,7},{3,0},{4,1},{5,2},{6,3},{7,4},{8,13},{9,14},{10,... | collective-permute-start | bytes 393224 | tf_op jit(solution)/shard_map/ppermute | solution.py:327
  58.6 2.2 %spread_out.4 = (bf16[2,32,2048]{2,1,0:T(8,128)(2,1)S(1)}, bf16[2,32,2048]{2,1,0:T(8,128)(2,1)S(1)}, bf16[2,32,2048]{2,1,0:T(8,128)(2,1)S(1)}, bf16[2,32,2048]{2...) custom-call(bf16[8,32,256]{2,1,0:T(8,128)(2,1)S(1)} %weigh.1.refs_0_, ...), custom_call_target="tpu_custom_call" | custom-call | flops 3000000000 | bytes 5000000 | tf_op jit(solution)/shard_map/spread_out/pallas_call | solution.py:239
  60.8 1.0 collective-permute-start.33
  61.9 1.1 collective-permute-done.29.refs_2_
  63.0 1.8 %collective-permute-start.21 = (bf16[2,32,2048]{2,1,0:T(8,128)(2,1)S(1)}, bf16[2,32,2048]{2,1,0:T(8,128)(2,1)S(1)}, u32[]{:S(2)}, u32[]{:S(2)}) collective-permute-start(bf16[2,32,2048]{2,1,0:T(8,128)(2,1)S(1)} %get-tuple-element.60), channel_id=1, source_target_pairs={{0,1},{1,2},{2,3},{3,4},{4,5},{5,6},{6,7},{7,0},{8,9},{9,10},{10,1... | collective-permute-start | bytes 786440 | tf_op jit(solution)/shard_map/ppermute | solution.py:327
  64.7 1.7 %collective-permute-start.22 = (bf16[2,32,2048]{2,1,0:T(8,128)(2,1)S(1)}, bf16[2,32,2048]{2,1,0:T(8,128)(2,1)S(1)}, u32[]{:S(2)}, u32[]{:S(2)}) collective-permute-start(bf16[2,32,2048]{2,1,0:T(8,128)(2,1)S(1)} %get-tuple-element.61), channel_id=1, source_target_pairs={{0,2},{1,3},{2,4},{3,5},{4,6},{5,7},{6,0},{7,1},{8,10},{9,11},{10,... | collective-permute-start | bytes 786440 | tf_op jit(solution)/shard_map/ppermute | solution.py:327
  66.4 1.1 spread_out.3
  67.5 0.9 collective-permute-start.34
  68.7 3.0 %collective-permute-start.14 = (bf16[1,32,2048]{2,1,0:T(8,128)(2,1)S(1)}, bf16[1,32,2048]{2,1,0:T(8,128)(2,1)S(1)}, u32[]{:S(2)}, u32[]{:S(2)}) collective-permute-start(bf16[1,32,2048]{2,1,0:T(8,128)(2,1)S(1)} %get-tuple-element.51), channel_id=1, source_target_pairs={{0,1},{1,2},{2,3},{3,4},{4,5},{5,6},{6,7},{7,0},{8,9},{9,10},{10,1... | collective-permute-start | bytes 393224 | tf_op jit(solution)/shard_map/ppermute | solution.py:327
  71.8 0.9 collective-permute-start.15
  72.6 4.3 %collective-permute-done.34.refs_7_ = bf16[1,32,2048]{2,1,0:T(8,128)(2,1)S(1)} collective-permute-done((bf16[1,32,2048]{2,1,0:T(8,128)(2,1)S(1)}, bf16[1,32,2048]{2,1,0:T(8,128)(2,1)S(1)}, u32[]{:S(2)}, u32[]{:S(2)}) %collective-permute-start.34) | collective-permute-done | bytes 131104 | tf_op jit(solution)/shard_map/ppermute | solution.py:327
  76.9 9.3 %collective-permute-start.23 = (bf16[2,32,2048]{2,1,0:T(8,128)(2,1)S(1)}, bf16[2,32,2048]{2,1,0:T(8,128)(2,1)S(1)}, u32[]{:S(2)}, u32[]{:S(2)}) collective-permute-start(bf16[2,32,2048]{2,1,0:T(8,128)(2,1)S(1)} %get-tuple-element.62), channel_id=1, source_target_pairs={{0,3},{1,4},{2,5},{3,6},{4,7},{5,0},{6,1},{7,2},{8,11},{9,12},{10,... | collective-permute-start | bytes 786440 | tf_op jit(solution)/shard_map/ppermute | solution.py:327
  86.2 3.7 %collective-permute-done.14.refs_1_ = bf16[1,32,2048]{2,1,0:T(8,128)(2,1)S(1)} collective-permute-done((bf16[1,32,2048]{2,1,0:T(8,128)(2,1)S(1)}, bf16[1,32,2048]{2,1,0:T(8,128)(2,1)S(1)}, u32[]{:S(2)}, u32[]{:S(2)}) %collective-permute-start.14) | collective-permute-done | bytes 131104 | tf_op jit(solution)/shard_map/ppermute | solution.py:327
  90.0 2.4 %collective-permute-start.25 = (bf16[2,32,2048]{2,1,0:T(8,128)(2,1)S(1)}, bf16[2,32,2048]{2,1,0:T(8,128)(2,1)S(1)}, u32[]{:S(2)}, u32[]{:S(2)}) collective-permute-start(bf16[2,32,2048]{2,1,0:T(8,128)(2,1)S(1)} %get-tuple-element.64), channel_id=1, source_target_pairs={{0,5},{1,6},{2,7},{3,0},{4,1},{5,2},{6,3},{7,4},{8,13},{9,14},{10,... | collective-permute-start | bytes 786440 | tf_op jit(solution)/shard_map/ppermute | solution.py:327
  93.1 0.7 collective-permute-start.27
  93.8 1.9 %finish.3.refs_9_ = bf16[4,64,32,256]{3,2,1,0:T(8,128)(2,1)} custom-call(s32[3]{0:T(128)S(1)} %pad_add_fusion.here_ref, bf16[1,32,2048]{2,1,0:T(8,128)(2,1)S(1)} %get-tuple-element.67.refs_0_, bf16[1,32,2048]{2,1,0:T(8,128)(2,1)S(1)} %collective-permute-done.28.refs_1_, bf16[1,32,2048]{2,1,0:T(8,128)(2,1)S(1)} %collective-permute-done.29.refs_2_, ...), custom_call_target="tpu_custom_call" | custom-call | flops 700000000 | bytes 2500000 | tf_op jit(solution)/shard_map/finish/pallas_call | solution.py:305
  95.7 3.1 %collective-permute-start.16 = (bf16[1,32,2048]{2,1,0:T(8,128)(2,1)S(1)}, bf16[1,32,2048]{2,1,0:T(8,128)(2,1)S(1)}, u32[]{:S(2)}, u32[]{:S(2)}) collective-permute-start(bf16[1,32,2048]{2,1,0:T(8,128)(2,1)S(1)} %get-tuple-element.53), channel_id=1, source_target_pairs={{0,3},{1,4},{2,5},{3,6},{4,7},{5,0},{6,1},{7,2},{8,11},{9,12},{10,... | collective-permute-start | bytes 393224 | tf_op jit(solution)/shard_map/ppermute | solution.py:327
  99.2 1.2 collective-permute-start.17
  100.4 6.3 %collective-permute-done.25.refs_5_ = bf16[2,32,2048]{2,1,0:T(8,128)(2,1)S(1)} collective-permute-done((bf16[2,32,2048]{2,1,0:T(8,128)(2,1)S(1)}, bf16[2,32,2048]{2,1,0:T(8,128)(2,1)S(1)}, u32[]{:S(2)}, u32[]{:S(2)}) %collective-permute-start.25) | collective-permute-done | bytes 262176 | tf_op jit(solution)/shard_map/ppermute | solution.py:327
  106.7 4.3 %collective-permute-done.26.refs_6_ = bf16[2,32,2048]{2,1,0:T(8,128)(2,1)S(1)} collective-permute-done((bf16[2,32,2048]{2,1,0:T(8,128)(2,1)S(1)}, bf16[2,32,2048]{2,1,0:T(8,128)(2,1)S(1)}, u32[]{:S(2)}, u32[]{:S(2)}) %collective-permute-start.26) | collective-permute-done | bytes 262176 | tf_op jit(solution)/shard_map/ppermute | solution.py:327
  111.0 2.3 %collective-permute-done.27.refs_7_ = bf16[2,32,2048]{2,1,0:T(8,128)(2,1)S(1)} collective-permute-done((bf16[2,32,2048]{2,1,0:T(8,128)(2,1)S(1)}, bf16[2,32,2048]{2,1,0:T(8,128)(2,1)S(1)}, u32[]{:S(2)}, u32[]{:S(2)}) %collective-permute-start.27) | collective-permute-done | bytes 262176 | tf_op jit(solution)/shard_map/ppermute | solution.py:327
  113.3 2.4 %finish.4.refs_9_ = bf16[4,64,32,256]{3,2,1,0:T(8,128)(2,1)} custom-call(s32[3]{0:T(128)S(1)} %pad_add_fusion.here_ref, bf16[2,32,2048]{2,1,0:T(8,128)(2,1)S(1)} %get-tuple-element.59.refs_0_, bf16[2,32,2048]{2,1,0:T(8,128)(2,1)S(1)} %collective-permute-done.21.refs_1_, ...), custom_call_target="tpu_custom_call", output_to_operand_aliasing={{}: (10, {})} | custom-call | flops 1400000000 | bytes 5000000 | tf_op jit(solution)/shard_map/finish/pallas_call | solution.py:305
  115.7 3.4 %collective-permute-done.19.refs_6_ = bf16[1,32,2048]{2,1,0:T(8,128)(2,1)S(1)} collective-permute-done((bf16[1,32,2048]{2,1,0:T(8,128)(2,1)S(1)}, bf16[1,32,2048]{2,1,0:T(8,128)(2,1)S(1)}, u32[]{:S(2)}, u32[]{:S(2)}) %collective-permute-start.19) | collective-permute-done | bytes 131104 | tf_op jit(solution)/shard_map/ppermute | solution.py:327
  119.2 2.4 %collective-permute-done.20.refs_7_ = bf16[1,32,2048]{2,1,0:T(8,128)(2,1)S(1)} collective-permute-done((bf16[1,32,2048]{2,1,0:T(8,128)(2,1)S(1)}, bf16[1,32,2048]{2,1,0:T(8,128)(2,1)S(1)}, u32[]{:S(2)}, u32[]{:S(2)}) %collective-permute-start.20) | collective-permute-done | bytes 131104 | tf_op jit(solution)/shard_map/ppermute | solution.py:327
  121.6 1.9 %finish.5 = bf16[4,64,32,256]{3,2,1,0:T(8,128)(2,1)} custom-call(s32[3]{0:T(128)S(1)} %pad_add_fusion.here_ref, bf16[1,32,2048]{2,1,0:T(8,128)(2,1)S(1)} %get-tuple-element.50.refs_0_, bf16[1,32,2048]{2,1,0:T(8,128)(2,1)S(1)} %collective-permute-done.14.refs_1_, ...), custom_call_target="tpu_custom_call", output_to_operand_aliasing={{}: (10, {})} | custom-call | flops 700000000 | bytes 2500000 | tf_op jit(solution)/shard_map/finish/pallas_call | solution.py:305
  (45 shorter events, 2.1 us)
Async XLA Ops:
  2.9 33.6 %copy-start = (s32[32,256]{1,0:T(8,128)S(1)}, s32[32,256]{1,0:T(8,128)}, u32[]{:S(2)}) copy-start(s32[32,256]{1,0:T(8,128)} %classes_ref.1) | copy-start | bytes 98308
  3.0 33.6 %copy-start.1 = (f32[8,64]{1,0:T(8,128)S(1)}, f32[8,64]{1,0:T(8,128)}, u32[]{:S(2)}) copy-start(f32[8,64]{1,0:T(8,128)} %table_ref.1) | copy-start | bytes 6148
  3.0 44.8 %copy-start.2 = (bf16[256,256]{1,0:T(8,128)(2,1)S(1)}, bf16[256,256]{1,0:T(8,128)(2,1)}, u32[]{:S(2)}) copy-start(bf16[256,256]{1,0:T(8,128)(2,1)} %lon_ref.1) | copy-start | bytes 393220
  3.0 44.8 %copy-start.3 = (bf16[256,256]{1,0:T(8,128)(2,1)S(1)}, bf16[256,256]{1,0:T(8,128)(2,1)}, u32[]{:S(2)}) copy-start(bf16[256,256]{1,0:T(8,128)(2,1)} %lat_ref.1) | copy-start | bytes 393220
  3.0 44.7 %copy-start.4 = (bf16[64,64]{1,0:T(8,128)(2,1)S(1)}, bf16[64,64]{1,0:T(8,128)(2,1)}, u32[]{:S(2)}) copy-start(bf16[64,64]{1,0:T(8,128)(2,1)} %vert_ref.1) | copy-start | bytes 24580
  3.0 2.9 %collective-permute-start = (bf16[4,8,32,256]{3,2,1,0:T(8,128)(2,1)S(1)}, bf16[4,8,32,256]{3,2,1,0:T(8,128)(2,1)S(1)}, u32[]{:S(2)}, u32[]{:S(2)}) collective-permute-start(bf16[4,8,32,256]{3,2,1,0:T(8,128)(2,1)S(1)} %get-tuple-element.41), channel_id=1, source_target_pairs={{0,8},{8,0},{1,9},{9,1},{2,10},{10,2},{3,11},{11,3},{4,12},{12,4},... | collective-permute-start | bytes 1572872 | tf_op jit(solution)/shard_map/ppermute | solution.py:341
  6.1 7.3 %collective-permute-start.1 = (bf16[8,32,256]{2,1,0:T(8,128)(2,1)S(1)}, bf16[8,32,256]{2,1,0:T(8,128)(2,1)S(1)}, u32[]{:S(2)}, u32[]{:S(2)}) collective-permute-start(bf16[8,32,256]{2,1,0:T(8,128)(2,1)S(1)} %get-tuple-element.43), channel_id=1, source_target_pairs={{0,16},{16,32},{32,48},{48,0},{1,17},{17,33},{33,49},{49,1},{2,18}... | collective-permute-start | bytes 393224 | tf_op jit(solution)/shard_map/ppermute | solution.py:327
  7.7 9.6 %collective-permute-start.2 = (bf16[8,32,256]{2,1,0:T(8,128)(2,1)S(1)}, bf16[8,32,256]{2,1,0:T(8,128)(2,1)S(1)}, u32[]{:S(2)}, u32[]{:S(2)}) collective-permute-start(bf16[8,32,256]{2,1,0:T(8,128)(2,1)S(1)} %get-tuple-element.44), channel_id=1, source_target_pairs={{0,32},{16,48},{32,0},{48,16},{1,33},{17,49},{33,1},{49,17},{2,34}... | collective-permute-start | bytes 393224 | tf_op jit(solution)/shard_map/ppermute | solution.py:327
  10.6 6.7 %collective-permute-start.3 = (bf16[8,32,256]{2,1,0:T(8,128)(2,1)S(1)}, bf16[8,32,256]{2,1,0:T(8,128)(2,1)S(1)}, u32[]{:S(2)}, u32[]{:S(2)}) collective-permute-start(bf16[8,32,256]{2,1,0:T(8,128)(2,1)S(1)} %get-tuple-element.45), channel_id=1, source_target_pairs={{0,48},{16,0},{32,16},{48,32},{1,49},{17,1},{33,17},{49,33},{2,50}... | collective-permute-start | bytes 393224 | tf_op jit(solution)/shard_map/ppermute | solution.py:327
  17.4 17.4 %collective-permute-start.6 = (bf16[8,32,256]{2,1,0:T(8,128)(2,1)S(1)}, bf16[8,32,256]{2,1,0:T(8,128)(2,1)S(1)}, u32[]{:S(2)}, u32[]{:S(2)}) collective-permute-start(bf16[8,32,256]{2,1,0:T(8,128)(2,1)S(1)} %join.1.refs_0_), channel_id=1, source_target_pairs={{0,192},{64,0},{128,64},{192,128},{1,193},{65,1},{129,65},{193,129... | collective-permute-start | bytes 393224 | tf_op jit(solution)/shard_map/ppermute | solution.py:327
  23.8 12.8 %collective-permute-start.5 = (bf16[8,32,256]{2,1,0:T(8,128)(2,1)S(1)}, bf16[8,32,256]{2,1,0:T(8,128)(2,1)S(1)}, u32[]{:S(2)}, u32[]{:S(2)}) collective-permute-start(bf16[8,32,256]{2,1,0:T(8,128)(2,1)S(1)} %join.1.refs_0_), channel_id=1, source_target_pairs={{0,128},{64,192},{128,0},{192,64},{1,129},{65,193},{129,1},{193,65... | collective-permute-start | bytes 393224 | tf_op jit(solution)/shard_map/ppermute | solution.py:327
  24.8 11.8 %collective-permute-start.4 = (bf16[8,32,256]{2,1,0:T(8,128)(2,1)S(1)}, bf16[8,32,256]{2,1,0:T(8,128)(2,1)S(1)}, u32[]{:S(2)}, u32[]{:S(2)}) collective-permute-start(bf16[8,32,256]{2,1,0:T(8,128)(2,1)S(1)} %join.1.refs_0_), channel_id=1, source_target_pairs={{0,64},{64,128},{128,192},{192,0},{1,65},{65,129},{129,193},{193,1... | collective-permute-start | bytes 393224 | tf_op jit(solution)/shard_map/ppermute | solution.py:327
  37.4 6.4 %collective-permute-start.9 = (bf16[8,32,256]{2,1,0:T(8,128)(2,1)S(1)}, bf16[8,32,256]{2,1,0:T(8,128)(2,1)S(1)}, u32[]{:S(2)}, u32[]{:S(2)}) collective-permute-start(bf16[8,32,256]{2,1,0:T(8,128)(2,1)S(1)} %weigh.1.refs_0_), channel_id=1, source_target_pairs={{0,48},{16,0},{32,16},{48,32},{1,49},{17,1},{33,17},{49,33},{2,50}... | collective-permute-start | bytes 393224 | tf_op jit(solution)/shard_map/ppermute | solution.py:327
  39.8 6.6 %collective-permute-start.8 = (bf16[8,32,256]{2,1,0:T(8,128)(2,1)S(1)}, bf16[8,32,256]{2,1,0:T(8,128)(2,1)S(1)}, u32[]{:S(2)}, u32[]{:S(2)}) collective-permute-start(bf16[8,32,256]{2,1,0:T(8,128)(2,1)S(1)} %weigh.1.refs_0_), channel_id=1, source_target_pairs={{0,32},{16,48},{32,0},{48,16},{1,33},{17,49},{33,1},{49,17},{2,34}... | collective-permute-start | bytes 393224 | tf_op jit(solution)/shard_map/ppermute | solution.py:327
  40.2 7.6 %collective-permute-start.7 = (bf16[8,32,256]{2,1,0:T(8,128)(2,1)S(1)}, bf16[8,32,256]{2,1,0:T(8,128)(2,1)S(1)}, u32[]{:S(2)}, u32[]{:S(2)}) collective-permute-start(bf16[8,32,256]{2,1,0:T(8,128)(2,1)S(1)} %weigh.1.refs_0_), channel_id=1, source_target_pairs={{0,16},{16,32},{32,48},{48,0},{1,17},{17,33},{33,49},{49,1},{2,18}... | collective-permute-start | bytes 393224 | tf_op jit(solution)/shard_map/ppermute | solution.py:327
  40.9 8.0 %collective-permute-start.10 = (bf16[8,32,256]{2,1,0:T(8,128)(2,1)S(1)}, bf16[8,32,256]{2,1,0:T(8,128)(2,1)S(1)}, u32[]{:S(2)}, u32[]{:S(2)}) collective-permute-start(bf16[8,32,256]{2,1,0:T(8,128)(2,1)S(1)} %weigh.1.refs_0_), channel_id=1, source_target_pairs={{0,8},{8,0},{1,9},{9,1},{2,10},{10,2},{3,11},{11,3},{4,12},{12,4},... | collective-permute-start | bytes 393224 | tf_op jit(solution)/shard_map/ppermute | solution.py:347
  43.8 5.2 %collective-permute-start.13 = (bf16[8,32,256]{2,1,0:T(8,128)(2,1)S(1)}, bf16[8,32,256]{2,1,0:T(8,128)(2,1)S(1)}, u32[]{:S(2)}, u32[]{:S(2)}) collective-permute-start(bf16[8,32,256]{2,1,0:T(8,128)(2,1)S(1)} %collective-permute-done.9.refs_3_), channel_id=1, source_target_pairs={{0,8},{8,0},{1,9},{9,1},{2,10},{10,2},{3,11},{11,3},{4,12},{12,4},... | collective-permute-start | bytes 393224 | tf_op jit(solution)/shard_map/ppermute | solution.py:347
  46.4 2.5 %collective-permute-start.12 = (bf16[8,32,256]{2,1,0:T(8,128)(2,1)S(1)}, bf16[8,32,256]{2,1,0:T(8,128)(2,1)S(1)}, u32[]{:S(2)}, u32[]{:S(2)}) collective-permute-start(bf16[8,32,256]{2,1,0:T(8,128)(2,1)S(1)} %collective-permute-done.8.refs_2_), channel_id=1, source_target_pairs={{0,8},{8,0},{1,9},{9,1},{2,10},{10,2},{3,11},{11,3},{4,12},{12,4},... | collective-permute-start | bytes 393224 | tf_op jit(solution)/shard_map/ppermute | solution.py:347
  47.7 1.3 %collective-permute-start.11 = (bf16[8,32,256]{2,1,0:T(8,128)(2,1)S(1)}, bf16[8,32,256]{2,1,0:T(8,128)(2,1)S(1)}, u32[]{:S(2)}, u32[]{:S(2)}) collective-permute-start(bf16[8,32,256]{2,1,0:T(8,128)(2,1)S(1)} %collective-permute-done.7.refs_1_), channel_id=1, source_target_pairs={{0,8},{8,0},{1,9},{9,1},{2,10},{10,2},{3,11},{11,3},{4,12},{12,4},... | collective-permute-start | bytes 393224 | tf_op jit(solution)/shard_map/ppermute | solution.py:347
  50.2 10.6 %collective-permute-start.28 = (bf16[1,32,2048]{2,1,0:T(8,128)(2,1)S(1)}, bf16[1,32,2048]{2,1,0:T(8,128)(2,1)S(1)}, u32[]{:S(2)}, u32[]{:S(2)}) collective-permute-start(bf16[1,32,2048]{2,1,0:T(8,128)(2,1)S(1)} %get-tuple-element.68), channel_id=1, source_target_pairs={{0,1},{1,2},{2,3},{3,4},{4,5},{5,6},{6,7},{7,0},{8,9},{9,10},{10,1... | collective-permute-start | bytes 393224 | tf_op jit(solution)/shard_map/ppermute | solution.py:327
  53.0 9.9 %collective-permute-start.29 = (bf16[1,32,2048]{2,1,0:T(8,128)(2,1)S(1)}, bf16[1,32,2048]{2,1,0:T(8,128)(2,1)S(1)}, u32[]{:S(2)}, u32[]{:S(2)}) collective-permute-start(bf16[1,32,2048]{2,1,0:T(8,128)(2,1)S(1)} %get-tuple-element.69), channel_id=1, source_target_pairs={{0,2},{1,3},{2,4},{3,5},{4,6},{5,7},{6,0},{7,1},{8,10},{9,11},{10,... | collective-permute-start | bytes 393224 | tf_op jit(solution)/shard_map/ppermute | solution.py:327
  55.4 9.4 %collective-permute-start.30 = (bf16[1,32,2048]{2,1,0:T(8,128)(2,1)S(1)}, bf16[1,32,2048]{2,1,0:T(8,128)(2,1)S(1)}, u32[]{:S(2)}, u32[]{:S(2)}) collective-permute-start(bf16[1,32,2048]{2,1,0:T(8,128)(2,1)S(1)} %get-tuple-element.70), channel_id=1, source_target_pairs={{0,3},{1,4},{2,5},{3,6},{4,7},{5,0},{6,1},{7,2},{8,11},{9,12},{10,... | collective-permute-start | bytes 393224 | tf_op jit(solution)/shard_map/ppermute | solution.py:327
  55.4 12.2 %collective-permute-start.31 = (bf16[1,32,2048]{2,1,0:T(8,128)(2,1)S(1)}, bf16[1,32,2048]{2,1,0:T(8,128)(2,1)S(1)}, u32[]{:S(2)}, u32[]{:S(2)}) collective-permute-start(bf16[1,32,2048]{2,1,0:T(8,128)(2,1)S(1)} %get-tuple-element.71), channel_id=1, source_target_pairs={{0,4},{1,5},{2,6},{3,7},{4,0},{5,1},{6,2},{7,3},{8,12},{9,13},{10,... | collective-permute-start | bytes 393224 | tf_op jit(solution)/shard_map/ppermute | solution.py:327
  56.8 12.0 %collective-permute-start.32 = (bf16[1,32,2048]{2,1,0:T(8,128)(2,1)S(1)}, bf16[1,32,2048]{2,1,0:T(8,128)(2,1)S(1)}, u32[]{:S(2)}, u32[]{:S(2)}) collective-permute-start(bf16[1,32,2048]{2,1,0:T(8,128)(2,1)S(1)} %get-tuple-element.72), channel_id=1, source_target_pairs={{0,5},{1,6},{2,7},{3,0},{4,1},{5,2},{6,3},{7,4},{8,13},{9,14},{10,... | collective-permute-start | bytes 393224 | tf_op jit(solution)/shard_map/ppermute | solution.py:327
  60.8 10.9 %collective-permute-start.33 = (bf16[1,32,2048]{2,1,0:T(8,128)(2,1)S(1)}, bf16[1,32,2048]{2,1,0:T(8,128)(2,1)S(1)}, u32[]{:S(2)}, u32[]{:S(2)}) collective-permute-start(bf16[1,32,2048]{2,1,0:T(8,128)(2,1)S(1)} %get-tuple-element.73), channel_id=1, source_target_pairs={{0,6},{1,7},{2,0},{3,1},{4,2},{5,3},{6,4},{7,5},{8,14},{9,15},{10,... | collective-permute-start | bytes 393224 | tf_op jit(solution)/shard_map/ppermute | solution.py:327
  63.0 29.5 %collective-permute-start.21 = (bf16[2,32,2048]{2,1,0:T(8,128)(2,1)S(1)}, bf16[2,32,2048]{2,1,0:T(8,128)(2,1)S(1)}, u32[]{:S(2)}, u32[]{:S(2)}) collective-permute-start(bf16[2,32,2048]{2,1,0:T(8,128)(2,1)S(1)} %get-tuple-element.60), channel_id=1, source_target_pairs={{0,1},{1,2},{2,3},{3,4},{4,5},{5,6},{6,7},{7,0},{8,9},{9,10},{10,1... | collective-permute-start | bytes 786440 | tf_op jit(solution)/shard_map/ppermute | solution.py:327
  64.7 28.4 %collective-permute-start.22 = (bf16[2,32,2048]{2,1,0:T(8,128)(2,1)S(1)}, bf16[2,32,2048]{2,1,0:T(8,128)(2,1)S(1)}, u32[]{:S(2)}, u32[]{:S(2)}) collective-permute-start(bf16[2,32,2048]{2,1,0:T(8,128)(2,1)S(1)} %get-tuple-element.61), channel_id=1, source_target_pairs={{0,2},{1,3},{2,4},{3,5},{4,6},{5,7},{6,0},{7,1},{8,10},{9,11},{10,... | collective-permute-start | bytes 786440 | tf_op jit(solution)/shard_map/ppermute | solution.py:327
  67.5 9.4 %collective-permute-start.34 = (bf16[1,32,2048]{2,1,0:T(8,128)(2,1)S(1)}, bf16[1,32,2048]{2,1,0:T(8,128)(2,1)S(1)}, u32[]{:S(2)}, u32[]{:S(2)}) collective-permute-start(bf16[1,32,2048]{2,1,0:T(8,128)(2,1)S(1)} %get-tuple-element.74), channel_id=1, source_target_pairs={{0,7},{1,0},{2,1},{3,2},{4,3},{5,4},{6,5},{7,6},{8,15},{9,8},{10,9... | collective-permute-start | bytes 393224 | tf_op jit(solution)/shard_map/ppermute | solution.py:327
  68.7 21.2 %collective-permute-start.14 = (bf16[1,32,2048]{2,1,0:T(8,128)(2,1)S(1)}, bf16[1,32,2048]{2,1,0:T(8,128)(2,1)S(1)}, u32[]{:S(2)}, u32[]{:S(2)}) collective-permute-start(bf16[1,32,2048]{2,1,0:T(8,128)(2,1)S(1)} %get-tuple-element.51), channel_id=1, source_target_pairs={{0,1},{1,2},{2,3},{3,4},{4,5},{5,6},{6,7},{7,0},{8,9},{9,10},{10,1... | collective-permute-start | bytes 393224 | tf_op jit(solution)/shard_map/ppermute | solution.py:327
  71.8 18.2 %collective-permute-start.15 = (bf16[1,32,2048]{2,1,0:T(8,128)(2,1)S(1)}, bf16[1,32,2048]{2,1,0:T(8,128)(2,1)S(1)}, u32[]{:S(2)}, u32[]{:S(2)}) collective-permute-start(bf16[1,32,2048]{2,1,0:T(8,128)(2,1)S(1)} %get-tuple-element.52), channel_id=1, source_target_pairs={{0,2},{1,3},{2,4},{3,5},{4,6},{5,7},{6,0},{7,1},{8,10},{9,11},{10,... | collective-permute-start | bytes 393224 | tf_op jit(solution)/shard_map/ppermute | solution.py:327
  76.9 18.8 %collective-permute-start.23 = (bf16[2,32,2048]{2,1,0:T(8,128)(2,1)S(1)}, bf16[2,32,2048]{2,1,0:T(8,128)(2,1)S(1)}, u32[]{:S(2)}, u32[]{:S(2)}) collective-permute-start(bf16[2,32,2048]{2,1,0:T(8,128)(2,1)S(1)} %get-tuple-element.62), channel_id=1, source_target_pairs={{0,3},{1,4},{2,5},{3,6},{4,7},{5,0},{6,1},{7,2},{8,11},{9,12},{10,... | collective-permute-start | bytes 786440 | tf_op jit(solution)/shard_map/ppermute | solution.py:327
  90.0 9.2 %collective-permute-start.24 = (bf16[2,32,2048]{2,1,0:T(8,128)(2,1)S(1)}, bf16[2,32,2048]{2,1,0:T(8,128)(2,1)S(1)}, u32[]{:S(2)}, u32[]{:S(2)}) collective-permute-start(bf16[2,32,2048]{2,1,0:T(8,128)(2,1)S(1)} %get-tuple-element.63), channel_id=1, source_target_pairs={{0,4},{1,5},{2,6},{3,7},{4,0},{5,1},{6,2},{7,3},{8,12},{9,13},{10,... | collective-permute-start | bytes 786440 | tf_op jit(solution)/shard_map/ppermute | solution.py:327
  90.0 16.7 %collective-permute-start.25 = (bf16[2,32,2048]{2,1,0:T(8,128)(2,1)S(1)}, bf16[2,32,2048]{2,1,0:T(8,128)(2,1)S(1)}, u32[]{:S(2)}, u32[]{:S(2)}) collective-permute-start(bf16[2,32,2048]{2,1,0:T(8,128)(2,1)S(1)} %get-tuple-element.64), channel_id=1, source_target_pairs={{0,5},{1,6},{2,7},{3,0},{4,1},{5,2},{6,3},{7,4},{8,13},{9,14},{10,... | collective-permute-start | bytes 786440 | tf_op jit(solution)/shard_map/ppermute | solution.py:327
  92.4 18.5 %collective-permute-start.26 = (bf16[2,32,2048]{2,1,0:T(8,128)(2,1)S(1)}, bf16[2,32,2048]{2,1,0:T(8,128)(2,1)S(1)}, u32[]{:S(2)}, u32[]{:S(2)}) collective-permute-start(bf16[2,32,2048]{2,1,0:T(8,128)(2,1)S(1)} %get-tuple-element.65), channel_id=1, source_target_pairs={{0,6},{1,7},{2,0},{3,1},{4,2},{5,3},{6,4},{7,5},{8,14},{9,15},{10,... | collective-permute-start | bytes 786440 | tf_op jit(solution)/shard_map/ppermute | solution.py:327
  93.1 20.2 %collective-permute-start.27 = (bf16[2,32,2048]{2,1,0:T(8,128)(2,1)S(1)}, bf16[2,32,2048]{2,1,0:T(8,128)(2,1)S(1)}, u32[]{:S(2)}, u32[]{:S(2)}) collective-permute-start(bf16[2,32,2048]{2,1,0:T(8,128)(2,1)S(1)} %get-tuple-element.66), channel_id=1, source_target_pairs={{0,7},{1,0},{2,1},{3,2},{4,3},{5,4},{6,5},{7,6},{8,15},{9,8},{10,9... | collective-permute-start | bytes 786440 | tf_op jit(solution)/shard_map/ppermute | solution.py:327
  95.7 20.0 %collective-permute-start.16 = (bf16[1,32,2048]{2,1,0:T(8,128)(2,1)S(1)}, bf16[1,32,2048]{2,1,0:T(8,128)(2,1)S(1)}, u32[]{:S(2)}, u32[]{:S(2)}) collective-permute-start(bf16[1,32,2048]{2,1,0:T(8,128)(2,1)S(1)} %get-tuple-element.53), channel_id=1, source_target_pairs={{0,3},{1,4},{2,5},{3,6},{4,7},{5,0},{6,1},{7,2},{8,11},{9,12},{10,... | collective-permute-start | bytes 393224 | tf_op jit(solution)/shard_map/ppermute | solution.py:327
  99.2 16.6 %collective-permute-start.17 = (bf16[1,32,2048]{2,1,0:T(8,128)(2,1)S(1)}, bf16[1,32,2048]{2,1,0:T(8,128)(2,1)S(1)}, u32[]{:S(2)}, u32[]{:S(2)}) collective-permute-start(bf16[1,32,2048]{2,1,0:T(8,128)(2,1)S(1)} %get-tuple-element.54), channel_id=1, source_target_pairs={{0,4},{1,5},{2,6},{3,7},{4,0},{5,1},{6,2},{7,3},{8,12},{9,13},{10,... | collective-permute-start | bytes 393224 | tf_op jit(solution)/shard_map/ppermute | solution.py:327
  106.7 9.0 %collective-permute-start.18 = (bf16[1,32,2048]{2,1,0:T(8,128)(2,1)S(1)}, bf16[1,32,2048]{2,1,0:T(8,128)(2,1)S(1)}, u32[]{:S(2)}, u32[]{:S(2)}) collective-permute-start(bf16[1,32,2048]{2,1,0:T(8,128)(2,1)S(1)} %get-tuple-element.55), channel_id=1, source_target_pairs={{0,5},{1,6},{2,7},{3,0},{4,1},{5,2},{6,3},{7,4},{8,13},{9,14},{10,... | collective-permute-start | bytes 393224 | tf_op jit(solution)/shard_map/ppermute | solution.py:327
  111.0 8.2 %collective-permute-start.19 = (bf16[1,32,2048]{2,1,0:T(8,128)(2,1)S(1)}, bf16[1,32,2048]{2,1,0:T(8,128)(2,1)S(1)}, u32[]{:S(2)}, u32[]{:S(2)}) collective-permute-start(bf16[1,32,2048]{2,1,0:T(8,128)(2,1)S(1)} %get-tuple-element.56), channel_id=1, source_target_pairs={{0,6},{1,7},{2,0},{3,1},{4,2},{5,3},{6,4},{7,5},{8,14},{9,15},{10,... | collective-permute-start | bytes 393224 | tf_op jit(solution)/shard_map/ppermute | solution.py:327
  113.3 8.3 %collective-permute-start.20 = (bf16[1,32,2048]{2,1,0:T(8,128)(2,1)S(1)}, bf16[1,32,2048]{2,1,0:T(8,128)(2,1)S(1)}, u32[]{:S(2)}, u32[]{:S(2)}) collective-permute-start(bf16[1,32,2048]{2,1,0:T(8,128)(2,1)S(1)} %get-tuple-element.57), channel_id=1, source_target_pairs={{0,7},{1,0},{2,1},{3,2},{4,3},{5,4},{6,5},{7,6},{8,15},{9,8},{10,9... | collective-permute-start | bytes 393224 | tf_op jit(solution)/shard_map/ppermute | solution.py:327

commit v3 on v2

--- a/solution.py
+++ b/solution.py
@@ -24,52 +24,79 @@
     return lax.dot_general(a, b, (((1,), (1,)), ((), ())), preferred_element_type=F32)
 
 
-def half_sum_kernel(other, here_ref, spread_ref, controls_ref, out_ref, kept_ref, controls_buf, sems):
+def other_half_kernel(here_ref, spread_ref, controls_ref, out_ref, kept_ref, own_ref, buf, sems):
     step = out_ref.shape[1]
     copies = []
-    for d in range(Y):
-        at = ((here_ref[0] ^ other) * Y + ((here_ref[1] + d) & (Y - 1))) * step
-        pair = (
-            pltpu.make_async_copy(
-                spread_ref.at[:, pl.ds(at, step)], kept_ref.at[d], sems.at[0, d]
-            ),
-            pltpu.make_async_copy(
-                controls_ref.at[:, pl.ds(at, step)], controls_buf.at[d], sems.at[1, d]
-            ),
-        )
-        for copy in pair:
-            copy.start()
-        copies.append(pair)
-    for d, pair in enumerate(copies):
+    for other in (1, 0):
+        for d in range(Y):
+            at = ((here_ref[0] ^ other) * Y + ((here_ref[1] + d) & (Y - 1))) * step
+            target = buf if other else own_ref
+            pair = (
+                pltpu.make_async_copy(
+                    spread_ref.at[:, pl.ds(at, step)], kept_ref.at[other, d], sems.at[0, other, d]
+                ),
+                pltpu.make_async_copy(
+                    controls_ref.at[:, pl.ds(at, step)], target.at[d], sems.at[1, other, d]
+                ),
+            )
+            for copy in pair:
+                copy.start()
+            copies.append(pair)
+    for n, pair in enumerate(copies):
         for copy in pair:
             copy.wait()
-        for l in range(step):
-            total = kept_ref[d, 0, l].astype(F32) * controls_buf[d, 0, l].astype(F32)
-            for k in range(1, kept_ref.shape[1]):
-                total += kept_ref[d, k, l].astype(F32) * controls_buf[d, k, l].astype(F32)
-            out_ref[d, l] = total.astype(out_ref.dtype)
-
-
-def half_sum(other, here, spread, controls, dtype):
+        if n < Y:
+            add_members(kept_ref.at[1, n], buf.at[n], out_ref.at[n])
+
+
+def add_members(spread_ref, controls_ref, out_ref):
+    for l in range(out_ref.shape[0]):
+        total = spread_ref[0, l].astype(F32) * controls_ref[0, l].astype(F32)
+        for k in range(1, spread_ref.shape[0]):
+            total += spread_ref[k, l].astype(F32) * controls_ref[k, l].astype(F32)
+        out_ref[l] = total.astype(out_ref.dtype)
+
+
+def other_half(here, spread, controls):
     members, levels, rows, cols = spread.shape
     step = levels // (CORE * Y)
     smem, vmem = (pl.BlockSpec(memory_space=space) for space in (pltpu.SMEM, pltpu.VMEM))
     hbm = pl.BlockSpec(memory_space=pltpu.HBM)
     field = (Y, members, step, rows, cols)
     return pl.pallas_call(
-        functools.partial(half_sum_kernel, other),
+        other_half_kernel,
         in_specs=[smem, hbm, hbm],
-        out_specs=[vmem, vmem],
+        out_specs=[vmem] * 3,
         out_shape=[
-            jax.ShapeDtypeStruct((Y, step, rows, cols), dtype),
+            jax.ShapeDtypeStruct((Y, step, rows, cols), BF16),
+            jax.ShapeDtypeStruct((CORE, *field), BF16),
             jax.ShapeDtypeStruct(field, BF16),
         ],
-        scratch_shapes=[pltpu.VMEM(field, BF16), pltpu.SemaphoreType.DMA((2, Y))],
+        scratch_shapes=[pltpu.VMEM(field, BF16), pltpu.SemaphoreType.DMA((2, CORE, Y))],
+        compiler_params=pltpu.CompilerParams(vmem_limit_bytes=12 * 1024 * 1024),
+        name="other_half",
+    )(here, spread, controls)
+
+
+def own_half_kernel(kept_ref, controls_ref, out_ref):
+    for d in range(Y):
+        add_members(kept_ref.at[0, d], controls_ref.at[d], out_ref.at[d])
+
+
+def own_half(kept, controls):
+    _, _, _, step, rows, cols = kept.shape
+    vmem = pl.BlockSpec(memory_space=pltpu.VMEM)
+    return pl.pallas_call(
+        own_half_kernel,
+        in_specs=[vmem] * 2,
+        out_specs=vmem,
+        out_shape=jax.ShapeDtypeStruct((Y, step, rows, cols), F32),
         compiler_params=pltpu.CompilerParams(vmem_limit_bytes=12 * 1024 * 1024),
         cost_estimate=pl.CostEstimate(
             flops=300_000_000, bytes_accessed=4_200_000, transcendentals=0
         ),
-    )(here, spread, controls)
+        name="own_half",
+    )(kept, controls)
 
 
 def chip_sum_kernel(keep_ref, arrived_ref, *outs):
@@ -92,7 +119,20 @@
     )(keep, arrived)
 
 
-def tables_kernel(here_ref, vert_ref, lon_ref, lat_ref, big_ref, lon_out_ref, turned_ref):
+def tables_kernel(
+    here_ref, table_ref, classes_ref, vert_ref, lon_ref, lat_ref,
+    precision_ref, big_ref, lon_out_ref, turned_ref,
+):
+    classes = classes_ref[...]
+    numbers = range(1, table_ref.shape[0])
+    is_class = [classes == n for n in numbers]
+    count = precision_ref.shape[0]
+    first = (here_ref[0] * Y + here_ref[1]) * count
+    for l in range(count):
+        precision = jnp.full(classes.shape, table_ref[0, first + l], F32)
+        for n in numbers:
+            precision = jnp.where(is_class[n - 1], table_ref[n, first + l], precision)
+        precision_ref[l] = precision
     me = here_ref[2]
     levels = vert_ref.shape[0]
     size = levels * 8
@@ -125,15 +165,16 @@
         ).astype(BF16)
 
 
-def tables(here, vert_loc, lon_loc, lat_loc):
+def tables(here, prec_table, classes, vert_loc, lon_loc, lat_loc):
     levels = vert_loc.shape[0]
     size = lat_loc.shape[0]
     return pl.pallas_call(
         tables_kernel,
-        in_specs=[pl.BlockSpec(memory_space=pltpu.SMEM)]
-        + [pl.BlockSpec(memory_space=pltpu.VMEM)] * 3,
-        out_specs=[pl.BlockSpec(memory_space=pltpu.VMEM)] * 3,
+        in_specs=[pl.BlockSpec(memory_space=pltpu.SMEM)] * 2
+        + [pl.BlockSpec(memory_space=pltpu.VMEM)] * 4,
+        out_specs=[pl.BlockSpec(memory_space=pltpu.VMEM)] * 4,
         out_shape=[
+            jax.ShapeDtypeStruct((levels // (CORE * Y), *classes.shape), F32),
             jax.ShapeDtypeStruct((levels * 8, levels * 8), BF16),
             jax.ShapeDtypeStruct(lon_loc.shape, BF16),
             jax.ShapeDtypeStruct((EACH, size, size), BF16),
@@ -143,7 +184,7 @@
             flops=600_000_000, bytes_accessed=2_000_000, transcendentals=0
         ),
         name="tables",
-    )(here, vert_loc, lon_loc, lat_loc)
+    )(here, prec_table, classes, vert_loc, lon_loc, lat_loc)
 
 
 def join_kernel(*refs):
@@ -167,38 +208,30 @@
     )(*pieces)
 
 
-def weigh_kernel(here_ref, classes_ref, table_ref, *refs):
+def weigh_kernel(precision_ref, *refs):
     *pieces, out_ref = refs
-    classes = classes_ref[...]
-    first = (here_ref[0] * Y + here_ref[1]) * out_ref.shape[0]
-    numbers = range(1, table_ref.shape[0])
-    at = [classes == n for n in numbers]
     for l in range(out_ref.shape[0]):
         total = pieces[0][l].astype(F32)
         for piece in pieces[1:]:
             total += piece[l].astype(F32)
-        precision = jnp.full(classes.shape, table_ref[0, first + l], F32)
-        for n in numbers:
-            precision = jnp.where(at[n - 1], table_ref[n, first + l], precision)
-        out_ref[l] = (total * precision).astype(BF16)
-
-
-def weigh(here, classes, prec_table, pieces):
+        out_ref[l] = (total * precision_ref[l]).astype(BF16)
+
+
+def weigh(precision, pieces):
     vmem = pl.BlockSpec(memory_space=pltpu.VMEM)
-    smem = pl.BlockSpec(memory_space=pltpu.SMEM)
     return pl.pallas_call(
         weigh_kernel,
-        in_specs=[smem, vmem, smem] + [vmem] * len(pieces),
+        in_specs=[vmem] * (1 + len(pieces)),
         out_specs=vmem,
         out_shape=jax.ShapeDtypeStruct(pieces[0].shape, BF16),
         compiler_params=pltpu.CompilerParams(vmem_limit_bytes=8 * 1024 * 1024),
         name="weigh",
-    )(here, classes, prec_table, *pieces)
+    )(precision, *pieces)
 
 
 def spread_out_kernel(first, *refs):
     pieces = CORE * Y
-    weights, kept, refs = refs[:pieces], refs[pieces : pieces + CORE], refs[pieces + CORE :]
+    weights, kept, refs = refs[:pieces], refs[pieces], refs[pieces + 1 :]
     big_ref, lon_ref, outs = refs[0], refs[1], refs[2 : 2 + LATS]
     adj, mixed = refs[2 + LATS :]
     levels, rows, cols = adj.shape
@@ -209,7 +242,7 @@
         for low in range(0, rows, 16):
             for n, piece in enumerate(weights):
                 for i in range(step):
-                    own = kept[n // Y][-n % Y, first + k, i, low : low + 16, :]
+                    own = kept[n // Y, -n % Y, first + k, i, low : low + 16, :]
                     weight = piece[i, low : low + 16, :]
                     adj[n * step + i, low : low + 16, :] = own.astype(F32) * weight.astype(F32)
             for at in range(low, low + 16, 8):
@@ -235,7 +268,7 @@
     _, rows, cols = weights[0].shape
     share = cols // LATS
     vmem = pl.BlockSpec(memory_space=pltpu.VMEM)
-    args = (*weights, *kept, big, lon)
+    args = (*weights, kept, big, lon)
     return pl.pallas_call(
         functools.partial(spread_out_kernel, first),
         in_specs=[vmem] * len(args),
@@ -335,20 +368,22 @@
     here = jnp.stack([lax.axis_index(name) for name in ("core", "y", LAT)])
     swap = [(0, 1), (1, 0)]
 
-    big, lon, turned = tables(here, vert_loc, lon_loc, lat_loc)
-    send, kept_other = half_sum(1, here, spread, controls, BF16)
-    keep, kept_own = half_sum(0, here, spread, controls, F32)
+    precision, big, lon, turned = tables(here, prec_table, classes, vert_loc, lon_loc, lat_loc)
+    send, kept, own_controls = other_half(here, spread, controls)
+    keep = own_half(kept, own_controls)
     arrived = lax.ppermute(send, "core", swap)
     pieces = chip_sum(keep, arrived)
     along_y = join(passed_on("y", pieces, range(1, Y)))
     along_z = passed_on("zh", [along_y] * ZH, Z_ORDER)
-    weighted = weigh(here, classes, prec_table, along_z)
+    weighted = weigh(precision, along_z)
     own = passed_on("y", [weighted] * Y, range(1, Y))
-    weights = own + [lax.ppermute(x, "core", swap) for x in own]
+    weights = list(own)
+    for x in own:
+        weights.append(lax.ppermute(x, "core", swap))
 
     result = None
     for start, count in GROUPS:
-        sending = spread_out(weights, (kept_own, kept_other), big, lon, start, count)
+        sending = spread_out(weights, kept, big, lon, start, count)
         parts = passed_on(LAT, sending, ORDER)
         result = finish(here, parts, turned, start, members, result)
     return result

time: 124 us -> 121 us (0.976)
  the two profiles are of different devices: /device:TPU:6 before, /device:TPU:1 now
where the time goes in v3:
time: 121 us; the launch traced here: 119 us
  starting transfers between devices  65.7 us (54%)
  waiting for transfers between devices  36.5 us (30%)
  Pallas kernels  16.4 us (14%)
    ppermute x30, starting transfers between devices, passed_on(): lax.ppermute(pieces[d], axis, [(i, (i + d) % count) for i in range(count)])  51.6 us
    ppermute x30, waiting for transfers between devices, passed_on(): lax.ppermute(pieces[d], axis, [(i, (i + d) % count) for i in range(count)])  34.2 us
    ppermute x4, starting transfers between devices, local(): weights.append(lax.ppermute(x, 'core', swap))  10.8 us
    pallas_call x3, Pallas kernels, finish(): pl.pallas_call(functools.partial(finish_kernel, first), in_specs=in_specs...  6.18 us
    pallas_call x3, Pallas kernels, spread_out(): pl.pallas_call(functools.partial(spread_out_kernel, first), in_specs=[vme...  4.38 us
    pallas_call x1, Pallas kernels, other_half(): pl.pallas_call(other_half_kernel, in_specs=[smem, hbm, hbm], out_specs=[v...  4.06 us
    ppermute x1, starting transfers between devices, local(): arrived = lax.ppermute(send, 'core', swap)  3.29 us
  transfers between devices with their start and end apart: 35, of which 13 were waited for; matrix products, arithmetic and copies ran while one was open for 0% of the time, Pallas kernels for 8%

profile of v3, /device:TPU:1, one launch (start us, length us, event | category | flops | bytes accessed | tf_op | source)
XLA Modules:
  0.0 119.0 jit_solution(13932671821434734037)
XLA Ops:
  0.1 4.1 %other_half.1 = (bf16[4,8,32,256]{3,2,1,0:T(8,128)(2,1)S(1)}, bf16[2,4,4,8,32,256]{5,4,3,2,1,0:T(8,128)(2,1)S(1)}, bf16[4,4,8,32,256]{4,3,2,1,0:T(8,128)(2,1)S(1)}) custom-call(s32[3]{0:T(128)S(1)} %pad_add_fusion.here_ref, bf16[4,64,32,256]{3,2,1,0:T(8,128)(2,1)} %spread_ref.1, bf16[4,64,32,256]{3,2,1,0:T(8,128)(2,1)} %controls_ref.1), custom_call_target="tpu_custom_call" | custom-call | tf_op jit(solution)/shard_map/other_half/pallas_call | solution.py:66
  4.1 3.3 %collective-permute-start = (bf16[4,8,32,256]{3,2,1,0:T(8,128)(2,1)S(1)}, bf16[4,8,32,256]{3,2,1,0:T(8,128)(2,1)S(1)}, u32[]{:S(2)}, u32[]{:S(2)}) collective-permute-start(bf16[4,8,32,256]{3,2,1,0:T(8,128)(2,1)S(1)} %get-tuple-element.43), channel_id=1, source_target_pairs={{0,8},{8,0},{1,9},{9,1},{2,10},{10,2},{3,11},{11,3},{4,12},{12,4},... | collective-permute-start | bytes 1572872 | tf_op jit(solution)/shard_map/ppermute | solution.py:374
  7.7 1.3 %collective-permute-done.arrived_ref = bf16[4,8,32,256]{3,2,1,0:T(8,128)(2,1)S(1)} collective-permute-done((bf16[4,8,32,256]{3,2,1,0:T(8,128)(2,1)S(1)}, bf16[4,8,32,256]{3,2,1,0:T(8,128)(2,1)S(1)}, u32[]{:S(2)}, u32[]{:S(2)}) %collective-permute-start) | collective-permute-done | bytes 524320 | tf_op jit(solution)/shard_map/ppermute | solution.py:374
  9.2 2.2 %collective-permute-start.2 = (bf16[8,32,256]{2,1,0:T(8,128)(2,1)S(1)}, bf16[8,32,256]{2,1,0:T(8,128)(2,1)S(1)}, u32[]{:S(2)}, u32[]{:S(2)}) collective-permute-start(bf16[8,32,256]{2,1,0:T(8,128)(2,1)S(1)} %get-tuple-element.46), channel_id=1, source_target_pairs={{0,32},{16,48},{32,0},{48,16},{1,33},{17,49},{33,1},{49,17},{2,34}... | collective-permute-start | bytes 393224 | tf_op jit(solution)/shard_map/ppermute | solution.py:360
  11.3 1.1 collective-permute-start.3
  12.4 3.1 %collective-permute-done.1.refs_1_ = bf16[8,32,256]{2,1,0:T(8,128)(2,1)S(1)} collective-permute-done((bf16[8,32,256]{2,1,0:T(8,128)(2,1)S(1)}, bf16[8,32,256]{2,1,0:T(8,128)(2,1)S(1)}, u32[]{:S(2)}, u32[]{:S(2)}) %collective-permute-start.1) | collective-permute-done | bytes 131104 | tf_op jit(solution)/shard_map/ppermute | solution.py:360
  15.5 1.9 %collective-permute-done.2.refs_2_ = bf16[8,32,256]{2,1,0:T(8,128)(2,1)S(1)} collective-permute-done((bf16[8,32,256]{2,1,0:T(8,128)(2,1)S(1)}, bf16[8,32,256]{2,1,0:T(8,128)(2,1)S(1)}, u32[]{:S(2)}, u32[]{:S(2)}) %collective-permute-start.2) | collective-permute-done | bytes 131104 | tf_op jit(solution)/shard_map/ppermute | solution.py:360
  17.4 0.7 collective-permute-done.3.refs_3_
  18.2 5.3 %collective-permute-start.6 = (bf16[8,32,256]{2,1,0:T(8,128)(2,1)S(1)}, bf16[8,32,256]{2,1,0:T(8,128)(2,1)S(1)}, u32[]{:S(2)}, u32[]{:S(2)}) collective-permute-start(bf16[8,32,256]{2,1,0:T(8,128)(2,1)S(1)} %join.1.refs_0_), channel_id=1, source_target_pairs={{0,192},{64,0},{128,64},{192,128},{1,193},{65,1},{129,65},{193,129... | collective-permute-start | bytes 393224 | tf_op jit(solution)/shard_map/ppermute | solution.py:360
  23.5 1.0 collective-permute-start.5
  24.5 2.3 %collective-permute-start.4 = (bf16[8,32,256]{2,1,0:T(8,128)(2,1)S(1)}, bf16[8,32,256]{2,1,0:T(8,128)(2,1)S(1)}, u32[]{:S(2)}, u32[]{:S(2)}) collective-permute-start(bf16[8,32,256]{2,1,0:T(8,128)(2,1)S(1)} %join.1.refs_0_), channel_id=1, source_target_pairs={{0,64},{64,128},{128,192},{192,0},{1,65},{65,129},{129,193},{193,1... | collective-permute-start | bytes 393224 | tf_op jit(solution)/shard_map/ppermute | solution.py:360
  26.8 1.3 %tables.1 = (f32[8,32,256]{2,1,0:T(8,128)S(1)}, bf16[512,512]{1,0:T(8,128)(2,1)S(1)}, bf16[256,256]{1,0:T(8,128)(2,1)S(1)}, bf16[4,256,256]{2,1,0:T(8,128)(2,1)S(1)}) custom-call(s32[3]{0:T(128)S(1)} %pad_add_fusion.here_ref, f32[8,64]{1,0:T(8,128)S(1)} %copy-done.4, s32[32,256]{1,0:T(8,128)S(1)} %copy-done.2, bf16[64,64]{1,0:T(8,128)(2,1)S(1)} %copy-done.3, ...), custom_call_target="tpu_custom_call" | custom-call | flops 600000000 | bytes 2000000 | tf_op jit(solution)/shard_map/tables/pallas_call | solution.py:171
  28.2 6.2 %collective-permute-done.5.refs_2_ = bf16[8,32,256]{2,1,0:T(8,128)(2,1)S(1)} collective-permute-done((bf16[8,32,256]{2,1,0:T(8,128)(2,1)S(1)}, bf16[8,32,256]{2,1,0:T(8,128)(2,1)S(1)}, u32[]{:S(2)}, u32[]{:S(2)}) %collective-permute-start.5) | collective-permute-done | bytes 131104 | tf_op jit(solution)/shard_map/ppermute | solution.py:360
  34.4 1.9 %collective-permute-start.9 = (bf16[8,32,256]{2,1,0:T(8,128)(2,1)S(1)}, bf16[8,32,256]{2,1,0:T(8,128)(2,1)S(1)}, u32[]{:S(2)}, u32[]{:S(2)}) collective-permute-start(bf16[8,32,256]{2,1,0:T(8,128)(2,1)S(1)} %weigh.1.refs_0_), channel_id=1, source_target_pairs={{0,48},{16,0},{32,16},{48,32},{1,49},{17,1},{33,17},{49,33},{2,50}... | collective-permute-start | bytes 393224 | tf_op jit(solution)/shard_map/ppermute | solution.py:360
  36.4 0.9 collective-permute-start.8
  37.3 3.9 %collective-permute-start.10 = (bf16[8,32,256]{2,1,0:T(8,128)(2,1)S(1)}, bf16[8,32,256]{2,1,0:T(8,128)(2,1)S(1)}, u32[]{:S(2)}, u32[]{:S(2)}) collective-permute-start(bf16[8,32,256]{2,1,0:T(8,128)(2,1)S(1)} %weigh.1.refs_0_), channel_id=1, source_target_pairs={{0,8},{8,0},{1,9},{9,1},{2,10},{10,2},{3,11},{11,3},{4,12},{12,4},... | collective-permute-start | bytes 393224 | tf_op jit(solution)/shard_map/ppermute | solution.py:382
  41.2 3.0 %collective-permute-start.13 = (bf16[8,32,256]{2,1,0:T(8,128)(2,1)S(1)}, bf16[8,32,256]{2,1,0:T(8,128)(2,1)S(1)}, u32[]{:S(2)}, u32[]{:S(2)}) collective-permute-start(bf16[8,32,256]{2,1,0:T(8,128)(2,1)S(1)} %collective-permute-done.9.refs_3_), channel_id=1, source_target_pairs={{0,8},{8,0},{1,9},{9,1},{2,10},{10,2},{3,11},{11,3},{4,12},{12,4},... | collective-permute-start | bytes 393224 | tf_op jit(solution)/shard_map/ppermute | solution.py:382
  44.2 2.6 %collective-permute-start.12 = (bf16[8,32,256]{2,1,0:T(8,128)(2,1)S(1)}, bf16[8,32,256]{2,1,0:T(8,128)(2,1)S(1)}, u32[]{:S(2)}, u32[]{:S(2)}) collective-permute-start(bf16[8,32,256]{2,1,0:T(8,128)(2,1)S(1)} %collective-permute-done.8.refs_2_), channel_id=1, source_target_pairs={{0,8},{8,0},{1,9},{9,1},{2,10},{10,2},{3,11},{11,3},{4,12},{12,4},... | collective-permute-start | bytes 393224 | tf_op jit(solution)/shard_map/ppermute | solution.py:382
  46.8 1.3 %collective-permute-start.11 = (bf16[8,32,256]{2,1,0:T(8,128)(2,1)S(1)}, bf16[8,32,256]{2,1,0:T(8,128)(2,1)S(1)}, u32[]{:S(2)}, u32[]{:S(2)}) collective-permute-start(bf16[8,32,256]{2,1,0:T(8,128)(2,1)S(1)} %collective-permute-done.7.refs_1_), channel_id=1, source_target_pairs={{0,8},{8,0},{1,9},{9,1},{2,10},{10,2},{3,11},{11,3},{4,12},{12,4},... | collective-permute-start | bytes 393224 | tf_op jit(solution)/shard_map/ppermute | solution.py:382
  48.2 1.0 collective-permute-done.11.refs_5_
  49.1 1.1 spread_out.5
  50.2 1.0 collective-permute-start.28
  51.2 2.4 %collective-permute-start.29 = (bf16[1,32,2048]{2,1,0:T(8,128)(2,1)S(1)}, bf16[1,32,2048]{2,1,0:T(8,128)(2,1)S(1)}, u32[]{:S(2)}, u32[]{:S(2)}) collective-permute-start(bf16[1,32,2048]{2,1,0:T(8,128)(2,1)S(1)} %get-tuple-element.69), channel_id=1, source_target_pairs={{0,2},{1,3},{2,4},{3,5},{4,6},{5,7},{6,0},{7,1},{8,10},{9,11},{10,... | collective-permute-start | bytes 393224 | tf_op jit(solution)/shard_map/ppermute | solution.py:360
  53.7 3.4 %collective-permute-start.30 = (bf16[1,32,2048]{2,1,0:T(8,128)(2,1)S(1)}, bf16[1,32,2048]{2,1,0:T(8,128)(2,1)S(1)}, u32[]{:S(2)}, u32[]{:S(2)}) collective-permute-start(bf16[1,32,2048]{2,1,0:T(8,128)(2,1)S(1)} %get-tuple-element.70), channel_id=1, source_target_pairs={{0,3},{1,4},{2,5},{3,6},{4,7},{5,0},{6,1},{7,2},{8,11},{9,12},{10,... | collective-permute-start | bytes 393224 | tf_op jit(solution)/shard_map/ppermute | solution.py:360
  57.1 1.5 %collective-permute-start.32 = (bf16[1,32,2048]{2,1,0:T(8,128)(2,1)S(1)}, bf16[1,32,2048]{2,1,0:T(8,128)(2,1)S(1)}, u32[]{:S(2)}, u32[]{:S(2)}) collective-permute-start(bf16[1,32,2048]{2,1,0:T(8,128)(2,1)S(1)} %get-tuple-element.72), channel_id=1, source_target_pairs={{0,5},{1,6},{2,7},{3,0},{4,1},{5,2},{6,3},{7,4},{8,13},{9,14},{10,... | collective-permute-start | bytes 393224 | tf_op jit(solution)/shard_map/ppermute | solution.py:360
  58.5 2.2 %spread_out.4 = (bf16[2,32,2048]{2,1,0:T(8,128)(2,1)S(1)}, bf16[2,32,2048]{2,1,0:T(8,128)(2,1)S(1)}, bf16[2,32,2048]{2,1,0:T(8,128)(2,1)S(1)}, bf16[2,32,2048]{2...) custom-call(bf16[8,32,256]{2,1,0:T(8,128)(2,1)S(1)} %weigh.1.refs_0_, ...), custom_call_target="tpu_custom_call" | custom-call | flops 3000000000 | bytes 5000000 | tf_op jit(solution)/shard_map/spread_out/pallas_call | solution.py:272
  60.8 1.5 %collective-permute-start.33 = (bf16[1,32,2048]{2,1,0:T(8,128)(2,1)S(1)}, bf16[1,32,2048]{2,1,0:T(8,128)(2,1)S(1)}, u32[]{:S(2)}, u32[]{:S(2)}) collective-permute-start(bf16[1,32,2048]{2,1,0:T(8,128)(2,1)S(1)} %get-tuple-element.73), channel_id=1, source_target_pairs={{0,6},{1,7},{2,0},{3,1},{4,2},{5,3},{6,4},{7,5},{8,14},{9,15},{10,... | collective-permute-start | bytes 393224 | tf_op jit(solution)/shard_map/ppermute | solution.py:360
  62.3 1.5 %collective-permute-start.21 = (bf16[2,32,2048]{2,1,0:T(8,128)(2,1)S(1)}, bf16[2,32,2048]{2,1,0:T(8,128)(2,1)S(1)}, u32[]{:S(2)}, u32[]{:S(2)}) collective-permute-start(bf16[2,32,2048]{2,1,0:T(8,128)(2,1)S(1)} %get-tuple-element.60), channel_id=1, source_target_pairs={{0,1},{1,2},{2,3},{3,4},{4,5},{5,6},{6,7},{7,0},{8,9},{9,10},{10,1... | collective-permute-start | bytes 786440 | tf_op jit(solution)/shard_map/ppermute | solution.py:360
  63.8 2.5 %collective-permute-start.22 = (bf16[2,32,2048]{2,1,0:T(8,128)(2,1)S(1)}, bf16[2,32,2048]{2,1,0:T(8,128)(2,1)S(1)}, u32[]{:S(2)}, u32[]{:S(2)}) collective-permute-start(bf16[2,32,2048]{2,1,0:T(8,128)(2,1)S(1)} %get-tuple-element.61), channel_id=1, source_target_pairs={{0,2},{1,3},{2,4},{3,5},{4,6},{5,7},{6,0},{7,1},{8,10},{9,11},{10,... | collective-permute-start | bytes 786440 | tf_op jit(solution)/shard_map/ppermute | solution.py:360
  66.3 1.1 spread_out.3
  67.4 0.9 collective-permute-start.34
  69.0 1.1 collective-permute-start.15
  70.1 7.9 %collective-permute-done.34.refs_7_ = bf16[1,32,2048]{2,1,0:T(8,128)(2,1)S(1)} collective-permute-done((bf16[1,32,2048]{2,1,0:T(8,128)(2,1)S(1)}, bf16[1,32,2048]{2,1,0:T(8,128)(2,1)S(1)}, u32[]{:S(2)}, u32[]{:S(2)}) %collective-permute-start.34) | collective-permute-done | bytes 131104 | tf_op jit(solution)/shard_map/ppermute | solution.py:360
  78.0 3.7 %collective-permute-done.14.refs_1_ = bf16[1,32,2048]{2,1,0:T(8,128)(2,1)S(1)} collective-permute-done((bf16[1,32,2048]{2,1,0:T(8,128)(2,1)S(1)}, bf16[1,32,2048]{2,1,0:T(8,128)(2,1)S(1)}, u32[]{:S(2)}, u32[]{:S(2)}) %collective-permute-start.14) | collective-permute-done | bytes 131104 | tf_op jit(solution)/shard_map/ppermute | solution.py:360
  81.7 3.5 %collective-permute-start.24 = (bf16[2,32,2048]{2,1,0:T(8,128)(2,1)S(1)}, bf16[2,32,2048]{2,1,0:T(8,128)(2,1)S(1)}, u32[]{:S(2)}, u32[]{:S(2)}) collective-permute-start(bf16[2,32,2048]{2,1,0:T(8,128)(2,1)S(1)} %get-tuple-element.63), channel_id=1, source_target_pairs={{0,4},{1,5},{2,6},{3,7},{4,0},{5,1},{6,2},{7,3},{8,12},{9,13},{10,... | collective-permute-start | bytes 786440 | tf_op jit(solution)/shard_map/ppermute | solution.py:360
  85.2 3.1 %collective-permute-start.25 = (bf16[2,32,2048]{2,1,0:T(8,128)(2,1)S(1)}, bf16[2,32,2048]{2,1,0:T(8,128)(2,1)S(1)}, u32[]{:S(2)}, u32[]{:S(2)}) collective-permute-start(bf16[2,32,2048]{2,1,0:T(8,128)(2,1)S(1)} %get-tuple-element.64), channel_id=1, source_target_pairs={{0,5},{1,6},{2,7},{3,0},{4,1},{5,2},{6,3},{7,4},{8,13},{9,14},{10,... | collective-permute-start | bytes 786440 | tf_op jit(solution)/shard_map/ppermute | solution.py:360
  88.3 2.9 %collective-permute-start.26 = (bf16[2,32,2048]{2,1,0:T(8,128)(2,1)S(1)}, bf16[2,32,2048]{2,1,0:T(8,128)(2,1)S(1)}, u32[]{:S(2)}, u32[]{:S(2)}) collective-permute-start(bf16[2,32,2048]{2,1,0:T(8,128)(2,1)S(1)} %get-tuple-element.65), channel_id=1, source_target_pairs={{0,6},{1,7},{2,0},{3,1},{4,2},{5,3},{6,4},{7,5},{8,14},{9,15},{10,... | collective-permute-start | bytes 786440 | tf_op jit(solution)/shard_map/ppermute | solution.py:360
  91.2 1.9 %finish.3.refs_9_ = bf16[4,64,32,256]{3,2,1,0:T(8,128)(2,1)} custom-call(s32[3]{0:T(128)S(1)} %pad_add_fusion.here_ref, bf16[1,32,2048]{2,1,0:T(8,128)(2,1)S(1)} %get-tuple-element.67.refs_0_, bf16[1,32,2048]{2,1,0:T(8,128)(2,1)S(1)} %collective-permute-done.28.refs_1_, bf16[1,32,2048]{2,1,0:T(8,128)(2,1)S(1)} %collective-permute-done.29.refs_2_, ...), custom_call_target="tpu_custom_call" | custom-call | flops 700000000 | bytes 2500000 | tf_op jit(solution)/shard_map/finish/pallas_call | solution.py:338
  93.2 0.9 collective-permute-start.16
  94.8 2.6 %collective-permute-done.25.refs_5_ = bf16[2,32,2048]{2,1,0:T(8,128)(2,1)S(1)} collective-permute-done((bf16[2,32,2048]{2,1,0:T(8,128)(2,1)S(1)}, bf16[2,32,2048]{2,1,0:T(8,128)(2,1)S(1)}, u32[]{:S(2)}, u32[]{:S(2)}) %collective-permute-start.25) | collective-permute-done | bytes 262176 | tf_op jit(solution)/shard_map/ppermute | solution.py:360
  97.6 2.5 %collective-permute-done.26.refs_6_ = bf16[2,32,2048]{2,1,0:T(8,128)(2,1)S(1)} collective-permute-done((bf16[2,32,2048]{2,1,0:T(8,128)(2,1)S(1)}, bf16[2,32,2048]{2,1,0:T(8,128)(2,1)S(1)}, u32[]{:S(2)}, u32[]{:S(2)}) %collective-permute-start.26) | collective-permute-done | bytes 262176 | tf_op jit(solution)/shard_map/ppermute | solution.py:360
  100.1 4.6 %collective-permute-start.19 = (bf16[1,32,2048]{2,1,0:T(8,128)(2,1)S(1)}, bf16[1,32,2048]{2,1,0:T(8,128)(2,1)S(1)}, u32[]{:S(2)}, u32[]{:S(2)}) collective-permute-start(bf16[1,32,2048]{2,1,0:T(8,128)(2,1)S(1)} %get-tuple-element.56), channel_id=1, source_target_pairs={{0,6},{1,7},{2,0},{3,1},{4,2},{5,3},{6,4},{7,5},{8,14},{9,15},{10,... | collective-permute-start | bytes 393224 | tf_op jit(solution)/shard_map/ppermute | solution.py:360
  104.7 1.0 collective-permute-done.27.refs_7_
  105.7 4.3 %collective-permute-start.20 = (bf16[1,32,2048]{2,1,0:T(8,128)(2,1)S(1)}, bf16[1,32,2048]{2,1,0:T(8,128)(2,1)S(1)}, u32[]{:S(2)}, u32[]{:S(2)}) collective-permute-start(bf16[1,32,2048]{2,1,0:T(8,128)(2,1)S(1)} %get-tuple-element.57), channel_id=1, source_target_pairs={{0,7},{1,0},{2,1},{3,2},{4,3},{5,4},{6,5},{7,6},{8,15},{9,8},{10,9... | collective-permute-start | bytes 393224 | tf_op jit(solution)/shard_map/ppermute | solution.py:360
  110.0 2.4 %finish.4.refs_9_ = bf16[4,64,32,256]{3,2,1,0:T(8,128)(2,1)} custom-call(s32[3]{0:T(128)S(1)} %pad_add_fusion.here_ref, bf16[2,32,2048]{2,1,0:T(8,128)(2,1)S(1)} %get-tuple-element.59.refs_0_, bf16[2,32,2048]{2,1,0:T(8,128)(2,1)S(1)} %collective-permute-done.21.refs_1_, ...), custom_call_target="tpu_custom_call", output_to_operand_aliasing={{}: (10, {})} | custom-call | flops 1400000000 | bytes 5000000 | tf_op jit(solution)/shard_map/finish/pallas_call | solution.py:338
  112.4 1.7 %collective-permute-done.19.refs_6_ = bf16[1,32,2048]{2,1,0:T(8,128)(2,1)S(1)} collective-permute-done((bf16[1,32,2048]{2,1,0:T(8,128)(2,1)S(1)}, bf16[1,32,2048]{2,1,0:T(8,128)(2,1)S(1)}, u32[]{:S(2)}, u32[]{:S(2)}) %collective-permute-start.19) | collective-permute-done | bytes 131104 | tf_op jit(solution)/shard_map/ppermute | solution.py:360
  114.1 2.8 %collective-permute-done.20.refs_7_ = bf16[1,32,2048]{2,1,0:T(8,128)(2,1)S(1)} collective-permute-done((bf16[1,32,2048]{2,1,0:T(8,128)(2,1)S(1)}, bf16[1,32,2048]{2,1,0:T(8,128)(2,1)S(1)}, u32[]{:S(2)}, u32[]{:S(2)}) %collective-permute-start.20) | collective-permute-done | bytes 131104 | tf_op jit(solution)/shard_map/ppermute | solution.py:360
  116.9 1.9 %finish.5 = bf16[4,64,32,256]{3,2,1,0:T(8,128)(2,1)} custom-call(s32[3]{0:T(128)S(1)} %pad_add_fusion.here_ref, bf16[1,32,2048]{2,1,0:T(8,128)(2,1)S(1)} %get-tuple-element.50.refs_0_, bf16[1,32,2048]{2,1,0:T(8,128)(2,1)S(1)} %collective-permute-done.14.refs_1_, ...), custom_call_target="tpu_custom_call", output_to_operand_aliasing={{}: (10, {})} | custom-call | flops 700000000 | bytes 2500000 | tf_op jit(solution)/shard_map/finish/pallas_call | solution.py:338
  (45 shorter events, 2.1 us)
Async XLA Ops:
  4.1 4.8 %collective-permute-start = (bf16[4,8,32,256]{3,2,1,0:T(8,128)(2,1)S(1)}, bf16[4,8,32,256]{3,2,1,0:T(8,128)(2,1)S(1)}, u32[]{:S(2)}, u32[]{:S(2)}) collective-permute-start(bf16[4,8,32,256]{3,2,1,0:T(8,128)(2,1)S(1)} %get-tuple-element.43), channel_id=1, source_target_pairs={{0,8},{8,0},{1,9},{9,1},{2,10},{10,2},{3,11},{11,3},{4,12},{12,4},... | collective-permute-start | bytes 1572872 | tf_op jit(solution)/shard_map/ppermute | solution.py:374
  7.4 19.4 %copy-start = (bf16[256,256]{1,0:T(8,128)(2,1)S(1)}, bf16[256,256]{1,0:T(8,128)(2,1)}, u32[]{:S(2)}) copy-start(bf16[256,256]{1,0:T(8,128)(2,1)} %lon_ref.1) | copy-start | bytes 393220
  7.4 19.4 %copy-start.1 = (bf16[256,256]{1,0:T(8,128)(2,1)S(1)}, bf16[256,256]{1,0:T(8,128)(2,1)}, u32[]{:S(2)}) copy-start(bf16[256,256]{1,0:T(8,128)(2,1)} %lat_ref.1) | copy-start | bytes 393220
  7.4 19.4 %copy-start.2 = (s32[32,256]{1,0:T(8,128)S(1)}, s32[32,256]{1,0:T(8,128)}, u32[]{:S(2)}) copy-start(s32[32,256]{1,0:T(8,128)} %classes_ref.1) | copy-start | bytes 98308
  7.4 19.4 %copy-start.3 = (bf16[64,64]{1,0:T(8,128)(2,1)S(1)}, bf16[64,64]{1,0:T(8,128)(2,1)}, u32[]{:S(2)}) copy-start(bf16[64,64]{1,0:T(8,128)(2,1)} %vert_ref.1) | copy-start | bytes 24580
  7.4 19.4 %copy-start.4 = (f32[8,64]{1,0:T(8,128)S(1)}, f32[8,64]{1,0:T(8,128)}, u32[]{:S(2)}) copy-start(f32[8,64]{1,0:T(8,128)} %table_ref.1) | copy-start | bytes 6148
  9.1 6.4 %collective-permute-start.1 = (bf16[8,32,256]{2,1,0:T(8,128)(2,1)S(1)}, bf16[8,32,256]{2,1,0:T(8,128)(2,1)S(1)}, u32[]{:S(2)}, u32[]{:S(2)}) collective-permute-start(bf16[8,32,256]{2,1,0:T(8,128)(2,1)S(1)} %get-tuple-element.45), channel_id=1, source_target_pairs={{0,16},{16,32},{32,48},{48,0},{1,17},{17,33},{33,49},{49,1},{2,18}... | collective-permute-start | bytes 393224 | tf_op jit(solution)/shard_map/ppermute | solution.py:360
  9.2 8.3 %collective-permute-start.2 = (bf16[8,32,256]{2,1,0:T(8,128)(2,1)S(1)}, bf16[8,32,256]{2,1,0:T(8,128)(2,1)S(1)}, u32[]{:S(2)}, u32[]{:S(2)}) collective-permute-start(bf16[8,32,256]{2,1,0:T(8,128)(2,1)S(1)} %get-tuple-element.46), channel_id=1, source_target_pairs={{0,32},{16,48},{32,0},{48,16},{1,33},{17,49},{33,1},{49,17},{2,34}... | collective-permute-start | bytes 393224 | tf_op jit(solution)/shard_map/ppermute | solution.py:360
  11.3 6.8 %collective-permute-start.3 = (bf16[8,32,256]{2,1,0:T(8,128)(2,1)S(1)}, bf16[8,32,256]{2,1,0:T(8,128)(2,1)S(1)}, u32[]{:S(2)}, u32[]{:S(2)}) collective-permute-start(bf16[8,32,256]{2,1,0:T(8,128)(2,1)S(1)} %get-tuple-element.47), channel_id=1, source_target_pairs={{0,48},{16,0},{32,16},{48,32},{1,49},{17,1},{33,17},{49,33},{2,50}... | collective-permute-start | bytes 393224 | tf_op jit(solution)/shard_map/ppermute | solution.py:360
  18.2 10.0 %collective-permute-start.6 = (bf16[8,32,256]{2,1,0:T(8,128)(2,1)S(1)}, bf16[8,32,256]{2,1,0:T(8,128)(2,1)S(1)}, u32[]{:S(2)}, u32[]{:S(2)}) collective-permute-start(bf16[8,32,256]{2,1,0:T(8,128)(2,1)S(1)} %join.1.refs_0_), channel_id=1, source_target_pairs={{0,192},{64,0},{128,64},{192,128},{1,193},{65,1},{129,65},{193,129... | collective-permute-start | bytes 393224 | tf_op jit(solution)/shard_map/ppermute | solution.py:360
  23.5 10.8 %collective-permute-start.5 = (bf16[8,32,256]{2,1,0:T(8,128)(2,1)S(1)}, bf16[8,32,256]{2,1,0:T(8,128)(2,1)S(1)}, u32[]{:S(2)}, u32[]{:S(2)}) collective-permute-start(bf16[8,32,256]{2,1,0:T(8,128)(2,1)S(1)} %join.1.refs_0_), channel_id=1, source_target_pairs={{0,128},{64,192},{128,0},{192,64},{1,129},{65,193},{129,1},{193,65... | collective-permute-start | bytes 393224 | tf_op jit(solution)/shard_map/ppermute | solution.py:360
  24.5 9.8 %collective-permute-start.4 = (bf16[8,32,256]{2,1,0:T(8,128)(2,1)S(1)}, bf16[8,32,256]{2,1,0:T(8,128)(2,1)S(1)}, u32[]{:S(2)}, u32[]{:S(2)}) collective-permute-start(bf16[8,32,256]{2,1,0:T(8,128)(2,1)S(1)} %join.1.refs_0_), channel_id=1, source_target_pairs={{0,64},{64,128},{128,192},{192,0},{1,65},{65,129},{129,193},{193,1... | collective-permute-start | bytes 393224 | tf_op jit(solution)/shard_map/ppermute | solution.py:360
  34.4 6.8 %collective-permute-start.9 = (bf16[8,32,256]{2,1,0:T(8,128)(2,1)S(1)}, bf16[8,32,256]{2,1,0:T(8,128)(2,1)S(1)}, u32[]{:S(2)}, u32[]{:S(2)}) collective-permute-start(bf16[8,32,256]{2,1,0:T(8,128)(2,1)S(1)} %weigh.1.refs_0_), channel_id=1, source_target_pairs={{0,48},{16,0},{32,16},{48,32},{1,49},{17,1},{33,17},{49,33},{2,50}... | collective-permute-start | bytes 393224 | tf_op jit(solution)/shard_map/ppermute | solution.py:360
  36.4 7.8 %collective-permute-start.8 = (bf16[8,32,256]{2,1,0:T(8,128)(2,1)S(1)}, bf16[8,32,256]{2,1,0:T(8,128)(2,1)S(1)}, u32[]{:S(2)}, u32[]{:S(2)}) collective-permute-start(bf16[8,32,256]{2,1,0:T(8,128)(2,1)S(1)} %weigh.1.refs_0_), channel_id=1, source_target_pairs={{0,32},{16,48},{32,0},{48,16},{1,33},{17,49},{33,1},{49,17},{2,34}... | collective-permute-start | bytes 393224 | tf_op jit(solution)/shard_map/ppermute | solution.py:360
  37.3 9.5 %collective-permute-start.7 = (bf16[8,32,256]{2,1,0:T(8,128)(2,1)S(1)}, bf16[8,32,256]{2,1,0:T(8,128)(2,1)S(1)}, u32[]{:S(2)}, u32[]{:S(2)}) collective-permute-start(bf16[8,32,256]{2,1,0:T(8,128)(2,1)S(1)} %weigh.1.refs_0_), channel_id=1, source_target_pairs={{0,16},{16,32},{32,48},{48,0},{1,17},{17,33},{33,49},{49,1},{2,18}... | collective-permute-start | bytes 393224 | tf_op jit(solution)/shard_map/ppermute | solution.py:360
  37.3 10.8 %collective-permute-start.10 = (bf16[8,32,256]{2,1,0:T(8,128)(2,1)S(1)}, bf16[8,32,256]{2,1,0:T(8,128)(2,1)S(1)}, u32[]{:S(2)}, u32[]{:S(2)}) collective-permute-start(bf16[8,32,256]{2,1,0:T(8,128)(2,1)S(1)} %weigh.1.refs_0_), channel_id=1, source_target_pairs={{0,8},{8,0},{1,9},{9,1},{2,10},{10,2},{3,11},{11,3},{4,12},{12,4},... | collective-permute-start | bytes 393224 | tf_op jit(solution)/shard_map/ppermute | solution.py:382
  41.2 6.9 %collective-permute-start.13 = (bf16[8,32,256]{2,1,0:T(8,128)(2,1)S(1)}, bf16[8,32,256]{2,1,0:T(8,128)(2,1)S(1)}, u32[]{:S(2)}, u32[]{:S(2)}) collective-permute-start(bf16[8,32,256]{2,1,0:T(8,128)(2,1)S(1)} %collective-permute-done.9.refs_3_), channel_id=1, source_target_pairs={{0,8},{8,0},{1,9},{9,1},{2,10},{10,2},{3,11},{11,3},{4,12},{12,4},... | collective-permute-start | bytes 393224 | tf_op jit(solution)/shard_map/ppermute | solution.py:382
  44.2 4.0 %collective-permute-start.12 = (bf16[8,32,256]{2,1,0:T(8,128)(2,1)S(1)}, bf16[8,32,256]{2,1,0:T(8,128)(2,1)S(1)}, u32[]{:S(2)}, u32[]{:S(2)}) collective-permute-start(bf16[8,32,256]{2,1,0:T(8,128)(2,1)S(1)} %collective-permute-done.8.refs_2_), channel_id=1, source_target_pairs={{0,8},{8,0},{1,9},{9,1},{2,10},{10,2},{3,11},{11,3},{4,12},{12,4},... | collective-permute-start | bytes 393224 | tf_op jit(solution)/shard_map/ppermute | solution.py:382
  46.8 2.3 %collective-permute-start.11 = (bf16[8,32,256]{2,1,0:T(8,128)(2,1)S(1)}, bf16[8,32,256]{2,1,0:T(8,128)(2,1)S(1)}, u32[]{:S(2)}, u32[]{:S(2)}) collective-permute-start(bf16[8,32,256]{2,1,0:T(8,128)(2,1)S(1)} %collective-permute-done.7.refs_1_), channel_id=1, source_target_pairs={{0,8},{8,0},{1,9},{9,1},{2,10},{10,2},{3,11},{11,3},{4,12},{12,4},... | collective-permute-start | bytes 393224 | tf_op jit(solution)/shard_map/ppermute | solution.py:382
  50.2 10.5 %collective-permute-start.28 = (bf16[1,32,2048]{2,1,0:T(8,128)(2,1)S(1)}, bf16[1,32,2048]{2,1,0:T(8,128)(2,1)S(1)}, u32[]{:S(2)}, u32[]{:S(2)}) collective-permute-start(bf16[1,32,2048]{2,1,0:T(8,128)(2,1)S(1)} %get-tuple-element.68), channel_id=1, source_target_pairs={{0,1},{1,2},{2,3},{3,4},{4,5},{5,6},{6,7},{7,0},{8,9},{9,10},{10,1... | collective-permute-start | bytes 393224 | tf_op jit(solution)/shard_map/ppermute | solution.py:360
  51.2 11.0 %collective-permute-start.29 = (bf16[1,32,2048]{2,1,0:T(8,128)(2,1)S(1)}, bf16[1,32,2048]{2,1,0:T(8,128)(2,1)S(1)}, u32[]{:S(2)}, u32[]{:S(2)}) collective-permute-start(bf16[1,32,2048]{2,1,0:T(8,128)(2,1)S(1)} %get-tuple-element.69), channel_id=1, source_target_pairs={{0,2},{1,3},{2,4},{3,5},{4,6},{5,7},{6,0},{7,1},{8,10},{9,11},{10,... | collective-permute-start | bytes 393224 | tf_op jit(solution)/shard_map/ppermute | solution.py:360
  53.7 10.1 %collective-permute-start.30 = (bf16[1,32,2048]{2,1,0:T(8,128)(2,1)S(1)}, bf16[1,32,2048]{2,1,0:T(8,128)(2,1)S(1)}, u32[]{:S(2)}, u32[]{:S(2)}) collective-permute-start(bf16[1,32,2048]{2,1,0:T(8,128)(2,1)S(1)} %get-tuple-element.70), channel_id=1, source_target_pairs={{0,3},{1,4},{2,5},{3,6},{4,7},{5,0},{6,1},{7,2},{8,11},{9,12},{10,... | collective-permute-start | bytes 393224 | tf_op jit(solution)/shard_map/ppermute | solution.py:360
  57.1 10.4 %collective-permute-start.31 = (bf16[1,32,2048]{2,1,0:T(8,128)(2,1)S(1)}, bf16[1,32,2048]{2,1,0:T(8,128)(2,1)S(1)}, u32[]{:S(2)}, u32[]{:S(2)}) collective-permute-start(bf16[1,32,2048]{2,1,0:T(8,128)(2,1)S(1)} %get-tuple-element.71), channel_id=1, source_target_pairs={{0,4},{1,5},{2,6},{3,7},{4,0},{5,1},{6,2},{7,3},{8,12},{9,13},{10,... | collective-permute-start | bytes 393224 | tf_op jit(solution)/shard_map/ppermute | solution.py:360
  57.1 11.3 %collective-permute-start.32 = (bf16[1,32,2048]{2,1,0:T(8,128)(2,1)S(1)}, bf16[1,32,2048]{2,1,0:T(8,128)(2,1)S(1)}, u32[]{:S(2)}, u32[]{:S(2)}) collective-permute-start(bf16[1,32,2048]{2,1,0:T(8,128)(2,1)S(1)} %get-tuple-element.72), channel_id=1, source_target_pairs={{0,5},{1,6},{2,7},{3,0},{4,1},{5,2},{6,3},{7,4},{8,13},{9,14},{10,... | collective-permute-start | bytes 393224 | tf_op jit(solution)/shard_map/ppermute | solution.py:360
  60.8 8.2 %collective-permute-start.33 = (bf16[1,32,2048]{2,1,0:T(8,128)(2,1)S(1)}, bf16[1,32,2048]{2,1,0:T(8,128)(2,1)S(1)}, u32[]{:S(2)}, u32[]{:S(2)}) collective-permute-start(bf16[1,32,2048]{2,1,0:T(8,128)(2,1)S(1)} %get-tuple-element.73), channel_id=1, source_target_pairs={{0,6},{1,7},{2,0},{3,1},{4,2},{5,3},{6,4},{7,5},{8,14},{9,15},{10,... | collective-permute-start | bytes 393224 | tf_op jit(solution)/shard_map/ppermute | solution.py:360
  62.3 26.1 %collective-permute-start.21 = (bf16[2,32,2048]{2,1,0:T(8,128)(2,1)S(1)}, bf16[2,32,2048]{2,1,0:T(8,128)(2,1)S(1)}, u32[]{:S(2)}, u32[]{:S(2)}) collective-permute-start(bf16[2,32,2048]{2,1,0:T(8,128)(2,1)S(1)} %get-tuple-element.60), channel_id=1, source_target_pairs={{0,1},{1,2},{2,3},{3,4},{4,5},{5,6},{6,7},{7,0},{8,9},{9,10},{10,1... | collective-permute-start | bytes 786440 | tf_op jit(solution)/shard_map/ppermute | solution.py:360
  63.8 27.4 %collective-permute-start.22 = (bf16[2,32,2048]{2,1,0:T(8,128)(2,1)S(1)}, bf16[2,32,2048]{2,1,0:T(8,128)(2,1)S(1)}, u32[]{:S(2)}, u32[]{:S(2)}) collective-permute-start(bf16[2,32,2048]{2,1,0:T(8,128)(2,1)S(1)} %get-tuple-element.61), channel_id=1, source_target_pairs={{0,2},{1,3},{2,4},{3,5},{4,6},{5,7},{6,0},{7,1},{8,10},{9,11},{10,... | collective-permute-start | bytes 786440 | tf_op jit(solution)/shard_map/ppermute | solution.py:360
  67.4 10.6 %collective-permute-start.34 = (bf16[1,32,2048]{2,1,0:T(8,128)(2,1)S(1)}, bf16[1,32,2048]{2,1,0:T(8,128)(2,1)S(1)}, u32[]{:S(2)}, u32[]{:S(2)}) collective-permute-start(bf16[1,32,2048]{2,1,0:T(8,128)(2,1)S(1)} %get-tuple-element.74), channel_id=1, source_target_pairs={{0,7},{1,0},{2,1},{3,2},{4,3},{5,4},{6,5},{7,6},{8,15},{9,8},{10,9... | collective-permute-start | bytes 393224 | tf_op jit(solution)/shard_map/ppermute | solution.py:360
  68.3 13.4 %collective-permute-start.14 = (bf16[1,32,2048]{2,1,0:T(8,128)(2,1)S(1)}, bf16[1,32,2048]{2,1,0:T(8,128)(2,1)S(1)}, u32[]{:S(2)}, u32[]{:S(2)}) collective-permute-start(bf16[1,32,2048]{2,1,0:T(8,128)(2,1)S(1)} %get-tuple-element.51), channel_id=1, source_target_pairs={{0,1},{1,2},{2,3},{3,4},{4,5},{5,6},{6,7},{7,0},{8,9},{9,10},{10,1... | collective-permute-start | bytes 393224 | tf_op jit(solution)/shard_map/ppermute | solution.py:360
  69.0 16.3 %collective-permute-start.15 = (bf16[1,32,2048]{2,1,0:T(8,128)(2,1)S(1)}, bf16[1,32,2048]{2,1,0:T(8,128)(2,1)S(1)}, u32[]{:S(2)}, u32[]{:S(2)}) collective-permute-start(bf16[1,32,2048]{2,1,0:T(8,128)(2,1)S(1)} %get-tuple-element.52), channel_id=1, source_target_pairs={{0,2},{1,3},{2,4},{3,5},{4,6},{5,7},{6,0},{7,1},{8,10},{9,11},{10,... | collective-permute-start | bytes 393224 | tf_op jit(solution)/shard_map/ppermute | solution.py:360
  78.0 15.2 %collective-permute-start.23 = (bf16[2,32,2048]{2,1,0:T(8,128)(2,1)S(1)}, bf16[2,32,2048]{2,1,0:T(8,128)(2,1)S(1)}, u32[]{:S(2)}, u32[]{:S(2)}) collective-permute-start(bf16[2,32,2048]{2,1,0:T(8,128)(2,1)S(1)} %get-tuple-element.62), channel_id=1, source_target_pairs={{0,3},{1,4},{2,5},{3,6},{4,7},{5,0},{6,1},{7,2},{8,11},{9,12},{10,... | collective-permute-start | bytes 786440 | tf_op jit(solution)/shard_map/ppermute | solution.py:360
  81.7 12.4 %collective-permute-start.24 = (bf16[2,32,2048]{2,1,0:T(8,128)(2,1)S(1)}, bf16[2,32,2048]{2,1,0:T(8,128)(2,1)S(1)}, u32[]{:S(2)}, u32[]{:S(2)}) collective-permute-start(bf16[2,32,2048]{2,1,0:T(8,128)(2,1)S(1)} %get-tuple-element.63), channel_id=1, source_target_pairs={{0,4},{1,5},{2,6},{3,7},{4,0},{5,1},{6,2},{7,3},{8,12},{9,13},{10,... | collective-permute-start | bytes 786440 | tf_op jit(solution)/shard_map/ppermute | solution.py:360
  85.2 12.2 %collective-permute-start.25 = (bf16[2,32,2048]{2,1,0:T(8,128)(2,1)S(1)}, bf16[2,32,2048]{2,1,0:T(8,128)(2,1)S(1)}, u32[]{:S(2)}, u32[]{:S(2)}) collective-permute-start(bf16[2,32,2048]{2,1,0:T(8,128)(2,1)S(1)} %get-tuple-element.64), channel_id=1, source_target_pairs={{0,5},{1,6},{2,7},{3,0},{4,1},{5,2},{6,3},{7,4},{8,13},{9,14},{10,... | collective-permute-start | bytes 786440 | tf_op jit(solution)/shard_map/ppermute | solution.py:360
  88.3 11.7 %collective-permute-start.26 = (bf16[2,32,2048]{2,1,0:T(8,128)(2,1)S(1)}, bf16[2,32,2048]{2,1,0:T(8,128)(2,1)S(1)}, u32[]{:S(2)}, u32[]{:S(2)}) collective-permute-start(bf16[2,32,2048]{2,1,0:T(8,128)(2,1)S(1)} %get-tuple-element.65), channel_id=1, source_target_pairs={{0,6},{1,7},{2,0},{3,1},{4,2},{5,3},{6,4},{7,5},{8,14},{9,15},{10,... | collective-permute-start | bytes 786440 | tf_op jit(solution)/shard_map/ppermute | solution.py:360
  91.2 14.5 %collective-permute-start.27 = (bf16[2,32,2048]{2,1,0:T(8,128)(2,1)S(1)}, bf16[2,32,2048]{2,1,0:T(8,128)(2,1)S(1)}, u32[]{:S(2)}, u32[]{:S(2)}) collective-permute-start(bf16[2,32,2048]{2,1,0:T(8,128)(2,1)S(1)} %get-tuple-element.66), channel_id=1, source_target_pairs={{0,7},{1,0},{2,1},{3,2},{4,3},{5,4},{6,5},{7,6},{8,15},{9,8},{10,9... | collective-permute-start | bytes 786440 | tf_op jit(solution)/shard_map/ppermute | solution.py:360
  93.2 19.3 %collective-permute-start.16 = (bf16[1,32,2048]{2,1,0:T(8,128)(2,1)S(1)}, bf16[1,32,2048]{2,1,0:T(8,128)(2,1)S(1)}, u32[]{:S(2)}, u32[]{:S(2)}) collective-permute-start(bf16[1,32,2048]{2,1,0:T(8,128)(2,1)S(1)} %get-tuple-element.53), channel_id=1, source_target_pairs={{0,3},{1,4},{2,5},{3,6},{4,7},{5,0},{6,1},{7,2},{8,11},{9,12},{10,... | collective-permute-start | bytes 393224 | tf_op jit(solution)/shard_map/ppermute | solution.py:360
  94.1 18.3 %collective-permute-start.17 = (bf16[1,32,2048]{2,1,0:T(8,128)(2,1)S(1)}, bf16[1,32,2048]{2,1,0:T(8,128)(2,1)S(1)}, u32[]{:S(2)}, u32[]{:S(2)}) collective-permute-start(bf16[1,32,2048]{2,1,0:T(8,128)(2,1)S(1)} %get-tuple-element.54), channel_id=1, source_target_pairs={{0,4},{1,5},{2,6},{3,7},{4,0},{5,1},{6,2},{7,3},{8,12},{9,13},{10,... | collective-permute-start | bytes 393224 | tf_op jit(solution)/shard_map/ppermute | solution.py:360
  97.4 15.0 %collective-permute-start.18 = (bf16[1,32,2048]{2,1,0:T(8,128)(2,1)S(1)}, bf16[1,32,2048]{2,1,0:T(8,128)(2,1)S(1)}, u32[]{:S(2)}, u32[]{:S(2)}) collective-permute-start(bf16[1,32,2048]{2,1,0:T(8,128)(2,1)S(1)} %get-tuple-element.55), channel_id=1, source_target_pairs={{0,5},{1,6},{2,7},{3,0},{4,1},{5,2},{6,3},{7,4},{8,13},{9,14},{10,... | collective-permute-start | bytes 393224 | tf_op jit(solution)/shard_map/ppermute | solution.py:360
  100.1 14.0 %collective-permute-start.19 = (bf16[1,32,2048]{2,1,0:T(8,128)(2,1)S(1)}, bf16[1,32,2048]{2,1,0:T(8,128)(2,1)S(1)}, u32[]{:S(2)}, u32[]{:S(2)}) collective-permute-start(bf16[1,32,2048]{2,1,0:T(8,128)(2,1)S(1)} %get-tuple-element.56), channel_id=1, source_target_pairs={{0,6},{1,7},{2,0},{3,1},{4,2},{5,3},{6,4},{7,5},{8,14},{9,15},{10,... | collective-permute-start | bytes 393224 | tf_op jit(solution)/shard_map/ppermute | solution.py:360
  105.7 11.2 %collective-permute-start.20 = (bf16[1,32,2048]{2,1,0:T(8,128)(2,1)S(1)}, bf16[1,32,2048]{2,1,0:T(8,128)(2,1)S(1)}, u32[]{:S(2)}, u32[]{:S(2)}) collective-permute-start(bf16[1,32,2048]{2,1,0:T(8,128)(2,1)S(1)} %get-tuple-element.57), channel_id=1, source_target_pairs={{0,7},{1,0},{2,1},{3,2},{4,3},{5,4},{6,5},{7,6},{8,15},{9,8},{10,9... | collective-permute-start | bytes 393224 | tf_op jit(solution)/shard_map/ppermute | solution.py:360

commit v4 on v3

--- a/solution.py
+++ b/solution.py
@@ -16,7 +16,7 @@
 LAT = "lat"
 EACH = 4
 Z_ORDER = (2, 1, 3)
-GROUPS = ((0, 1), (1, 2), (3, 1))
+GROUPS = ((0, 2), (2, 2))
 ORDER = (6, 4, 2, 5, 7, 1, 3)
 
 
@@ -283,74 +283,60 @@
     )(*args)
 
 
-def finish_kernel(first, here_ref, *refs):
-    parts, turned_ref = refs[:LATS], refs[LATS]
-    out_ref, done, sems = refs[-3:]
-    count, share, _ = parts[0].shape
-    levels = done.shape[1]
-    groups = levels // EACH // 2
+def finish_kernel(here_ref, *refs):
+    parts = refs[:LATS]
+    turned_ref, out_ref = refs[LATS], refs[-1]
+    share = parts[0].shape[1]
+    groups = parts[0].shape[2] // 128
     lane = lax.broadcasted_iota(jnp.int32, (share, 128), 1) >> 5
     at = [lane == q for q in range(3)]
-    copies = []
-    for k in range(count):
-        for h in range(2):
-            for turn in range(EACH):
-                lines = []
-                for g in range(h * groups, h * groups + groups):
-                    sides = []
-                    for part in range(2):
-                        tiles = [
-                            parts[EACH * part + (turn - q) % EACH][k, :, 128 * g : 128 * g + 128]
-                            for q in range(EACH)
-                        ]
-                        side = tiles[3]
-                        for q in range(3):
-                            side = jnp.where(at[q], tiles[q], side)
-                        sides.append(side)
-                    lines.append(jnp.concatenate(sides, axis=1))
-                x = jnp.concatenate(lines, axis=0)
-                y = nt_dot(x, turned_ref[turn]).astype(BF16)
-                level = (turn + 8 - here_ref[2]) & 3
-                for g in range(groups):
-                    done[k, EACH * (h * groups + g) + level] = y[share * g : share * g + share]
-            half = pl.ds(h * (levels // 2), levels // 2)
-            copy = pltpu.make_async_copy(
-                done.at[k, half], out_ref.at[first + k, half], sems.at[k, h]
-            )
-            copy.start()
-            copies.append(copy)
-    for copy in copies:
-        copy.wait()
+    for turn in range(EACH):
+        lines = []
+        for g in range(groups):
+            sides = []
+            for part in range(2):
+                tiles = [
+                    parts[EACH * part + (turn - q) % EACH][0, :, 128 * g : 128 * g + 128]
+                    for q in range(EACH)
+                ]
+                side = tiles[3]
+                for q in range(3):
+                    side = jnp.where(at[q], tiles[q], side)
+                sides.append(side)
+            lines.append(jnp.concatenate(sides, axis=1))
+        x = jnp.concatenate(lines, axis=0)
+        y = nt_dot(x, turned_ref[turn]).astype(BF16)
+        level = (turn + 8 - here_ref[2]) & 3
+        for g in range(groups):
+            out_ref[0, EACH * g + level] = y[share * g : share * g + share]
 
 
 def finish(here, parts, turned, first, members, so_far=None):
     count, share, wide = parts[0].shape
     size = turned.shape[1]
     levels = wide // 32
-    args = (here, *parts, turned)
-    smem, vmem = (pl.BlockSpec(memory_space=space) for space in (pltpu.SMEM, pltpu.VMEM))
-    hbm = pl.BlockSpec(memory_space=pltpu.HBM)
-    in_specs = [smem] + [vmem] * (LATS + 1)
-    aliases = {}
-    if so_far is not None:
-        aliases = {len(args): 0}
-        args, in_specs = (*args, so_far), in_specs + [hbm]
-    return pl.pallas_call(
-        functools.partial(finish_kernel, first),
-        in_specs=in_specs,
-        out_specs=hbm,
+    args = (*parts, turned) if so_far is None else (*parts, turned, so_far)
+    extra = [] if so_far is None else [pl.BlockSpec(memory_space=pl.ANY)]
+    return pl.pallas_call(
+        finish_kernel,
+        grid_spec=pltpu.PrefetchScalarGridSpec(
+            num_scalar_prefetch=1,
+            grid=(count,),
+            in_specs=[pl.BlockSpec((1, share, wide), lambda k, s: (k, 0, 0))] * LATS
+            + [pl.BlockSpec(turned.shape, lambda k, s: (0, 0, 0))]
+            + extra,
+            out_specs=pl.BlockSpec((1, levels, share, size), lambda k, s: (first + k, 0, 0, 0)),
+        ),
         out_shape=jax.ShapeDtypeStruct((members, levels, share, size), BF16),
-        input_output_aliases=aliases,
-        scratch_shapes=[
-            pltpu.VMEM((count, levels, share, size), BF16),
-            pltpu.SemaphoreType.DMA((count, 2)),
-        ],
-        compiler_params=pltpu.CompilerParams(vmem_limit_bytes=16 * 1024 * 1024),
+        input_output_aliases={} if so_far is None else {len(args): 0},
+        compiler_params=pltpu.CompilerParams(
+            dimension_semantics=("arbitrary",), vmem_limit_bytes=16 * 1024 * 1024
+        ),
         cost_estimate=pl.CostEstimate(
             flops=count * 700_000_000, bytes_accessed=count * 2_500_000, transcendentals=0
         ),
         name="finish",
-    )(*args)
+    )(here, *args)
 
 
 def passed_on(axis, pieces, order):

time: 121 us -> 124 us (1.025); the launches traced: 119 us -> 123 us
  starting transfers between devices: 65.7 us -> 77.3 us
  waiting for transfers between devices: 36.5 us -> 30.6 us
    ppermute x30 -> x23, starting transfers between devices: 51.6 us -> 63.2 us  [passed_on(): lax.ppermute(pieces[d], axis, [(i, (i + d) % count) for i in range(count)])]
    ppermute x30 -> x23, waiting for transfers between devices: 34.2 us -> 28.3 us  [passed_on(): lax.ppermute(pieces[d], axis, [(i, (i + d) % count) for i in range(count)])]
    pallas_call x3 -> x2, Pallas kernels: 6.18 us -> 5.04 us  [finish(): pl.pallas_call(finish_kernel, grid_spec=pltpu.PrefetchScalarGridSpec(num_...]
    pallas_call x3 -> x2, Pallas kernels: 4.38 us -> 4.4 us  [spread_out(): pl.pallas_call(functools.partial(spread_out_kernel, first), in_specs=[vme...]
  transfers between devices with their start and end apart: 35 -> 28, of which waited for: 13 -> 11; matrix products, arithmetic and copies ran while one was open for 0% -> 0% of each run, Pallas kernels for 8% -> 5%
where the time goes in v4:
time: 124 us; the launch traced here: 123 us
  starting transfers between devices  77.3 us (62%)
  waiting for transfers between devices  30.6 us (25%)
  Pallas kernels  15.3 us (12%)
    ppermute x23, starting transfers between devices, passed_on(): lax.ppermute(pieces[d], axis, [(i, (i + d) % count) for i in range(count)])  63.2 us
    ppermute x23, waiting for transfers between devices, passed_on(): lax.ppermute(pieces[d], axis, [(i, (i + d) % count) for i in range(count)])  28.3 us
    ppermute x4, starting transfers between devices, local(): weights.append(lax.ppermute(x, 'core', swap))  10.8 us
    pallas_call x2, Pallas kernels, finish(): pl.pallas_call(finish_kernel, grid_spec=pltpu.PrefetchScalarGridSpec(num_...  5.04 us
    pallas_call x2, Pallas kernels, spread_out(): pl.pallas_call(functools.partial(spread_out_kernel, first), in_specs=[vme...  4.4 us
    pallas_call x1, Pallas kernels, other_half(): pl.pallas_call(other_half_kernel, in_specs=[smem, hbm, hbm], out_specs=[v...  4.06 us
    ppermute x1, starting transfers between devices, local(): arrived = lax.ppermute(send, 'core', swap)  3.29 us
  transfers between devices with their start and end apart: 28, of which 11 were waited for; matrix products, arithmetic and copies ran while one was open for 0% of the time, Pallas kernels for 5%

profile of v4, /device:TPU:1, one launch (start us, length us, event | category | flops | bytes accessed | tf_op | source)
XLA Modules:
  0.0 123.4 jit_solution(7844582282004604368)
XLA Ops:
  0.0 0.1 pad_add_fusion.here_ref
  0.1 4.1 %other_half.1 = (bf16[4,8,32,256]{3,2,1,0:T(8,128)(2,1)S(1)}, bf16[2,4,4,8,32,256]{5,4,3,2,1,0:T(8,128)(2,1)S(1)}, bf16[4,4,8,32,256]{4,3,2,1,0:T(8,128)(2,1)S(1)}) custom-call(s32[3]{0:T(128)S(1)} %pad_add_fusion.here_ref, bf16[4,64,32,256]{3,2,1,0:T(8,128)(2,1)} %spread_ref.1, bf16[4,64,32,256]{3,2,1,0:T(8,128)(2,1)} %controls_ref.1), custom_call_target="tpu_custom_call" | custom-call | tf_op jit(solution)/shard_map/other_half/pallas_call | solution.py:66
  4.1 3.3 %collective-permute-start = (bf16[4,8,32,256]{3,2,1,0:T(8,128)(2,1)S(1)}, bf16[4,8,32,256]{3,2,1,0:T(8,128)(2,1)S(1)}, u32[]{:S(2)}, u32[]{:S(2)}) collective-permute-start(bf16[4,8,32,256]{3,2,1,0:T(8,128)(2,1)S(1)} %get-tuple-element.35), channel_id=1, source_target_pairs={{0,8},{8,0},{1,9},{9,1},{2,10},{10,2},{3,11},{11,3},{4,12},{12,4},... | collective-permute-start | bytes 1572872 | tf_op jit(solution)/shard_map/ppermute | solution.py:360
  7.4 0.0 copy-start.4
  7.5 0.2 own_half.1.keep_ref
  7.7 1.3 %collective-permute-done.arrived_ref = bf16[4,8,32,256]{3,2,1,0:T(8,128)(2,1)S(1)} collective-permute-done((bf16[4,8,32,256]{3,2,1,0:T(8,128)(2,1)S(1)}, bf16[4,8,32,256]{3,2,1,0:T(8,128)(2,1)S(1)}, u32[]{:S(2)}, u32[]{:S(2)}) %collective-permute-start) | collective-permute-done | bytes 524320 | tf_op jit(solution)/shard_map/ppermute | solution.py:360
  9.0 0.1 chip_sum.1
  9.1 0.1 collective-permute-start.1
  9.2 2.2 %collective-permute-start.2 = (bf16[8,32,256]{2,1,0:T(8,128)(2,1)S(1)}, bf16[8,32,256]{2,1,0:T(8,128)(2,1)S(1)}, u32[]{:S(2)}, u32[]{:S(2)}) collective-permute-start(bf16[8,32,256]{2,1,0:T(8,128)(2,1)S(1)} %get-tuple-element.38), channel_id=1, source_target_pairs={{0,32},{16,48},{32,0},{48,16},{1,33},{17,49},{33,1},{49,17},{2,34}... | collective-permute-start | bytes 393224 | tf_op jit(solution)/shard_map/ppermute | solution.py:346
  11.3 1.1 collective-permute-start.3
  12.4 3.1 %collective-permute-done.1.refs_1_ = bf16[8,32,256]{2,1,0:T(8,128)(2,1)S(1)} collective-permute-done((bf16[8,32,256]{2,1,0:T(8,128)(2,1)S(1)}, bf16[8,32,256]{2,1,0:T(8,128)(2,1)S(1)}, u32[]{:S(2)}, u32[]{:S(2)}) %collective-permute-start.1) | collective-permute-done | bytes 131104 | tf_op jit(solution)/shard_map/ppermute | solution.py:346
  15.5 1.9 %collective-permute-done.2.refs_2_ = bf16[8,32,256]{2,1,0:T(8,128)(2,1)S(1)} collective-permute-done((bf16[8,32,256]{2,1,0:T(8,128)(2,1)S(1)}, bf16[8,32,256]{2,1,0:T(8,128)(2,1)S(1)}, u32[]{:S(2)}, u32[]{:S(2)}) %collective-permute-start.2) | collective-permute-done | bytes 131104 | tf_op jit(solution)/shard_map/ppermute | solution.py:346
  17.4 0.7 collective-permute-done.3.refs_3_
  18.1 0.1 join.1.refs_0_
  18.2 5.3 %collective-permute-start.6 = (bf16[8,32,256]{2,1,0:T(8,128)(2,1)S(1)}, bf16[8,32,256]{2,1,0:T(8,128)(2,1)S(1)}, u32[]{:S(2)}, u32[]{:S(2)}) collective-permute-start(bf16[8,32,256]{2,1,0:T(8,128)(2,1)S(1)} %join.1.refs_0_), channel_id=1, source_target_pairs={{0,192},{64,0},{128,64},{192,128},{1,193},{65,1},{129,65},{193,129... | collective-permute-start | bytes 393224 | tf_op jit(solution)/shard_map/ppermute | solution.py:346
  23.5 1.0 collective-permute-start.5
  24.5 2.3 %collective-permute-start.4 = (bf16[8,32,256]{2,1,0:T(8,128)(2,1)S(1)}, bf16[8,32,256]{2,1,0:T(8,128)(2,1)S(1)}, u32[]{:S(2)}, u32[]{:S(2)}) collective-permute-start(bf16[8,32,256]{2,1,0:T(8,128)(2,1)S(1)} %join.1.refs_0_), channel_id=1, source_target_pairs={{0,64},{64,128},{128,192},{192,0},{1,65},{65,129},{129,193},{193,1... | collective-permute-start | bytes 393224 | tf_op jit(solution)/shard_map/ppermute | solution.py:346
  26.8 1.3 %tables.1 = (f32[8,32,256]{2,1,0:T(8,128)S(1)}, bf16[512,512]{1,0:T(8,128)(2,1)S(1)}, bf16[256,256]{1,0:T(8,128)(2,1)S(1)}, bf16[4,256,256]{2,1,0:T(8,128)(2,1)S(1)}) custom-call(s32[3]{0:T(128)S(1)} %pad_add_fusion.here_ref, f32[8,64]{1,0:T(8,128)S(1)} %copy-done.4, s32[32,256]{1,0:T(8,128)S(1)} %copy-done.2, bf16[64,64]{1,0:T(8,128)(2,1)S(1)} %copy-done.3, ...), custom_call_target="tpu_custom_call" | custom-call | flops 600000000 | bytes 2000000 | tf_op jit(solution)/shard_map/tables/pallas_call | solution.py:171
  28.2 6.2 %collective-permute-done.5.refs_2_ = bf16[8,32,256]{2,1,0:T(8,128)(2,1)S(1)} collective-permute-done((bf16[8,32,256]{2,1,0:T(8,128)(2,1)S(1)}, bf16[8,32,256]{2,1,0:T(8,128)(2,1)S(1)}, u32[]{:S(2)}, u32[]{:S(2)}) %collective-permute-start.5) | collective-permute-done | bytes 131104 | tf_op jit(solution)/shard_map/ppermute | solution.py:346
  34.4 0.1 weigh.1.refs_0_
  34.5 1.9 %collective-permute-start.9 = (bf16[8,32,256]{2,1,0:T(8,128)(2,1)S(1)}, bf16[8,32,256]{2,1,0:T(8,128)(2,1)S(1)}, u32[]{:S(2)}, u32[]{:S(2)}) collective-permute-start(bf16[8,32,256]{2,1,0:T(8,128)(2,1)S(1)} %weigh.1.refs_0_), channel_id=1, source_target_pairs={{0,48},{16,0},{32,16},{48,32},{1,49},{17,1},{33,17},{49,33},{2,50}... | collective-permute-start | bytes 393224 | tf_op jit(solution)/shard_map/ppermute | solution.py:346
  36.4 0.9 collective-permute-start.8
  37.4 3.9 %collective-permute-start.10 = (bf16[8,32,256]{2,1,0:T(8,128)(2,1)S(1)}, bf16[8,32,256]{2,1,0:T(8,128)(2,1)S(1)}, u32[]{:S(2)}, u32[]{:S(2)}) collective-permute-start(bf16[8,32,256]{2,1,0:T(8,128)(2,1)S(1)} %weigh.1.refs_0_), channel_id=1, source_target_pairs={{0,8},{8,0},{1,9},{9,1},{2,10},{10,2},{3,11},{11,3},{4,12},{12,4},... | collective-permute-start | bytes 393224 | tf_op jit(solution)/shard_map/ppermute | solution.py:368
  41.2 3.0 %collective-permute-start.13 = (bf16[8,32,256]{2,1,0:T(8,128)(2,1)S(1)}, bf16[8,32,256]{2,1,0:T(8,128)(2,1)S(1)}, u32[]{:S(2)}, u32[]{:S(2)}) collective-permute-start(bf16[8,32,256]{2,1,0:T(8,128)(2,1)S(1)} %collective-permute-done.9.refs_3_), channel_id=1, source_target_pairs={{0,8},{8,0},{1,9},{9,1},{2,10},{10,2},{3,11},{11,3},{4,12},{12,4},... | collective-permute-start | bytes 393224 | tf_op jit(solution)/shard_map/ppermute | solution.py:368
  44.2 2.6 %collective-permute-start.12 = (bf16[8,32,256]{2,1,0:T(8,128)(2,1)S(1)}, bf16[8,32,256]{2,1,0:T(8,128)(2,1)S(1)}, u32[]{:S(2)}, u32[]{:S(2)}) collective-permute-start(bf16[8,32,256]{2,1,0:T(8,128)(2,1)S(1)} %collective-permute-done.8.refs_2_), channel_id=1, source_target_pairs={{0,8},{8,0},{1,9},{9,1},{2,10},{10,2},{3,11},{11,3},{4,12},{12,4},... | collective-permute-start | bytes 393224 | tf_op jit(solution)/shard_map/ppermute | solution.py:368
  46.8 1.3 %collective-permute-start.11 = (bf16[8,32,256]{2,1,0:T(8,128)(2,1)S(1)}, bf16[8,32,256]{2,1,0:T(8,128)(2,1)S(1)}, u32[]{:S(2)}, u32[]{:S(2)}) collective-permute-start(bf16[8,32,256]{2,1,0:T(8,128)(2,1)S(1)} %collective-permute-done.7.refs_1_), channel_id=1, source_target_pairs={{0,8},{8,0},{1,9},{9,1},{2,10},{10,2},{3,11},{11,3},{4,12},{12,4},... | collective-permute-start | bytes 393224 | tf_op jit(solution)/shard_map/ppermute | solution.py:368
  48.2 1.0 collective-permute-done.11.refs_5_
  49.1 2.2 %spread_out.3 = (bf16[2,32,2048]{2,1,0:T(8,128)(2,1)S(1)}, bf16[2,32,2048]{2,1,0:T(8,128)(2,1)S(1)}, bf16[2,32,2048]{2,1,0:T(8,128)(2,1)S(1)}, bf16[2,32,2048]{2...) custom-call(bf16[8,32,256]{2,1,0:T(8,128)(2,1)S(1)} %weigh.1.refs_0_, ...), custom_call_target="tpu_custom_call" | custom-call | flops 3000000000 | bytes 5000000 | tf_op jit(solution)/shard_map/spread_out/pallas_call | solution.py:272
  51.3 1.0 collective-permute-start.21
  52.3 2.5 %collective-permute-start.22 = (bf16[2,32,2048]{2,1,0:T(8,128)(2,1)S(1)}, bf16[2,32,2048]{2,1,0:T(8,128)(2,1)S(1)}, u32[]{:S(2)}, u32[]{:S(2)}) collective-permute-start(bf16[2,32,2048]{2,1,0:T(8,128)(2,1)S(1)} %get-tuple-element.53), channel_id=1, source_target_pairs={{0,2},{1,3},{2,4},{3,5},{4,6},{5,7},{6,0},{7,1},{8,10},{9,11},{10,... | collective-permute-start | bytes 786440 | tf_op jit(solution)/shard_map/ppermute | solution.py:346
  54.8 3.4 %collective-permute-start.23 = (bf16[2,32,2048]{2,1,0:T(8,128)(2,1)S(1)}, bf16[2,32,2048]{2,1,0:T(8,128)(2,1)S(1)}, u32[]{:S(2)}, u32[]{:S(2)}) collective-permute-start(bf16[2,32,2048]{2,1,0:T(8,128)(2,1)S(1)} %get-tuple-element.54), channel_id=1, source_target_pairs={{0,3},{1,4},{2,5},{3,6},{4,7},{5,0},{6,1},{7,2},{8,11},{9,12},{10,... | collective-permute-start | bytes 786440 | tf_op jit(solution)/shard_map/ppermute | solution.py:346
  58.2 1.5 %collective-permute-start.25 = (bf16[2,32,2048]{2,1,0:T(8,128)(2,1)S(1)}, bf16[2,32,2048]{2,1,0:T(8,128)(2,1)S(1)}, u32[]{:S(2)}, u32[]{:S(2)}) collective-permute-start(bf16[2,32,2048]{2,1,0:T(8,128)(2,1)S(1)} %get-tuple-element.56), channel_id=1, source_target_pairs={{0,5},{1,6},{2,7},{3,0},{4,1},{5,2},{6,3},{7,4},{8,13},{9,14},{10,... | collective-permute-start | bytes 786440 | tf_op jit(solution)/shard_map/ppermute | solution.py:346
  59.7 2.2 %spread_out.2 = (bf16[2,32,2048]{2,1,0:T(8,128)(2,1)S(1)}, bf16[2,32,2048]{2,1,0:T(8,128)(2,1)S(1)}, bf16[2,32,2048]{2,1,0:T(8,128)(2,1)S(1)}, bf16[2,32,2048]{2...) custom-call(bf16[8,32,256]{2,1,0:T(8,128)(2,1)S(1)} %weigh.1.refs_0_, ...), custom_call_target="tpu_custom_call" | custom-call | flops 3000000000 | bytes 5000000 | tf_op jit(solution)/shard_map/spread_out/pallas_call | solution.py:272
  61.9 4.6 %collective-permute-done.21.refs_1_ = bf16[2,32,2048]{2,1,0:T(8,128)(2,1)S(1)} collective-permute-done((bf16[2,32,2048]{2,1,0:T(8,128)(2,1)S(1)}, bf16[2,32,2048]{2,1,0:T(8,128)(2,1)S(1)}, u32[]{:S(2)}, u32[]{:S(2)}) %collective-permute-start.21) | collective-permute-done | bytes 262176 | tf_op jit(solution)/shard_map/ppermute | solution.py:346
  66.5 0.0 collective-permute-start.26
  66.6 0.4 collective-permute-done.22.refs_2_
  66.9 6.4 %collective-permute-start.27 = (bf16[2,32,2048]{2,1,0:T(8,128)(2,1)S(1)}, bf16[2,32,2048]{2,1,0:T(8,128)(2,1)S(1)}, u32[]{:S(2)}, u32[]{:S(2)}) collective-permute-start(bf16[2,32,2048]{2,1,0:T(8,128)(2,1)S(1)} %get-tuple-element.58), channel_id=1, source_target_pairs={{0,7},{1,0},{2,1},{3,2},{4,3},{5,4},{6,5},{7,6},{8,15},{9,8},{10,9... | collective-permute-start | bytes 786440 | tf_op jit(solution)/shard_map/ppermute | solution.py:346
  73.3 2.7 %collective-permute-start.14 = (bf16[2,32,2048]{2,1,0:T(8,128)(2,1)S(1)}, bf16[2,32,2048]{2,1,0:T(8,128)(2,1)S(1)}, u32[]{:S(2)}, u32[]{:S(2)}) collective-permute-start(bf16[2,32,2048]{2,1,0:T(8,128)(2,1)S(1)} %get-tuple-element.43), channel_id=1, source_target_pairs={{0,1},{1,2},{2,3},{3,4},{4,5},{5,6},{6,7},{7,0},{8,9},{9,10},{10,1... | collective-permute-start | bytes 786440 | tf_op jit(solution)/shard_map/ppermute | solution.py:346
  76.0 5.6 %collective-permute-start.15 = (bf16[2,32,2048]{2,1,0:T(8,128)(2,1)S(1)}, bf16[2,32,2048]{2,1,0:T(8,128)(2,1)S(1)}, u32[]{:S(2)}, u32[]{:S(2)}) collective-permute-start(bf16[2,32,2048]{2,1,0:T(8,128)(2,1)S(1)} %get-tuple-element.44), channel_id=1, source_target_pairs={{0,2},{1,3},{2,4},{3,5},{4,6},{5,7},{6,0},{7,1},{8,10},{9,11},{10,... | collective-permute-start | bytes 786440 | tf_op jit(solution)/shard_map/ppermute | solution.py:346
  81.6 4.9 %collective-permute-start.16 = (bf16[2,32,2048]{2,1,0:T(8,128)(2,1)S(1)}, bf16[2,32,2048]{2,1,0:T(8,128)(2,1)S(1)}, u32[]{:S(2)}, u32[]{:S(2)}) collective-permute-start(bf16[2,32,2048]{2,1,0:T(8,128)(2,1)S(1)} %get-tuple-element.45), channel_id=1, source_target_pairs={{0,3},{1,4},{2,5},{3,6},{4,7},{5,0},{6,1},{7,2},{8,11},{9,12},{10,... | collective-permute-start | bytes 786440 | tf_op jit(solution)/shard_map/ppermute | solution.py:346
  86.5 0.8 collective-permute-start.17
  87.3 17.2 %collective-permute-start.18 = (bf16[2,32,2048]{2,1,0:T(8,128)(2,1)S(1)}, bf16[2,32,2048]{2,1,0:T(8,128)(2,1)S(1)}, u32[]{:S(2)}, u32[]{:S(2)}) collective-permute-start(bf16[2,32,2048]{2,1,0:T(8,128)(2,1)S(1)} %get-tuple-element.47), channel_id=1, source_target_pairs={{0,5},{1,6},{2,7},{3,0},{4,1},{5,2},{6,3},{7,4},{8,13},{9,14},{10,... | collective-permute-start | bytes 786440 | tf_op jit(solution)/shard_map/ppermute | solution.py:346
  104.6 2.4 %collective-permute-start.20 = (bf16[2,32,2048]{2,1,0:T(8,128)(2,1)S(1)}, bf16[2,32,2048]{2,1,0:T(8,128)(2,1)S(1)}, u32[]{:S(2)}, u32[]{:S(2)}) collective-permute-start(bf16[2,32,2048]{2,1,0:T(8,128)(2,1)S(1)} %get-tuple-element.49), channel_id=1, source_target_pairs={{0,7},{1,0},{2,1},{3,2},{4,3},{5,4},{6,5},{7,6},{8,15},{9,8},{10,9... | collective-permute-start | bytes 786440 | tf_op jit(solution)/shard_map/ppermute | solution.py:346
  107.0 2.5 %finish.2.refs_9_ = bf16[4,64,32,256]{3,2,1,0:T(8,128)(2,1)} custom-call(s32[3]{0:T(128)S(1)} %pad_add_fusion.here_ref, bf16[2,32,2048]{2,1,0:T(8,128)(2,1)S(1)} %get-tuple-element.51.refs_0_, bf16[2,32,2048]{2,1,0:T(8,128)(2,1)S(1)} %collective-permute-done.21.refs_1_, bf16[2,32,2048]{2,1,0:T(8,128)(2,1)S(1)} %collective-permute-done.22.refs_2_, ...), custom_call_target="tpu_custom_call" | custom-call | flops 1400000000 | bytes 5000000 | tf_op jit(solution)/shard_map/finish/pallas_call | solution.py:320
  109.5 0.1 collective-permute-done.18.refs_5_
  109.6 6.8 %collective-permute-done.19.refs_6_ = bf16[2,32,2048]{2,1,0:T(8,128)(2,1)S(1)} collective-permute-done((bf16[2,32,2048]{2,1,0:T(8,128)(2,1)S(1)}, bf16[2,32,2048]{2,1,0:T(8,128)(2,1)S(1)}, u32[]{:S(2)}, u32[]{:S(2)}) %collective-permute-start.19) | collective-permute-done | bytes 262176 | tf_op jit(solution)/shard_map/ppermute | solution.py:346
  116.4 4.5 %collective-permute-done.20.refs_7_ = bf16[2,32,2048]{2,1,0:T(8,128)(2,1)S(1)} collective-permute-done((bf16[2,32,2048]{2,1,0:T(8,128)(2,1)S(1)}, bf16[2,32,2048]{2,1,0:T(8,128)(2,1)S(1)}, u32[]{:S(2)}, u32[]{:S(2)}) %collective-permute-start.20) | collective-permute-done | bytes 262176 | tf_op jit(solution)/shard_map/ppermute | solution.py:346
  120.9 2.5 %finish.3 = bf16[4,64,32,256]{3,2,1,0:T(8,128)(2,1)} custom-call(s32[3]{0:T(128)S(1)} %pad_add_fusion.here_ref, bf16[2,32,2048]{2,1,0:T(8,128)(2,1)S(1)} %get-tuple-element.42.refs_0_, bf16[2,32,2048]{2,1,0:T(8,128)(2,1)S(1)} %collective-permute-done.14.refs_1_, ...), custom_call_target="tpu_custom_call", output_to_operand_aliasing={{}: (10, {})} | custom-call | flops 1400000000 | bytes 5000000 | tf_op jit(solution)/shard_map/finish/pallas_call | solution.py:320
  (29 shorter events, 0.1 us)
Async XLA Ops:
  4.1 4.8 %collective-permute-start = (bf16[4,8,32,256]{3,2,1,0:T(8,128)(2,1)S(1)}, bf16[4,8,32,256]{3,2,1,0:T(8,128)(2,1)S(1)}, u32[]{:S(2)}, u32[]{:S(2)}) collective-permute-start(bf16[4,8,32,256]{3,2,1,0:T(8,128)(2,1)S(1)} %get-tuple-element.35), channel_id=1, source_target_pairs={{0,8},{8,0},{1,9},{9,1},{2,10},{10,2},{3,11},{11,3},{4,12},{12,4},... | collective-permute-start | bytes 1572872 | tf_op jit(solution)/shard_map/ppermute | solution.py:360
  7.4 19.4 %copy-start = (bf16[256,256]{1,0:T(8,128)(2,1)S(1)}, bf16[256,256]{1,0:T(8,128)(2,1)}, u32[]{:S(2)}) copy-start(bf16[256,256]{1,0:T(8,128)(2,1)} %lon_ref.1) | copy-start | bytes 393220
  7.4 19.4 %copy-start.1 = (bf16[256,256]{1,0:T(8,128)(2,1)S(1)}, bf16[256,256]{1,0:T(8,128)(2,1)}, u32[]{:S(2)}) copy-start(bf16[256,256]{1,0:T(8,128)(2,1)} %lat_ref.1) | copy-start | bytes 393220
  7.4 19.4 %copy-start.2 = (s32[32,256]{1,0:T(8,128)S(1)}, s32[32,256]{1,0:T(8,128)}, u32[]{:S(2)}) copy-start(s32[32,256]{1,0:T(8,128)} %classes_ref.1) | copy-start | bytes 98308
  7.4 19.4 %copy-start.3 = (bf16[64,64]{1,0:T(8,128)(2,1)S(1)}, bf16[64,64]{1,0:T(8,128)(2,1)}, u32[]{:S(2)}) copy-start(bf16[64,64]{1,0:T(8,128)(2,1)} %vert_ref.1) | copy-start | bytes 24580
  7.4 19.4 %copy-start.4 = (f32[8,64]{1,0:T(8,128)S(1)}, f32[8,64]{1,0:T(8,128)}, u32[]{:S(2)}) copy-start(f32[8,64]{1,0:T(8,128)} %table_ref.1) | copy-start | bytes 6148
  9.1 6.4 %collective-permute-start.1 = (bf16[8,32,256]{2,1,0:T(8,128)(2,1)S(1)}, bf16[8,32,256]{2,1,0:T(8,128)(2,1)S(1)}, u32[]{:S(2)}, u32[]{:S(2)}) collective-permute-start(bf16[8,32,256]{2,1,0:T(8,128)(2,1)S(1)} %get-tuple-element.37), channel_id=1, source_target_pairs={{0,16},{16,32},{32,48},{48,0},{1,17},{17,33},{33,49},{49,1},{2,18}... | collective-permute-start | bytes 393224 | tf_op jit(solution)/shard_map/ppermute | solution.py:346
  9.2 8.3 %collective-permute-start.2 = (bf16[8,32,256]{2,1,0:T(8,128)(2,1)S(1)}, bf16[8,32,256]{2,1,0:T(8,128)(2,1)S(1)}, u32[]{:S(2)}, u32[]{:S(2)}) collective-permute-start(bf16[8,32,256]{2,1,0:T(8,128)(2,1)S(1)} %get-tuple-element.38), channel_id=1, source_target_pairs={{0,32},{16,48},{32,0},{48,16},{1,33},{17,49},{33,1},{49,17},{2,34}... | collective-permute-start | bytes 393224 | tf_op jit(solution)/shard_map/ppermute | solution.py:346
  11.3 6.8 %collective-permute-start.3 = (bf16[8,32,256]{2,1,0:T(8,128)(2,1)S(1)}, bf16[8,32,256]{2,1,0:T(8,128)(2,1)S(1)}, u32[]{:S(2)}, u32[]{:S(2)}) collective-permute-start(bf16[8,32,256]{2,1,0:T(8,128)(2,1)S(1)} %get-tuple-element.39), channel_id=1, source_target_pairs={{0,48},{16,0},{32,16},{48,32},{1,49},{17,1},{33,17},{49,33},{2,50}... | collective-permute-start | bytes 393224 | tf_op jit(solution)/shard_map/ppermute | solution.py:346
  18.2 10.0 %collective-permute-start.6 = (bf16[8,32,256]{2,1,0:T(8,128)(2,1)S(1)}, bf16[8,32,256]{2,1,0:T(8,128)(2,1)S(1)}, u32[]{:S(2)}, u32[]{:S(2)}) collective-permute-start(bf16[8,32,256]{2,1,0:T(8,128)(2,1)S(1)} %join.1.refs_0_), channel_id=1, source_target_pairs={{0,192},{64,0},{128,64},{192,128},{1,193},{65,1},{129,65},{193,129... | collective-permute-start | bytes 393224 | tf_op jit(solution)/shard_map/ppermute | solution.py:346
  23.5 10.8 %collective-permute-start.5 = (bf16[8,32,256]{2,1,0:T(8,128)(2,1)S(1)}, bf16[8,32,256]{2,1,0:T(8,128)(2,1)S(1)}, u32[]{:S(2)}, u32[]{:S(2)}) collective-permute-start(bf16[8,32,256]{2,1,0:T(8,128)(2,1)S(1)} %join.1.refs_0_), channel_id=1, source_target_pairs={{0,128},{64,192},{128,0},{192,64},{1,129},{65,193},{129,1},{193,65... | collective-permute-start | bytes 393224 | tf_op jit(solution)/shard_map/ppermute | solution.py:346
  24.5 9.8 %collective-permute-start.4 = (bf16[8,32,256]{2,1,0:T(8,128)(2,1)S(1)}, bf16[8,32,256]{2,1,0:T(8,128)(2,1)S(1)}, u32[]{:S(2)}, u32[]{:S(2)}) collective-permute-start(bf16[8,32,256]{2,1,0:T(8,128)(2,1)S(1)} %join.1.refs_0_), channel_id=1, source_target_pairs={{0,64},{64,128},{128,192},{192,0},{1,65},{65,129},{129,193},{193,1... | collective-permute-start | bytes 393224 | tf_op jit(solution)/shard_map/ppermute | solution.py:346
  34.5 6.8 %collective-permute-start.9 = (bf16[8,32,256]{2,1,0:T(8,128)(2,1)S(1)}, bf16[8,32,256]{2,1,0:T(8,128)(2,1)S(1)}, u32[]{:S(2)}, u32[]{:S(2)}) collective-permute-start(bf16[8,32,256]{2,1,0:T(8,128)(2,1)S(1)} %weigh.1.refs_0_), channel_id=1, source_target_pairs={{0,48},{16,0},{32,16},{48,32},{1,49},{17,1},{33,17},{49,33},{2,50}... | collective-permute-start | bytes 393224 | tf_op jit(solution)/shard_map/ppermute | solution.py:346
  36.4 7.8 %collective-permute-start.8 = (bf16[8,32,256]{2,1,0:T(8,128)(2,1)S(1)}, bf16[8,32,256]{2,1,0:T(8,128)(2,1)S(1)}, u32[]{:S(2)}, u32[]{:S(2)}) collective-permute-start(bf16[8,32,256]{2,1,0:T(8,128)(2,1)S(1)} %weigh.1.refs_0_), channel_id=1, source_target_pairs={{0,32},{16,48},{32,0},{48,16},{1,33},{17,49},{33,1},{49,17},{2,34}... | collective-permute-start | bytes 393224 | tf_op jit(solution)/shard_map/ppermute | solution.py:346
  37.3 9.5 %collective-permute-start.7 = (bf16[8,32,256]{2,1,0:T(8,128)(2,1)S(1)}, bf16[8,32,256]{2,1,0:T(8,128)(2,1)S(1)}, u32[]{:S(2)}, u32[]{:S(2)}) collective-permute-start(bf16[8,32,256]{2,1,0:T(8,128)(2,1)S(1)} %weigh.1.refs_0_), channel_id=1, source_target_pairs={{0,16},{16,32},{32,48},{48,0},{1,17},{17,33},{33,49},{49,1},{2,18}... | collective-permute-start | bytes 393224 | tf_op jit(solution)/shard_map/ppermute | solution.py:346
  37.4 10.8 %collective-permute-start.10 = (bf16[8,32,256]{2,1,0:T(8,128)(2,1)S(1)}, bf16[8,32,256]{2,1,0:T(8,128)(2,1)S(1)}, u32[]{:S(2)}, u32[]{:S(2)}) collective-permute-start(bf16[8,32,256]{2,1,0:T(8,128)(2,1)S(1)} %weigh.1.refs_0_), channel_id=1, source_target_pairs={{0,8},{8,0},{1,9},{9,1},{2,10},{10,2},{3,11},{11,3},{4,12},{12,4},... | collective-permute-start | bytes 393224 | tf_op jit(solution)/shard_map/ppermute | solution.py:368
  41.2 6.9 %collective-permute-start.13 = (bf16[8,32,256]{2,1,0:T(8,128)(2,1)S(1)}, bf16[8,32,256]{2,1,0:T(8,128)(2,1)S(1)}, u32[]{:S(2)}, u32[]{:S(2)}) collective-permute-start(bf16[8,32,256]{2,1,0:T(8,128)(2,1)S(1)} %collective-permute-done.9.refs_3_), channel_id=1, source_target_pairs={{0,8},{8,0},{1,9},{9,1},{2,10},{10,2},{3,11},{11,3},{4,12},{12,4},... | collective-permute-start | bytes 393224 | tf_op jit(solution)/shard_map/ppermute | solution.py:368
  44.2 4.0 %collective-permute-start.12 = (bf16[8,32,256]{2,1,0:T(8,128)(2,1)S(1)}, bf16[8,32,256]{2,1,0:T(8,128)(2,1)S(1)}, u32[]{:S(2)}, u32[]{:S(2)}) collective-permute-start(bf16[8,32,256]{2,1,0:T(8,128)(2,1)S(1)} %collective-permute-done.8.refs_2_), channel_id=1, source_target_pairs={{0,8},{8,0},{1,9},{9,1},{2,10},{10,2},{3,11},{11,3},{4,12},{12,4},... | collective-permute-start | bytes 393224 | tf_op jit(solution)/shard_map/ppermute | solution.py:368
  46.8 2.3 %collective-permute-start.11 = (bf16[8,32,256]{2,1,0:T(8,128)(2,1)S(1)}, bf16[8,32,256]{2,1,0:T(8,128)(2,1)S(1)}, u32[]{:S(2)}, u32[]{:S(2)}) collective-permute-start(bf16[8,32,256]{2,1,0:T(8,128)(2,1)S(1)} %collective-permute-done.7.refs_1_), channel_id=1, source_target_pairs={{0,8},{8,0},{1,9},{9,1},{2,10},{10,2},{3,11},{11,3},{4,12},{12,4},... | collective-permute-start | bytes 393224 | tf_op jit(solution)/shard_map/ppermute | solution.py:368
  51.3 15.2 %collective-permute-start.21 = (bf16[2,32,2048]{2,1,0:T(8,128)(2,1)S(1)}, bf16[2,32,2048]{2,1,0:T(8,128)(2,1)S(1)}, u32[]{:S(2)}, u32[]{:S(2)}) collective-permute-start(bf16[2,32,2048]{2,1,0:T(8,128)(2,1)S(1)} %get-tuple-element.52), channel_id=1, source_target_pairs={{0,1},{1,2},{2,3},{3,4},{4,5},{5,6},{6,7},{7,0},{8,9},{9,10},{10,1... | collective-permute-start | bytes 786440 | tf_op jit(solution)/shard_map/ppermute | solution.py:346
  52.3 14.6 %collective-permute-start.22 = (bf16[2,32,2048]{2,1,0:T(8,128)(2,1)S(1)}, bf16[2,32,2048]{2,1,0:T(8,128)(2,1)S(1)}, u32[]{:S(2)}, u32[]{:S(2)}) collective-permute-start(bf16[2,32,2048]{2,1,0:T(8,128)(2,1)S(1)} %get-tuple-element.53), channel_id=1, source_target_pairs={{0,2},{1,3},{2,4},{3,5},{4,6},{5,7},{6,0},{7,1},{8,10},{9,11},{10,... | collective-permute-start | bytes 786440 | tf_op jit(solution)/shard_map/ppermute | solution.py:346
  54.8 18.5 %collective-permute-start.23 = (bf16[2,32,2048]{2,1,0:T(8,128)(2,1)S(1)}, bf16[2,32,2048]{2,1,0:T(8,128)(2,1)S(1)}, u32[]{:S(2)}, u32[]{:S(2)}) collective-permute-start(bf16[2,32,2048]{2,1,0:T(8,128)(2,1)S(1)} %get-tuple-element.54), channel_id=1, source_target_pairs={{0,3},{1,4},{2,5},{3,6},{4,7},{5,0},{6,1},{7,2},{8,11},{9,12},{10,... | collective-permute-start | bytes 786440 | tf_op jit(solution)/shard_map/ppermute | solution.py:346
  58.2 17.8 %collective-permute-start.24 = (bf16[2,32,2048]{2,1,0:T(8,128)(2,1)S(1)}, bf16[2,32,2048]{2,1,0:T(8,128)(2,1)S(1)}, u32[]{:S(2)}, u32[]{:S(2)}) collective-permute-start(bf16[2,32,2048]{2,1,0:T(8,128)(2,1)S(1)} %get-tuple-element.55), channel_id=1, source_target_pairs={{0,4},{1,5},{2,6},{3,7},{4,0},{5,1},{6,2},{7,3},{8,12},{9,13},{10,... | collective-permute-start | bytes 786440 | tf_op jit(solution)/shard_map/ppermute | solution.py:346
  58.2 23.4 %collective-permute-start.25 = (bf16[2,32,2048]{2,1,0:T(8,128)(2,1)S(1)}, bf16[2,32,2048]{2,1,0:T(8,128)(2,1)S(1)}, u32[]{:S(2)}, u32[]{:S(2)}) collective-permute-start(bf16[2,32,2048]{2,1,0:T(8,128)(2,1)S(1)} %get-tuple-element.56), channel_id=1, source_target_pairs={{0,5},{1,6},{2,7},{3,0},{4,1},{5,2},{6,3},{7,4},{8,13},{9,14},{10,... | collective-permute-start | bytes 786440 | tf_op jit(solution)/shard_map/ppermute | solution.py:346
  66.5 20.0 %collective-permute-start.26 = (bf16[2,32,2048]{2,1,0:T(8,128)(2,1)S(1)}, bf16[2,32,2048]{2,1,0:T(8,128)(2,1)S(1)}, u32[]{:S(2)}, u32[]{:S(2)}) collective-permute-start(bf16[2,32,2048]{2,1,0:T(8,128)(2,1)S(1)} %get-tuple-element.57), channel_id=1, source_target_pairs={{0,6},{1,7},{2,0},{3,1},{4,2},{5,3},{6,4},{7,5},{8,14},{9,15},{10,... | collective-permute-start | bytes 786440 | tf_op jit(solution)/shard_map/ppermute | solution.py:346
  66.9 20.4 %collective-permute-start.27 = (bf16[2,32,2048]{2,1,0:T(8,128)(2,1)S(1)}, bf16[2,32,2048]{2,1,0:T(8,128)(2,1)S(1)}, u32[]{:S(2)}, u32[]{:S(2)}) collective-permute-start(bf16[2,32,2048]{2,1,0:T(8,128)(2,1)S(1)} %get-tuple-element.58), channel_id=1, source_target_pairs={{0,7},{1,0},{2,1},{3,2},{4,3},{5,4},{6,5},{7,6},{8,15},{9,8},{10,9... | collective-permute-start | bytes 786440 | tf_op jit(solution)/shard_map/ppermute | solution.py:346
  73.3 31.3 %collective-permute-start.14 = (bf16[2,32,2048]{2,1,0:T(8,128)(2,1)S(1)}, bf16[2,32,2048]{2,1,0:T(8,128)(2,1)S(1)}, u32[]{:S(2)}, u32[]{:S(2)}) collective-permute-start(bf16[2,32,2048]{2,1,0:T(8,128)(2,1)S(1)} %get-tuple-element.43), channel_id=1, source_target_pairs={{0,1},{1,2},{2,3},{3,4},{4,5},{5,6},{6,7},{7,0},{8,9},{9,10},{10,1... | collective-permute-start | bytes 786440 | tf_op jit(solution)/shard_map/ppermute | solution.py:346
  76.0 28.6 %collective-permute-start.15 = (bf16[2,32,2048]{2,1,0:T(8,128)(2,1)S(1)}, bf16[2,32,2048]{2,1,0:T(8,128)(2,1)S(1)}, u32[]{:S(2)}, u32[]{:S(2)}) collective-permute-start(bf16[2,32,2048]{2,1,0:T(8,128)(2,1)S(1)} %get-tuple-element.44), channel_id=1, source_target_pairs={{0,2},{1,3},{2,4},{3,5},{4,6},{5,7},{6,0},{7,1},{8,10},{9,11},{10,... | collective-permute-start | bytes 786440 | tf_op jit(solution)/shard_map/ppermute | solution.py:346
  81.6 27.8 %collective-permute-start.16 = (bf16[2,32,2048]{2,1,0:T(8,128)(2,1)S(1)}, bf16[2,32,2048]{2,1,0:T(8,128)(2,1)S(1)}, u32[]{:S(2)}, u32[]{:S(2)}) collective-permute-start(bf16[2,32,2048]{2,1,0:T(8,128)(2,1)S(1)} %get-tuple-element.45), channel_id=1, source_target_pairs={{0,3},{1,4},{2,5},{3,6},{4,7},{5,0},{6,1},{7,2},{8,11},{9,12},{10,... | collective-permute-start | bytes 786440 | tf_op jit(solution)/shard_map/ppermute | solution.py:346
  86.5 23.0 %collective-permute-start.17 = (bf16[2,32,2048]{2,1,0:T(8,128)(2,1)S(1)}, bf16[2,32,2048]{2,1,0:T(8,128)(2,1)S(1)}, u32[]{:S(2)}, u32[]{:S(2)}) collective-permute-start(bf16[2,32,2048]{2,1,0:T(8,128)(2,1)S(1)} %get-tuple-element.46), channel_id=1, source_target_pairs={{0,4},{1,5},{2,6},{3,7},{4,0},{5,1},{6,2},{7,3},{8,12},{9,13},{10,... | collective-permute-start | bytes 786440 | tf_op jit(solution)/shard_map/ppermute | solution.py:346
  87.3 22.3 %collective-permute-start.18 = (bf16[2,32,2048]{2,1,0:T(8,128)(2,1)S(1)}, bf16[2,32,2048]{2,1,0:T(8,128)(2,1)S(1)}, u32[]{:S(2)}, u32[]{:S(2)}) collective-permute-start(bf16[2,32,2048]{2,1,0:T(8,128)(2,1)S(1)} %get-tuple-element.47), channel_id=1, source_target_pairs={{0,5},{1,6},{2,7},{3,0},{4,1},{5,2},{6,3},{7,4},{8,13},{9,14},{10,... | collective-permute-start | bytes 786440 | tf_op jit(solution)/shard_map/ppermute | solution.py:346
  104.6 11.8 %collective-permute-start.19 = (bf16[2,32,2048]{2,1,0:T(8,128)(2,1)S(1)}, bf16[2,32,2048]{2,1,0:T(8,128)(2,1)S(1)}, u32[]{:S(2)}, u32[]{:S(2)}) collective-permute-start(bf16[2,32,2048]{2,1,0:T(8,128)(2,1)S(1)} %get-tuple-element.48), channel_id=1, source_target_pairs={{0,6},{1,7},{2,0},{3,1},{4,2},{5,3},{6,4},{7,5},{8,14},{9,15},{10,... | collective-permute-start | bytes 786440 | tf_op jit(solution)/shard_map/ppermute | solution.py:346
  104.6 16.3 %collective-permute-start.20 = (bf16[2,32,2048]{2,1,0:T(8,128)(2,1)S(1)}, bf16[2,32,2048]{2,1,0:T(8,128)(2,1)S(1)}, u32[]{:S(2)}, u32[]{:S(2)}) collective-permute-start(bf16[2,32,2048]{2,1,0:T(8,128)(2,1)S(1)} %get-tuple-element.49), channel_id=1, source_target_pairs={{0,7},{1,0},{2,1},{3,2},{4,3},{5,4},{6,5},{7,6},{8,15},{9,8},{10,9... | collective-permute-start | bytes 786440 | tf_op jit(solution)/shard_map/ppermute | solution.py:346
